TPU v7x, 8 devices: a whole 2x2x1 slice. The times are simulated.
8 devices in a mesh: fsdp: 2 (over z, y), ep: 4 (over x, core).
Axes of the slice: x: 2, y: 2, z: 1, core: 2. Of those that a mesh axis runs over, the one named last changes fastest.
Arguments:
- x_tok: bfloat16 [16384, 512], P(('fsdp', 'ep'))
- dy_tok: bfloat16 [16384, 512], P(('fsdp', 'ep'))
- expert_ids: int32 [16384, 6], P(('fsdp', 'ep'))
- route_w: float32 [16384, 6], P(('fsdp', 'ep'))
- w_gate: bfloat16 [64, 512, 1408], P('ep', 'fsdp')
- w_up: bfloat16 [64, 512, 1408], P('ep', 'fsdp')
- w_down: bfloat16 [64, 1408, 512], P('ep', None, 'fsdp')
Outputs:
- output 1: bfloat16 [16384, 512], P(('fsdp', 'ep'))
- output 2: float32 [16384, 6], P(('fsdp', 'ep'))
- output 3: float32 [64, 512, 1408], P('ep', 'fsdp')
- output 4: float32 [64, 512, 1408], P('ep', 'fsdp')
- output 5: float32 [64, 1408, 512], P('ep', None, 'fsdp')
All inputs are finite; a program needn't handle non-finite values.
Results may differ from a plain program's by a relative error of at most 0.00900672.
Values are sent between devices in bfloat16 or wider.
A program may use at most 1 GiB of HBM per device.

v0:
```python
import functools

import jax
import jax.numpy as jnp
from jax import lax
from jax.experimental import pallas as pl
from jax.experimental.pallas import tpu as pltpu
from jax.sharding import PartitionSpec as P


CAP_FACTOR = 3
CHUNKS = 4
GROUPS = (3, 3, 3, 3, 2, 2)
PAD = 8
LANES = 128
SUB = 8
INTERPRET = False
VMEM_BYTES = 67_043_328


def capacity_of(tok_dev, top_k, experts):
    return max(8, ((CAP_FACTOR * tok_dev * top_k // experts + 7) // 8) * 8)


def route_kernel(n_pairs, top_k, experts, capacity, ids_ref, gate_ref, tok_ref, slot_gate_ref, cnt_ref):
    stride = capacity + PAD
    for e in range(experts):
        cnt_ref[e] = 0

    def step(t, carry):
        ids = [ids_ref[t * top_k + j] for j in range(top_k)]
        gates = [gate_ref[t * top_k + j] for j in range(top_k)]
        counts = [cnt_ref[e] for e in ids]
        for j in range(top_k):
            slot = ids[j] * stride + jnp.minimum(counts[j], capacity)
            tok_ref[slot] = t
            slot_gate_ref[slot] = gates[j]
            cnt_ref[ids[j]] = counts[j] + 1
        return carry

    lax.fori_loop(0, n_pairs // top_k, step, 0, unroll=2)
    for e in range(experts):
        tok_ref[e * stride + capacity + 1] = jnp.minimum(cnt_ref[e], capacity)


def route_slots(ids_flat, gates_flat, top_k, experts, capacity):
    n_pairs = ids_flat.shape[0]
    smem = pl.BlockSpec(memory_space=pltpu.SMEM)
    words = experts * (capacity + PAD)
    return pl.pallas_call(
        functools.partial(route_kernel, n_pairs, top_k, experts, capacity),
        in_specs=[smem, smem],
        out_specs=[smem, smem],
        out_shape=[jax.ShapeDtypeStruct((words,), jnp.int32), jax.ShapeDtypeStruct((words,), jnp.float32)],
        scratch_shapes=[pltpu.SMEM((experts,), jnp.int32)],
        name="route",
        interpret=INTERPRET,
    )(ids_flat, gates_flat)


def gather_kernel(n_src, with_dy, region, exp_local, capacity, chunk, nt_ref, tok_ref, gate_ref, *refs):
    stride = capacity + PAD
    token_refs = refs[:n_src]
    refs = list(refs[n_src if with_dy else n_src + 1:])
    xg_hbm = refs.pop(0)
    dy_hbm = refs.pop(0) if with_dy else None
    rows_v, buf_x, buf_g, xg_v, dy_v, xg_sem, dy_sem, tok_sem = refs
    src = pl.program_id(0)
    for k in range(n_src):
        @pl.when(src == k)
        def _(k=k):
            copy = pltpu.make_async_copy(token_refs[k], rows_v, tok_sem)
            copy.start()
            copy.wait()

    def copies(e, j, slot):
        at = pl.ds(src * chunk, chunk)
        out = [pltpu.make_async_copy(xg_v.at[slot], xg_hbm.at[e, region, j, at], xg_sem.at[slot])]
        if with_dy:
            out.append(pltpu.make_async_copy(dy_v.at[slot], dy_hbm.at[e, j, at], dy_sem.at[slot]))
        return out

    def one_expert(e, done):
        n = tok_ref[0, 0, e * stride + capacity + 1]

        def one_chunk(j, done):
            slot = lax.rem(done, 2)

            @pl.when(done >= 2)
            def _():
                for copy in copies(e, j, slot):
                    copy.wait()

            def rows(r8, carry):
                at0 = j * chunk + r8 * 8
                toks = [jnp.where(at0 + u < n, tok_ref[0, 0, e * stride + at0 + u], 0) for u in range(8)]
                gates = [jnp.where(at0 + u < n, gate_ref[0, 0, e * stride + at0 + u], 0.0) for u in range(8)]
                loaded = [rows_v[t].astype(jnp.float32) for t in toks]
                for u in range(8):
                    at = pl.ds(pl.multiple_of((r8 * 8 + u) * SUB, SUB), SUB)
                    buf_x[at, :] = loaded[u]
                    buf_g[at, :] = loaded[u] * gates[u]
                return carry

            lax.fori_loop(0, chunk // 8, rows, 0)
            half = SUB // 2
            for c in range(half):
                lanes = slice(c * LANES, (c + 1) * LANES)
                g_lanes = slice((half + c) * LANES, (half + c + 1) * LANES)
                xg_v[slot, :, lanes] = buf_x[pl.ds(c, chunk, stride=SUB), :].astype(jnp.bfloat16)
                xg_v[slot, :, g_lanes] = buf_g[pl.ds(half + c, chunk, stride=SUB), :].astype(jnp.bfloat16)
                if with_dy:
                    dy_v[slot, :, lanes] = buf_x[pl.ds(half + c, chunk, stride=SUB), :].astype(jnp.bfloat16)
            for copy in copies(e, j, slot):
                copy.start()
            return done + 1

        return lax.fori_loop(0, nt_ref[e * 2 + region], one_chunk, done)

    lax.fori_loop(0, exp_local, one_expert, 0)
    for slot in range(2):
        for copy in copies(0, 0, slot):
            copy.wait()


def gather_rows(tokens, slot_tok, slot_gate, nt, region, capacity, carried=()):
    with_dy = region == 0
    n_src = len(tokens)
    exp_local = nt.shape[0]
    chunk = capacity // CHUNKS
    tok_dev = tokens[0].shape[0]
    width = SUB * LANES
    tile_rows = n_src * chunk
    hbm = pl.BlockSpec(memory_space=pl.ANY)
    per_src = pl.BlockSpec((1, 1, slot_tok.shape[2]), lambda s, *_: (s, 0, 0), memory_space=pltpu.SMEM)
    out_shape = [jax.ShapeDtypeStruct((exp_local, 2, CHUNKS, tile_rows, width), jnp.bfloat16)]
    if with_dy:
        out_shape.append(jax.ShapeDtypeStruct((exp_local, CHUNKS, tile_rows, width // 2), jnp.bfloat16))
    return pl.pallas_call(
        functools.partial(gather_kernel, n_src, with_dy, region, exp_local, capacity, chunk),
        grid_spec=pltpu.PrefetchScalarGridSpec(
            num_scalar_prefetch=1,
            grid=(n_src,),
            in_specs=[per_src, per_src] + [hbm] * (n_src + len(carried)),
            out_specs=[hbm] * len(out_shape),
            scratch_shapes=[
                pltpu.VMEM((tok_dev, SUB, LANES), jnp.bfloat16),
                pltpu.VMEM((chunk * SUB, LANES), jnp.float32),
                pltpu.VMEM((chunk * SUB, LANES), jnp.float32),
                pltpu.VMEM((2, chunk, width), jnp.bfloat16),
                pltpu.VMEM((2, chunk, width // 2), jnp.bfloat16),
                pltpu.SemaphoreType.DMA((2,)),
                pltpu.SemaphoreType.DMA((2,)),
                pltpu.SemaphoreType.DMA,
            ]),
        out_shape=out_shape,
        input_output_aliases={3 + n_src + k: k for k in range(len(carried))},
        compiler_params=pltpu.CompilerParams(dimension_semantics=("arbitrary",), vmem_limit_bytes=VMEM_BYTES),
        interpret=INTERPRET,
    )(nt.reshape(-1), slot_tok, slot_gate, *tokens, *carried)


def dot(a, b, dims):
    return lax.dot_general(a, b, (dims, ((), ())), preferred_element_type=jnp.float32)


NN, NT, TN = ((1,), (0,)), ((1,), (1,)), ((0,), (0,))


def expert_kernel(e0, step_rows, nt_ref, mine_ref, xg_ref, dy_ref, w1o, w1p, w3o, w3p, w2o, w2p, *refs):
    dx_ref, dr_ref, dw1_ref, dw3_ref, dw2_ref, h1, h3, da, hid, dh1, dh3, dw2t = refs[-12:]
    e = pl.program_id(0)
    t = pl.program_id(1)
    region, j = t // CHUNKS, t % CHUNKS
    half = w1o.shape[1]
    d_model = 2 * half
    mine = pl.multiple_of(mine_ref[0] * half, half)
    other = pl.multiple_of(half - mine_ref[0] * half, half)

    @pl.when(t == 0)
    def _():
        dw1_ref[...] = jnp.zeros_like(dw1_ref)
        dw3_ref[...] = jnp.zeros_like(dw3_ref)
        dw2t[...] = jnp.zeros_like(dw2t)

    @pl.when(j < nt_ref[(e0 + e) * 2 + region])
    def _():
        xo = xg_ref[0, 0, 0, :, pl.ds(mine, half)]
        xp = xg_ref[0, 0, 0, :, pl.ds(other, half)]
        go = xg_ref[0, 0, 0, :, pl.ds(d_model + mine, half)]
        gp = xg_ref[0, 0, 0, :, pl.ds(d_model + other, half)]
        h1[...] = dot(xo, w1o[0], NN) + dot(xp, w1p[0], NN)
        h3[...] = dot(xo, w3o[0], NN) + dot(xp, w3p[0], NN)
        da[...] = dot(go, w2o[0], NT) + dot(gp, w2p[0], NT)

        def rows(k, carry):
            at = pl.ds(pl.multiple_of(k * step_rows, step_rows), step_rows)
            p1, p3, d = h1[at, :], h3[at, :], da[at, :]
            s = jax.nn.sigmoid(p1)
            hid[at, :] = (p1 * s * p3).astype(jnp.bfloat16)
            dh1[at, :] = (d * p3 * s * (1.0 + p1 * (1.0 - s))).astype(jnp.bfloat16)
            dh3[at, :] = (d * p1 * s).astype(jnp.bfloat16)
            return carry

        lax.fori_loop(0, h1.shape[0] // step_rows, rows, 0)
        dw1_ref[0] += dot(xo, dh1[...], TN)
        dw3_ref[0] += dot(xo, dh3[...], TN)
        dw2t[...] += dot(go, hid[...], TN)

    @pl.when((region == 0) & (j < nt_ref[(e0 + e) * 2]))
    def _():
        dyo = dy_ref[0, 0, :, pl.ds(mine, half)].astype(jnp.float32)
        dyp = dy_ref[0, 0, :, pl.ds(other, half)].astype(jnp.float32)
        prod = dyo * dot(hid[...], w2o[0], NN) + dyp * dot(hid[...], w2p[0], NN)
        dr = jnp.sum(prod, axis=1, keepdims=True)
        lane = lax.broadcasted_iota(jnp.int32, dr_ref.shape[2:], 1)
        dr_ref[0, 0] = jnp.where(lane == e0 + e, dr, 0.0)
        dxo = dot(dh1[...], w1o[0], NT) + dot(dh3[...], w3o[0], NT)
        dx_ref[0, 0, :, pl.ds(mine, half)] = dxo.astype(jnp.bfloat16)
        dxp = dot(dh1[...], w1p[0], NT) + dot(dh3[...], w3p[0], NT)
        dx_ref[0, 0, :, pl.ds(other, half)] = dxp.astype(jnp.bfloat16)

    @pl.when(t == pl.num_programs(1) - 1)
    def _():
        dw2_ref[0] = dw2t[...].T


def expert_group(e0, count, xg, dy, nt, mine, own, peer, carried):
    exp_local, _, _, tile_rows, width = xg.shape
    half, d_ff = own[0].shape[1:]
    step_rows = 16

    def own_tile(e, t, nt_ref, _):
        return (e0 + e, jnp.minimum(jnp.where(t < CHUNKS, t, CHUNKS - 1), nt_ref[(e0 + e) * 2] - 1), 0, 0)

    def xg_tile(e, t, nt_ref, _):
        region = t // CHUNKS
        return (e0 + e, region, jnp.minimum(t % CHUNKS, nt_ref[(e0 + e) * 2 + region] - 1), 0, 0)

    at_own = lambda e, t, *_: (e0 + e, 0, 0)
    at_peer = lambda e, t, *_: (e, 0, 0)
    up = lambda at: pl.BlockSpec((1, half, d_ff), at)
    down = lambda at: pl.BlockSpec((1, d_ff, half), at)
    out_shape = [
        jax.ShapeDtypeStruct((exp_local, CHUNKS, tile_rows, width // 2), jnp.bfloat16),
        jax.ShapeDtypeStruct((exp_local, CHUNKS, tile_rows, LANES), jnp.float32),
        jax.ShapeDtypeStruct((exp_local, half, d_ff), jnp.float32),
        jax.ShapeDtypeStruct((exp_local, half, d_ff), jnp.float32),
        jax.ShapeDtypeStruct((exp_local, d_ff, half), jnp.float32),
    ]
    n_in = 2 + 8
    carried = list(carried)
    return pl.pallas_call(
        functools.partial(expert_kernel, e0, step_rows),
        grid_spec=pltpu.PrefetchScalarGridSpec(
            num_scalar_prefetch=2,
            grid=(count, 2 * CHUNKS),
            in_specs=[
                pl.BlockSpec((1, 1, 1, tile_rows, width), xg_tile),
                pl.BlockSpec((1, 1, tile_rows, width // 2), own_tile),
                up(at_own), up(at_peer), up(at_own), up(at_peer), down(at_own), down(at_peer),
            ] + [pl.BlockSpec(memory_space=pl.ANY)] * len(carried),
            out_specs=[
                pl.BlockSpec((1, 1, tile_rows, width // 2), own_tile),
                pl.BlockSpec((1, 1, tile_rows, LANES), own_tile),
                up(at_own), up(at_own), down(at_own),
            ],
            scratch_shapes=[
                pltpu.VMEM((tile_rows, d_ff), jnp.float32),
                pltpu.VMEM((tile_rows, d_ff), jnp.float32),
                pltpu.VMEM((tile_rows, d_ff), jnp.float32),
                pltpu.VMEM((tile_rows, d_ff), jnp.bfloat16),
                pltpu.VMEM((tile_rows, d_ff), jnp.bfloat16),
                pltpu.VMEM((tile_rows, d_ff), jnp.bfloat16),
                pltpu.VMEM((half, d_ff), jnp.float32),
            ]),
        out_shape=out_shape,
        input_output_aliases={n_in + k: k for k in range(len(carried))},
        compiler_params=pltpu.CompilerParams(
            dimension_semantics=("arbitrary", "arbitrary"), vmem_limit_bytes=VMEM_BYTES),
        interpret=INTERPRET,
    )(nt.reshape(-1), mine, xg, dy, own[0], peer[0], own[1], peer[1], own[2], peer[2], *carried)


def scatter_kernel(exp_local, capacity, chunk, tok_ref, dx_hbm, dr_hbm,
                   dx_out, dr_out, acc, tmp, dx_v, dr_v, dx_sem, dr_sem):
    src = pl.program_id(0)
    stride = capacity + PAD
    tok_dev = dx_out.shape[1]

    def copies(e, j):
        k = e * CHUNKS + j
        rows = pl.ds(src * chunk, chunk)
        return (pltpu.make_async_copy(dx_hbm.at[e, j, rows], dx_v.at[k], dx_sem.at[k]),
                pltpu.make_async_copy(dr_hbm.at[e, j, rows], dr_v.at[k], dr_sem.at[k]))

    def each(fn):
        def per_expert(e, carry):
            n = tok_ref[0, 0, e * stride + capacity + 1]
            lax.fori_loop(0, (n + chunk - 1) // chunk, lambda j, c: fn(e, j, n, c), 0)
            return carry

        lax.fori_loop(0, exp_local, per_expert, 0)

    def start(e, j, n, carry):
        for copy in copies(e, j):
            copy.start()
        return carry

    each(start)
    acc[...] = jnp.zeros_like(acc)

    def add(e, j, n, carry):
        k = e * CHUNKS + j
        for copy in copies(e, j):
            copy.wait()
        for c in range(SUB // 2):
            tmp[pl.ds(c, chunk, stride=SUB), :] = dx_v[k, :, c * LANES:(c + 1) * LANES].astype(jnp.float32)
        tmp[pl.ds(SUB // 2, chunk, stride=SUB), :] = dr_v[k]

        def rows(r8, c):
            r0 = r8 * 8
            toks = [jnp.where(j * chunk + r0 + u < n, tok_ref[0, 0, e * stride + j * chunk + r0 + u], tok_dev)
                    for u in range(8)]
            ats = [pl.ds(pl.multiple_of(t * SUB, SUB), SUB) for t in toks]
            sums = [acc[ats[u], :] + tmp[pl.ds(pl.multiple_of((r0 + u) * SUB, SUB), SUB), :] for u in range(8)]
            for u in range(8):
                acc[ats[u], :] = sums[u]
            return c

        lax.fori_loop(0, (jnp.minimum(n - j * chunk, chunk) + 7) // 8, rows, 0)
        return carry

    each(add)
    for c in range(SUB // 2):
        dx_out[0, :, c * LANES:(c + 1) * LANES] = acc[pl.ds(c, tok_dev, stride=SUB), :]
    dr_out[0] = acc[pl.ds(SUB // 2, tok_dev, stride=SUB), :]


def scatter_rows(dx_rows, dr_rows, slot_tok, capacity, tok_dev):
    exp_local, _, tile_rows, d_model = dx_rows.shape
    chunk = capacity // CHUNKS
    n_own = tile_rows // chunk
    hbm = pl.BlockSpec(memory_space=pl.ANY)
    return pl.pallas_call(
        functools.partial(scatter_kernel, exp_local, capacity, chunk),
        grid_spec=pltpu.PrefetchScalarGridSpec(
            num_scalar_prefetch=0,
            grid=(n_own,),
            in_specs=[
                pl.BlockSpec((1, 1, slot_tok.shape[2]), lambda s, *_: (s, 0, 0), memory_space=pltpu.SMEM),
                hbm, hbm,
            ],
            out_specs=[
                pl.BlockSpec((1, tok_dev, d_model), lambda s, *_: (s, 0, 0)),
                pl.BlockSpec((1, tok_dev, LANES), lambda s, *_: (s, 0, 0)),
            ],
            scratch_shapes=[
                pltpu.VMEM(((tok_dev + 1) * SUB, LANES), jnp.float32),
                pltpu.VMEM((chunk * SUB, LANES), jnp.float32),
                pltpu.VMEM((exp_local * CHUNKS, chunk, d_model), jnp.bfloat16),
                pltpu.VMEM((exp_local * CHUNKS, chunk, LANES), jnp.float32),
                pltpu.SemaphoreType.DMA((exp_local * CHUNKS,)),
                pltpu.SemaphoreType.DMA((exp_local * CHUNKS,)),
            ]),
        out_shape=[
            jax.ShapeDtypeStruct((n_own, tok_dev, d_model), jnp.float32),
            jax.ShapeDtypeStruct((n_own, tok_dev, LANES), jnp.float32),
        ],
        compiler_params=pltpu.CompilerParams(
            dimension_semantics=("arbitrary",), vmem_limit_bytes=VMEM_BYTES),
        name="scatter_rows",
        interpret=INTERPRET,
    )(slot_tok, dx_rows, dr_rows)


def solution(mesh):
    n_ep = mesh.shape["ep"]
    n_fsdp = mesh.shape["fsdp"]
    tok_spec = P(("fsdp", "ep"), None)
    spec_in = P("ep", "fsdp", None)
    spec_out = P("ep", None, "fsdp")

    def swap(value, axis, mask):
        size = n_fsdp if axis == "fsdp" else n_ep
        return lax.ppermute(value, axis, [(k, k ^ mask) for k in range(size)])

    def per_device(x_tok, dy_tok, expert_ids, route_w, w_gate, w_up, w_down):
        tok_dev, top_k = expert_ids.shape
        exp_local = w_gate.shape[0]
        experts = exp_local * n_ep
        capacity = capacity_of(tok_dev, top_k, experts)
        chunk = capacity // CHUNKS
        my_fsdp = lax.axis_index("fsdp")
        my_ep = lax.axis_index("ep")

        tokens = jnp.concatenate([x_tok, dy_tok], axis=1).reshape(tok_dev, SUB, LANES)
        tok_y = swap(tokens, "fsdp", 1)
        tok_x = swap(tokens, "ep", 2)
        tok_c = swap(tokens, "ep", 1)
        tok_yx = swap(tok_y, "ep", 2)
        tok_cx = swap(tok_x, "ep", 1)
        tok_cy = swap(tok_y, "ep", 1)
        tok_cyx = swap(tok_yx, "ep", 1)
        all_tokens = (tokens, tok_c, tok_x, tok_cx, tok_y, tok_cy, tok_yx, tok_cyx)

        slot_tok, slot_gate = route_slots(
            expert_ids.reshape(-1), route_w.reshape(-1), top_k, experts, capacity)
        slot_tok = lax.all_gather(slot_tok, ("fsdp", "ep"), axis=0, tiled=False)
        slot_gate = lax.all_gather(slot_gate, ("fsdp", "ep"), axis=0, tiled=False)

        def for_me(v):
            v = v.reshape(n_fsdp * n_ep, n_ep, -1)
            v = lax.dynamic_index_in_dim(v, my_ep, axis=1, keepdims=False)
            order = [(my_fsdp ^ a) * n_ep + (my_ep ^ b) for a in range(n_fsdp) for b in range(n_ep)]
            return jnp.stack([lax.dynamic_index_in_dim(v, k, axis=0, keepdims=True) for k in order])

        slot_tok, slot_gate = for_me(slot_tok), for_me(slot_gate)
        cnt = slot_tok.reshape(n_fsdp, n_ep, exp_local, capacity + PAD)[..., capacity + 1]
        most = jnp.max(cnt, axis=1)
        nt = jnp.maximum((most + chunk - 1) // chunk, 1).T

        xg, dy = gather_rows(all_tokens[:n_ep], slot_tok[:n_ep], slot_gate[:n_ep], nt, 0, capacity)
        xg, = gather_rows(all_tokens[n_ep:], slot_tok[n_ep:], slot_gate[n_ep:], nt, 1, capacity, (xg,))

        own = (w_gate, w_up, w_down)
        mine = my_fsdp.astype(jnp.int32).reshape(1)
        carried = ()
        e0 = 0
        for count in GROUPS:
            peer = [swap(w[e0:e0 + count], "fsdp", 1) for w in own]
            carried = expert_group(e0, count, xg, dy, nt, mine, own, peer, carried)
            e0 += count
        dx_rows, dr_rows, grad_w_gate, grad_w_up, grad_w_down = carried

        part, dr_part = scatter_rows(dx_rows, dr_rows, slot_tok[:n_ep], capacity, tok_dev)
        from_core_near = swap(part[1], "ep", 1)
        from_core_far = swap(part[3], "ep", 1)
        far = part[2] + from_core_far
        near = part[0] + from_core_near
        grad_x = (near + swap(far, "ep", 2)).astype(jnp.bfloat16)
        dr_mine = dr_part[:, :, :exp_local]
        by_ep = jnp.stack([dr_mine[0]] + [swap(dr_mine[b], "ep", b) for b in range(1, n_ep)])
        rel = (expert_ids // exp_local) ^ my_ep
        loc = expert_ids % exp_local
        hit = ((rel[:, :, None, None] == jnp.arange(n_ep)[None, None, :, None])
               & (loc[:, :, None, None] == jnp.arange(exp_local)[None, None, None, :]))
        dense = jnp.transpose(by_ep, (1, 0, 2))[:, None]
        route_grad = jnp.sum(jnp.where(hit, dense, 0.0), axis=(2, 3))
        return grad_x, route_grad, grad_w_gate, grad_w_up, grad_w_down

    return jax.shard_map(
        per_device, mesh=mesh,
        in_specs=(tok_spec, tok_spec, tok_spec, tok_spec, spec_in, spec_in, spec_out),
        out_specs=(tok_spec, tok_spec, spec_in, spec_in, spec_out),
        check_vma=False)
```

profile of v0, /device:TPU:0, one launch (start us, length us, event | category | flops | bytes accessed | tf_op | source)
XLA Modules:
  0.0 1624.6 jit_solution(1353839327103065793)
XLA Ops:
  12.4 66.0 %route.1 = (s32[37376]{0:T(1024)}, f32[37376]{0:T(1024)}) custom-call(s32[12288]{0:T(1024)} %reshape.90.ids_ref, f32[12288]{0:T(1024)} %reshape.91.gate_ref), custom_call_target="tpu_custom_call" | custom-call | tf_op jit(solution)/shard_map/route/pallas_call | solution.py:50
  90.1 4.1 fusion.8
  95.1 3.9 fusion.7
  100.4 5.6 fusion.6
  118.0 4.1 reduce.1
  125.3 9.2 all-gather.9.cloned.1.call-done
  134.4 4.1 reduce.3
  141.7 218.2 %collective-permute-done.10.w1p = bf16[2,256,1408]{2,1,0:T(8,128)(2,1)} collective-permute-done((bf16[2,256,1408]{2,1,0:T(8,128)(2,1)}, bf16[2,256,1408]{2,1,0:T(8,128)(2,1)}, u32[]{:S(2)}, u32[]{:S(2)}) %collective-permute-start.10) | collective-permute-done | bytes 1441824 | tf_op jit(solution)/shard_map/ppermute | solution.py:386
  367.4 42.8 %collective-permute-done.19.w1p = bf16[3,256,1408]{2,1,0:T(8,128)(2,1)} collective-permute-done((bf16[3,256,1408]{2,1,0:T(8,128)(2,1)}, bf16[3,256,1408]{2,1,0:T(8,128)(2,1)}, u32[]{:S(2)}, u32[]{:S(2)}) %collective-permute-start.19) | collective-permute-done | bytes 2162720 | tf_op jit(solution)/shard_map/ppermute | solution.py:386
  415.5 41.0 %collective-permute-done.20.w3p = bf16[3,256,1408]{2,1,0:T(8,128)(2,1)} collective-permute-done((bf16[3,256,1408]{2,1,0:T(8,128)(2,1)}, bf16[3,256,1408]{2,1,0:T(8,128)(2,1)}, u32[]{:S(2)}, u32[]{:S(2)}) %collective-permute-start.20) | collective-permute-done | bytes 2162720 | tf_op jit(solution)/shard_map/ppermute | solution.py:386
  457.2 45.6 %collective-permute-done.21.w2p = bf16[3,1408,256]{2,1,0:T(8,128)(2,1)} collective-permute-done((bf16[3,1408,256]{2,1,0:T(8,128)(2,1)}, bf16[3,1408,256]{2,1,0:T(8,128)(2,1)}, u32[]{:S(2)}, u32[]{:S(2)}) %collective-permute-start.21) | collective-permute-done | bytes 2162720 | tf_op jit(solution)/shard_map/ppermute | solution.py:386
  503.6 45.6 %collective-permute-done.16.w1p = bf16[3,256,1408]{2,1,0:T(8,128)(2,1)} collective-permute-done((bf16[3,256,1408]{2,1,0:T(8,128)(2,1)}, bf16[3,256,1408]{2,1,0:T(8,128)(2,1)}, u32[]{:S(2)}, u32[]{:S(2)}) %collective-permute-start.16) | collective-permute-done | bytes 2162720 | tf_op jit(solution)/shard_map/ppermute | solution.py:386
  555.0 40.6 %collective-permute-done.17.w3p = bf16[3,256,1408]{2,1,0:T(8,128)(2,1)} collective-permute-done((bf16[3,256,1408]{2,1,0:T(8,128)(2,1)}, bf16[3,256,1408]{2,1,0:T(8,128)(2,1)}, u32[]{:S(2)}, u32[]{:S(2)}) %collective-permute-start.17) | collective-permute-done | bytes 2162720 | tf_op jit(solution)/shard_map/ppermute | solution.py:386
  595.5 46.3 %collective-permute-done.18.w2p = bf16[3,1408,256]{2,1,0:T(8,128)(2,1)} collective-permute-done((bf16[3,1408,256]{2,1,0:T(8,128)(2,1)}, bf16[3,1408,256]{2,1,0:T(8,128)(2,1)}, u32[]{:S(2)}, u32[]{:S(2)}) %collective-permute-start.18) | collective-permute-done | bytes 2162720 | tf_op jit(solution)/shard_map/ppermute | solution.py:386
  642.6 45.6 %collective-permute-done.13.w1p = bf16[3,256,1408]{2,1,0:T(8,128)(2,1)} collective-permute-done((bf16[3,256,1408]{2,1,0:T(8,128)(2,1)}, bf16[3,256,1408]{2,1,0:T(8,128)(2,1)}, u32[]{:S(2)}, u32[]{:S(2)}) %collective-permute-start.13) | collective-permute-done | bytes 2162720 | tf_op jit(solution)/shard_map/ppermute | solution.py:386
  691.2 42.1 %collective-permute-done.14.w3p = bf16[3,256,1408]{2,1,0:T(8,128)(2,1)S(1)} collective-permute-done((bf16[3,256,1408]{2,1,0:T(8,128)(2,1)}, bf16[3,256,1408]{2,1,0:T(8,128)(2,1)S(1)}, u32[]{:S(2)}, u32[]{:S(2)}) %collective-permute-start.14) | collective-permute-done | bytes 2162720 | tf_op jit(solution)/shard_map/ppermute | solution.py:386
  735.2 45.8 %collective-permute-done.15.w2p = bf16[3,1408,256]{2,1,0:T(8,128)(2,1)S(1)} collective-permute-done((bf16[3,1408,256]{2,1,0:T(8,128)(2,1)S(1)}, bf16[3,1408,256]{2,1,0:T(8,128)(2,1)S(1)}, u32[]{:S(2)}, u32[]{:S(2)}) %collective-permute-start.15) | collective-permute-done | bytes 2162720 | tf_op jit(solution)/shard_map/ppermute | solution.py:386
  788.4 68.7 %shard_map.110 = (bf16[16,2,4,576,1024]{4,3,2,1,0:T(8,128)(2,1)}, bf16[16,4,576,512]{3,2,1,0:T(8,128)(2,1)}) custom-call(s32[32]{0:T(128)} %reshape.94.nt_ref, s32[4,1,9344]{2,1,0:T(1,128)} %pad_add_fusion.tok_ref, f32[4,1,9344]{2,1,0:T(1,128)} %pad_maximum_fusion.1.gate_ref, bf16[2048,8,128]{2,1,0:T(8,128)(2,1)} %bitcast.15.refs_0_, ...), custom_call_target="tpu_custom_call" | custom-call | tf_op jit(solution)/shard_map/pallas_call | solution.py:139
  857.1 66.5 %shard_map.111.xg_ref = bf16[16,2,4,576,1024]{4,3,2,1,0:T(8,128)(2,1)} custom-call(s32[32]{0:T(128)} %reshape.94.nt_ref, s32[4,1,9344]{2,1,0:T(1,128)} %pad_add_fusion.1.tok_ref, f32[4,1,9344]{2,1,0:T(1,128)} %pad_maximum_fusion.gate_ref, bf16[2048,8,128]{2,1,0:T(8,128)(2,1)} %collective-permute-done.refs_0_, ...), custom_call_target="tpu_custom_call", output_to_operand_aliasing={{}: (7, {})} | custom-call | tf_op jit(solution)/shard_map/pallas_call | solution.py:139
  923.6 73.7 %shard_map.112 = (bf16[16,4,576,512]{3,2,1,0:T(8,128)(2,1)}, f32[16,4,576,128]{3,2,1,0:T(8,128)}, f32[16,256,1408]{2,1,0:T(8,128)}, f32[16,256,1408]{2,1,0:T(8,128)}, f32[16,1408,256]{2,1,0:T(8,128)}) custom-call(s32[32]{0:T(128)} %reshape.94.nt_ref, s32[1]{0:T(128)} %bitcast.2.mine_ref, bf16[16,2,4,576,1024]{4,3,2,1,0:T(8,128)(2,1)} %shard_map.111.xg_ref, ...), custom_call_target="tpu_custom_call" | custom-call | tf_op jit(solution)/shard_map/pallas_call | solution.py:253
  997.3 81.2 %shard_map.113 = (bf16[16,4,576,512]{3,2,1,0:T(8,128)(2,1)}, f32[16,4,576,128]{3,2,1,0:T(8,128)}, f32[16,256,1408]{2,1,0:T(8,128)}, f32[16,256,1408]{2,1,0:T(8,128)}, f32[16,1408,256]{2,1,0:T(8,128)}) custom-call(s32[32]{0:T(128)} %reshape.94.nt_ref, ...), custom_call_target="tpu_custom_call", output_to_operand_aliasing={{0}: (10, {}), {1}: (11, {}), {2}: (12, {}), {3}: (13, {}),... | custom-call | tf_op jit(solution)/shard_map/pallas_call | solution.py:253
  1078.5 119.4 %shard_map.114 = (bf16[16,4,576,512]{3,2,1,0:T(8,128)(2,1)}, f32[16,4,576,128]{3,2,1,0:T(8,128)}, f32[16,256,1408]{2,1,0:T(8,128)}, f32[16,256,1408]{2,1,0:T(8,128)}, f32[16,1408,256]{2,1,0:T(8,128)}) custom-call(s32[32]{0:T(128)} %reshape.94.nt_ref, ...), custom_call_target="tpu_custom_call", output_to_operand_aliasing={{0}: (10, {}), {1}: (11, {}), {2}: (12, {}), {3}: (13, {}),... | custom-call | tf_op jit(solution)/shard_map/pallas_call | solution.py:253
  1198.0 74.0 %shard_map.115 = (bf16[16,4,576,512]{3,2,1,0:T(8,128)(2,1)}, f32[16,4,576,128]{3,2,1,0:T(8,128)}, f32[16,256,1408]{2,1,0:T(8,128)}, f32[16,256,1408]{2,1,0:T(8,128)}, f32[16,1408,256]{2,1,0:T(8,128)}) custom-call(s32[32]{0:T(128)} %reshape.94.nt_ref, ...), custom_call_target="tpu_custom_call", output_to_operand_aliasing={{0}: (10, {}), {1}: (11, {}), {2}: (12, {}), {3}: (13, {}),... | custom-call | tf_op jit(solution)/shard_map/pallas_call | solution.py:253
  1272.0 50.0 %shard_map.116 = (bf16[16,4,576,512]{3,2,1,0:T(8,128)(2,1)}, f32[16,4,576,128]{3,2,1,0:T(8,128)}, f32[16,256,1408]{2,1,0:T(8,128)}, f32[16,256,1408]{2,1,0:T(8,128)}, f32[16,1408,256]{2,1,0:T(8,128)}) custom-call(s32[32]{0:T(128)} %reshape.94.nt_ref, ...), custom_call_target="tpu_custom_call", output_to_operand_aliasing={{0}: (10, {}), {1}: (11, {}), {2}: (12, {}), {3}: (13, {}),... | custom-call | tf_op jit(solution)/shard_map/pallas_call | solution.py:253
  1322.1 50.1 %shard_map.117 = (bf16[16,4,576,512]{3,2,1,0:T(8,128)(2,1)}, f32[16,4,576,128]{3,2,1,0:T(8,128)}, f32[16,256,1408]{2,1,0:T(8,128)}, f32[16,256,1408]{2,1,0:T(8,128)}, f32[16,1408,256]{2,1,0:T(8,128)}) custom-call(s32[32]{0:T(128)} %reshape.94.nt_ref, ...), custom_call_target="tpu_custom_call", output_to_operand_aliasing={{0}: (10, {}), {1}: (11, {}), {2}: (12, {}), {3}: (13, {}),... | custom-call | tf_op jit(solution)/shard_map/pallas_call | solution.py:253
  1372.2 50.6 %scatter_rows.1 = (f32[4,2048,512]{2,1,0:T(8,128)}, f32[4,2048,128]{2,1,0:T(8,128)}) custom-call(s32[4,1,9344]{2,1,0:T(1,128)} %pad_add_fusion.tok_ref, bf16[16,4,576,512]{3,2,1,0:T(8,128)(2,1)} %get-tuple-element.70.dx_hbm, f32[16,4,576,128]{3,2,1,0:T(8,128)} %get-tuple-element.71.dr_hbm), custom_call_target="tpu_custom_call" | custom-call | tf_op jit(solution)/shard_map/scatter_rows/pallas_call | solution.py:345
  1422.8 6.4 slice_bitcast_fusion.1
  1429.2 68.4 %collective-permute-start.26 = (f32[2048,512]{1,0:T(8,128)S(1)}, f32[2048,512]{1,0:T(8,128)S(1)}, u32[]{:S(2)}, u32[]{:S(2)}) collective-permute-start(f32[2048,512]{1,0:T(8,128)S(1)} %get-tuple-element.94), channel_id=1, source_target_pairs={{0,1},{1,0},{2,3},{3,2},{4,5},{5,4},{6,7},{7,6}} | collective-permute-start | bytes 12582920 | tf_op jit(solution)/shard_map/ppermute | solution.py:386
  1497.7 6.8 collective-permute-done.26
  1504.4 5.3 bitcast_add_fusion
  1516.4 89.8 %collective-permute-done.29 = f32[2048,16]{0,1:T(8,128)} collective-permute-done((f32[2048,16]{0,1:T(8,128)S(1)}, f32[2048,16]{0,1:T(8,128)}, u32[]{:S(2)}, u32[]{:S(2)}) %collective-permute-start.29) | collective-permute-done | bytes 131104 | tf_op jit(solution)/shard_map/ppermute | solution.py:386
  1610.0 7.2 fusion.1
  (117 shorter events, 80.8 us)
Async XLA Ops:
  7.2 110.8 %all-gather.7.cloned.1.call-start = ((), (), s32[]{:S(2)}) async-start(), calls=%async_computation | async-start | bytes 1345536 | tf_op jit(solution)/shard_map/all_gather | solution.py:409
  80.1 54.3 %all-gather.9.cloned.1.call-start = ((), (), s32[]{:S(2)}) async-start(), calls=%async_computation.1 | async-start | bytes 1345536 | tf_op jit(solution)/shard_map/all_gather | solution.py:410
  86.8 324.1 %collective-permute-start = (bf16[2048,8,128]{2,1,0:T(8,128)(2,1)}, bf16[2048,8,128]{2,1,0:T(8,128)(2,1)}, u32[]{:S(2)}, u32[]{:S(2)}) collective-permute-start(bf16[2048,8,128]{2,1,0:T(8,128)(2,1)} %bitcast.15.refs_0_), channel_id=1, source_target_pairs={{0,4},{4,0},{1,5},{5,1},{2,6},{6,2},{3,7},{7,3}} | collective-permute-start | bytes 12582920 | tf_op jit(solution)/shard_map/ppermute | solution.py:386
  94.2 269.6 %collective-permute-start.22 = (bf16[3,256,1408]{2,1,0:T(8,128)(2,1)}, bf16[3,256,1408]{2,1,0:T(8,128)(2,1)}, u32[]{:S(2)}, u32[]{:S(2)}) collective-permute-start(bf16[3,256,1408]{2,1,0:T(8,128)(2,1)} %get-tuple-element.103), channel_id=1, source_target_pairs={{0,4},{4,0},{1,5},{5,1},{2,6},{6,2},{3,7},{7,3}} | collective-permute-start | bytes 6488072 | tf_op jit(solution)/shard_map/ppermute | solution.py:386
  99.0 266.3 %collective-permute-start.23 = (bf16[3,256,1408]{2,1,0:T(8,128)(2,1)}, bf16[3,256,1408]{2,1,0:T(8,128)(2,1)}, u32[]{:S(2)}, u32[]{:S(2)}) collective-permute-start(bf16[3,256,1408]{2,1,0:T(8,128)(2,1)} %get-tuple-element.99), channel_id=1, source_target_pairs={{0,4},{4,0},{1,5},{5,1},{2,6},{6,2},{3,7},{7,3}} | collective-permute-start | bytes 6488072 | tf_op jit(solution)/shard_map/ppermute | solution.py:386
  106.0 260.6 %collective-permute-start.24 = (bf16[3,1408,256]{2,1,0:T(8,128)(2,1)}, bf16[3,1408,256]{2,1,0:T(8,128)(2,1)}, u32[]{:S(2)}, u32[]{:S(2)}) collective-permute-start(bf16[3,1408,256]{2,1,0:T(8,128)(2,1)} %get-tuple-element.95), channel_id=1, source_target_pairs={{0,4},{4,0},{1,5},{5,1},{2,6},{6,2},{3,7},{7,3}} | collective-permute-start | bytes 6488072 | tf_op jit(solution)/shard_map/ppermute | solution.py:386
  108.4 251.5 %collective-permute-start.10 = (bf16[2,256,1408]{2,1,0:T(8,128)(2,1)}, bf16[2,256,1408]{2,1,0:T(8,128)(2,1)}, u32[]{:S(2)}, u32[]{:S(2)}) collective-permute-start(bf16[2,256,1408]{2,1,0:T(8,128)(2,1)} %get-tuple-element.111), channel_id=1, source_target_pairs={{0,4},{4,0},{1,5},{5,1},{2,6},{6,2},{3,7},{7,3}} | collective-permute-start | bytes 4325384 | tf_op jit(solution)/shard_map/ppermute | solution.py:386
  359.9 50.2 %collective-permute-start.19 = (bf16[3,256,1408]{2,1,0:T(8,128)(2,1)}, bf16[3,256,1408]{2,1,0:T(8,128)(2,1)}, u32[]{:S(2)}, u32[]{:S(2)}) collective-permute-start(bf16[3,256,1408]{2,1,0:T(8,128)(2,1)} %get-tuple-element.104), channel_id=1, source_target_pairs={{0,4},{4,0},{1,5},{5,1},{2,6},{6,2},{3,7},{7,3}} | collective-permute-start | bytes 6488072 | tf_op jit(solution)/shard_map/ppermute | solution.py:386
  363.8 324.4 %collective-permute-start.5 = (bf16[2048,8,128]{2,1,0:T(8,128)(2,1)}, bf16[2048,8,128]{2,1,0:T(8,128)(2,1)}, u32[]{:S(2)}, u32[]{:S(2)}) collective-permute-start(bf16[2048,8,128]{2,1,0:T(8,128)(2,1)} %bitcast.15.refs_0_), channel_id=1, source_target_pairs={{0,2},{1,3},{2,0},{3,1},{4,6},{5,7},{6,4},{7,5}} | collective-permute-start | bytes 12582920 | tf_op jit(solution)/shard_map/ppermute | solution.py:386
  365.3 91.2 %collective-permute-start.20 = (bf16[3,256,1408]{2,1,0:T(8,128)(2,1)}, bf16[3,256,1408]{2,1,0:T(8,128)(2,1)}, u32[]{:S(2)}, u32[]{:S(2)}) collective-permute-start(bf16[3,256,1408]{2,1,0:T(8,128)(2,1)} %get-tuple-element.100), channel_id=1, source_target_pairs={{0,4},{4,0},{1,5},{5,1},{2,6},{6,2},{3,7},{7,3}} | collective-permute-start | bytes 6488072 | tf_op jit(solution)/shard_map/ppermute | solution.py:386
  366.6 136.3 %collective-permute-start.21 = (bf16[3,1408,256]{2,1,0:T(8,128)(2,1)}, bf16[3,1408,256]{2,1,0:T(8,128)(2,1)}, u32[]{:S(2)}, u32[]{:S(2)}) collective-permute-start(bf16[3,1408,256]{2,1,0:T(8,128)(2,1)} %get-tuple-element.96), channel_id=1, source_target_pairs={{0,4},{4,0},{1,5},{5,1},{2,6},{6,2},{3,7},{7,3}} | collective-permute-start | bytes 6488072 | tf_op jit(solution)/shard_map/ppermute | solution.py:386
  410.2 139.0 %collective-permute-start.16 = (bf16[3,256,1408]{2,1,0:T(8,128)(2,1)}, bf16[3,256,1408]{2,1,0:T(8,128)(2,1)}, u32[]{:S(2)}, u32[]{:S(2)}) collective-permute-start(bf16[3,256,1408]{2,1,0:T(8,128)(2,1)} %get-tuple-element.105), channel_id=1, source_target_pairs={{0,4},{4,0},{1,5},{5,1},{2,6},{6,2},{3,7},{7,3}} | collective-permute-start | bytes 6488072 | tf_op jit(solution)/shard_map/ppermute | solution.py:386
  410.9 277.8 %collective-permute-start.2 = (bf16[2048,8,128]{2,1,0:T(8,128)(2,1)}, bf16[2048,8,128]{2,1,0:T(8,128)(2,1)}, u32[]{:S(2)}, u32[]{:S(2)}) collective-permute-start(bf16[2048,8,128]{2,1,0:T(8,128)(2,1)} %collective-permute-done.refs_0_), channel_id=1, source_target_pairs={{0,2},{1,3},{2,0},{3,1},{4,6},{5,7},{6,4},{7,5}} | collective-permute-start | bytes 12582920 | tf_op jit(solution)/shard_map/ppermute | solution.py:386
  456.5 139.0 %collective-permute-start.17 = (bf16[3,256,1408]{2,1,0:T(8,128)(2,1)}, bf16[3,256,1408]{2,1,0:T(8,128)(2,1)}, u32[]{:S(2)}, u32[]{:S(2)}) collective-permute-start(bf16[3,256,1408]{2,1,0:T(8,128)(2,1)} %get-tuple-element.101), channel_id=1, source_target_pairs={{0,4},{4,0},{1,5},{5,1},{2,6},{6,2},{3,7},{7,3}} | collective-permute-start | bytes 6488072 | tf_op jit(solution)/shard_map/ppermute | solution.py:386
  502.8 139.0 %collective-permute-start.18 = (bf16[3,1408,256]{2,1,0:T(8,128)(2,1)}, bf16[3,1408,256]{2,1,0:T(8,128)(2,1)}, u32[]{:S(2)}, u32[]{:S(2)}) collective-permute-start(bf16[3,1408,256]{2,1,0:T(8,128)(2,1)} %get-tuple-element.97), channel_id=1, source_target_pairs={{0,4},{4,0},{1,5},{5,1},{2,6},{6,2},{3,7},{7,3}} | collective-permute-start | bytes 6488072 | tf_op jit(solution)/shard_map/ppermute | solution.py:386
  549.2 139.0 %collective-permute-start.13 = (bf16[3,256,1408]{2,1,0:T(8,128)(2,1)}, bf16[3,256,1408]{2,1,0:T(8,128)(2,1)}, u32[]{:S(2)}, u32[]{:S(2)}) collective-permute-start(bf16[3,256,1408]{2,1,0:T(8,128)(2,1)} %get-tuple-element.106), channel_id=1, source_target_pairs={{0,4},{4,0},{1,5},{5,1},{2,6},{6,2},{3,7},{7,3}} | collective-permute-start | bytes 6488072 | tf_op jit(solution)/shard_map/ppermute | solution.py:386
  595.5 187.2 %collective-permute-start.4 = (bf16[2048,8,128]{2,1,0:T(8,128)(2,1)}, bf16[2048,8,128]{2,1,0:T(8,128)(2,1)}, u32[]{:S(2)}, u32[]{:S(2)}) collective-permute-start(bf16[2048,8,128]{2,1,0:T(8,128)(2,1)} %bitcast.15.refs_0_), channel_id=1, source_target_pairs={{0,1},{1,0},{2,3},{3,2},{4,5},{5,4},{6,7},{7,6}} | collective-permute-start | bytes 12582920 | tf_op jit(solution)/shard_map/ppermute | solution.py:386
  641.9 91.4 %collective-permute-start.14 = (bf16[3,256,1408]{2,1,0:T(8,128)(2,1)}, bf16[3,256,1408]{2,1,0:T(8,128)(2,1)S(1)}, u32[]{:S(2)}, u32[]{:S(2)}) collective-permute-start(bf16[3,256,1408]{2,1,0:T(8,128)(2,1)} %get-tuple-element.102), channel_id=1, source_target_pairs={{0,4},{4,0},{1,5},{5,1},{2,6},{6,2},{3,7},{7,3}} | collective-permute-start | bytes 6488072 | tf_op jit(solution)/shard_map/ppermute | solution.py:386
  688.2 96.5 %collective-permute-start.1 = (bf16[2048,8,128]{2,1,0:T(8,128)(2,1)}, bf16[2048,8,128]{2,1,0:T(8,128)(2,1)}, u32[]{:S(2)}, u32[]{:S(2)}) collective-permute-start(bf16[2048,8,128]{2,1,0:T(8,128)(2,1)} %collective-permute-done.refs_0_), channel_id=1, source_target_pairs={{0,1},{1,0},{2,3},{3,2},{4,5},{5,4},{6,7},{7,6}} | collective-permute-start | bytes 12582920 | tf_op jit(solution)/shard_map/ppermute | solution.py:386
  688.2 96.2 %collective-permute-start.6 = (bf16[2048,8,128]{2,1,0:T(8,128)(2,1)}, bf16[2048,8,128]{2,1,0:T(8,128)(2,1)}, u32[]{:S(2)}, u32[]{:S(2)}) collective-permute-start(bf16[2048,8,128]{2,1,0:T(8,128)(2,1)} %collective-permute-done.5.refs_2_), channel_id=1, source_target_pairs={{0,1},{1,0},{2,3},{3,2},{4,5},{5,4},{6,7},{7,6}} | collective-permute-start | bytes 12582920 | tf_op jit(solution)/shard_map/ppermute | solution.py:386
  688.7 97.8 %collective-permute-start.3 = (bf16[2048,8,128]{2,1,0:T(8,128)(2,1)}, bf16[2048,8,128]{2,1,0:T(8,128)(2,1)}, u32[]{:S(2)}, u32[]{:S(2)}) collective-permute-start(bf16[2048,8,128]{2,1,0:T(8,128)(2,1)} %collective-permute-done.2.refs_2_), channel_id=1, source_target_pairs={{0,1},{1,0},{2,3},{3,2},{4,5},{5,4},{6,7},{7,6}} | collective-permute-start | bytes 12582920 | tf_op jit(solution)/shard_map/ppermute | solution.py:386
  782.4 489.6 %collective-permute-start.11 = (bf16[2,256,1408]{2,1,0:T(8,128)(2,1)}, bf16[2,256,1408]{2,1,0:T(8,128)(2,1)}, u32[]{:S(2)}, u32[]{:S(2)}) collective-permute-start(bf16[2,256,1408]{2,1,0:T(8,128)(2,1)} %get-tuple-element.109), channel_id=1, source_target_pairs={{0,4},{4,0},{1,5},{5,1},{2,6},{6,2},{3,7},{7,3}} | collective-permute-start | bytes 4325384 | tf_op jit(solution)/shard_map/ppermute | solution.py:386
  782.7 489.3 %collective-permute-start.12 = (bf16[2,1408,256]{2,1,0:T(8,128)(2,1)}, bf16[2,1408,256]{2,1,0:T(8,128)(2,1)}, u32[]{:S(2)}, u32[]{:S(2)}) collective-permute-start(bf16[2,1408,256]{2,1,0:T(8,128)(2,1)} %get-tuple-element.107), channel_id=1, source_target_pairs={{0,4},{4,0},{1,5},{5,1},{2,6},{6,2},{3,7},{7,3}} | collective-permute-start | bytes 4325384 | tf_op jit(solution)/shard_map/ppermute | solution.py:386
  784.5 537.6 %collective-permute-start.7 = (bf16[2,256,1408]{2,1,0:T(8,128)(2,1)}, bf16[2,256,1408]{2,1,0:T(8,128)(2,1)}, u32[]{:S(2)}, u32[]{:S(2)}) collective-permute-start(bf16[2,256,1408]{2,1,0:T(8,128)(2,1)} %get-tuple-element.112), channel_id=1, source_target_pairs={{0,4},{4,0},{1,5},{5,1},{2,6},{6,2},{3,7},{7,3}} | collective-permute-start | bytes 4325384 | tf_op jit(solution)/shard_map/ppermute | solution.py:386
  784.8 537.3 %collective-permute-start.8 = (bf16[2,256,1408]{2,1,0:T(8,128)(2,1)}, bf16[2,256,1408]{2,1,0:T(8,128)(2,1)}, u32[]{:S(2)}, u32[]{:S(2)}) collective-permute-start(bf16[2,256,1408]{2,1,0:T(8,128)(2,1)} %get-tuple-element.110), channel_id=1, source_target_pairs={{0,4},{4,0},{1,5},{5,1},{2,6},{6,2},{3,7},{7,3}} | collective-permute-start | bytes 4325384 | tf_op jit(solution)/shard_map/ppermute | solution.py:386
  786.5 535.6 %collective-permute-start.9 = (bf16[2,1408,256]{2,1,0:T(8,128)(2,1)}, bf16[2,1408,256]{2,1,0:T(8,128)(2,1)}, u32[]{:S(2)}, u32[]{:S(2)}) collective-permute-start(bf16[2,1408,256]{2,1,0:T(8,128)(2,1)} %get-tuple-element.108), channel_id=1, source_target_pairs={{0,4},{4,0},{1,5},{5,1},{2,6},{6,2},{3,7},{7,3}} | collective-permute-start | bytes 4325384 | tf_op jit(solution)/shard_map/ppermute | solution.py:386
  1429.2 75.2 %collective-permute-start.26 = (f32[2048,512]{1,0:T(8,128)S(1)}, f32[2048,512]{1,0:T(8,128)S(1)}, u32[]{:S(2)}, u32[]{:S(2)}) collective-permute-start(f32[2048,512]{1,0:T(8,128)S(1)} %get-tuple-element.94), channel_id=1, source_target_pairs={{0,1},{1,0},{2,3},{3,2},{4,5},{5,4},{6,7},{7,6}} | collective-permute-start | bytes 12582920 | tf_op jit(solution)/shard_map/ppermute | solution.py:386
  1497.6 112.3 %collective-permute-start.25 = (f32[2048,512]{1,0:T(8,128)}, f32[2048,512]{1,0:T(8,128)}, u32[]{:S(2)}, u32[]{:S(2)}) collective-permute-start(f32[2048,512]{1,0:T(8,128)} %get-tuple-element.93), channel_id=1, source_target_pairs={{0,1},{1,0},{2,3},{3,2},{4,5},{5,4},{6,7},{7,6}} | collective-permute-start | bytes 12582920 | tf_op jit(solution)/shard_map/ppermute | solution.py:386
  1509.7 100.3 %collective-permute-start.27 = (f32[2048,512]{1,0:T(8,128)}, f32[2048,512]{1,0:T(8,128)}, u32[]{:S(2)}, u32[]{:S(2)}) collective-permute-start(f32[2048,512]{1,0:T(8,128)} %bitcast_add_fusion), channel_id=1, source_target_pairs={{0,2},{1,3},{2,0},{3,1},{4,6},{5,7},{6,4},{7,5}} | collective-permute-start | bytes 12582920 | tf_op jit(solution)/shard_map/ppermute | solution.py:386
  1512.6 93.6 %collective-permute-start.29 = (f32[2048,16]{0,1:T(8,128)S(1)}, f32[2048,16]{0,1:T(8,128)}, u32[]{:S(2)}, u32[]{:S(2)}) collective-permute-start(f32[2048,16]{0,1:T(8,128)S(1)} %copy.60), channel_id=1, source_target_pairs={{0,2},{1,3},{2,0},{3,1},{4,6},{5,7},{6,4},{7,5}} | collective-permute-start | bytes 393224 | tf_op jit(solution)/shard_map/ppermute | solution.py:386
  1515.6 92.1 %collective-permute-start.30 = (f32[2048,16]{0,1:T(8,128)}, f32[2048,16]{0,1:T(8,128)S(1)}, u32[]{:S(2)}, u32[]{:S(2)}) collective-permute-start(f32[2048,16]{0,1:T(8,128)} %copy.61), channel_id=1, source_target_pairs={{0,3},{1,2},{2,1},{3,0},{4,7},{5,6},{6,5},{7,4}} | collective-permute-start | bytes 393224 | tf_op jit(solution)/shard_map/ppermute | solution.py:386
  1515.9 91.8 %collective-permute-start.28 = (f32[2048,16]{0,1:T(8,128)S(1)}, f32[2048,16]{0,1:T(8,128)S(1)}, u32[]{:S(2)}, u32[]{:S(2)}) collective-permute-start(f32[2048,16]{0,1:T(8,128)S(1)} %copy.59), channel_id=1, source_target_pairs={{0,1},{1,0},{2,3},{3,2},{4,5},{5,4},{6,7},{7,6}} | collective-permute-start | bytes 393224 | tf_op jit(solution)/shard_map/ppermute | solution.py:386
  (11 other events, 236.4 us)
Sparse Core Ops, SparseCore 0:
  80.3 25.2 all-gather.6
  110.7 23.6 all-gather.8
where the time goes:
time: 1630 us; the launch traced here: 1620 us
  waiting for transfers between devices  721 us (44%)
  Pallas kernels  700 us (43%)
  starting transfers between devices  93 us (6%)
  local copies, waits for them, and re-layouts  64 us (4%)
  other arithmetic  31.4 us (2%)
    ppermute x31, waiting for transfers between devices, swap(): return lax.ppermute(value, axis, [(k, k ^ mask) for k in range(size)])  712 us
    pallas_call x6, Pallas kernels, expert_group(): pl.pallas_call(functools.partial(expert_kernel, e0, step_rows), grid_spec...  449 us
    pallas_call x2, Pallas kernels, gather_rows(): pl.pallas_call(functools.partial(gather_kernel, n_src, with_dy, region, e...  135 us
    ppermute x31, starting transfers between devices, swap(): return lax.ppermute(value, axis, [(k, k ^ mask) for k in range(size)])  92.9 us
    pallas_call x1, Pallas kernels, route_slots(): pl.pallas_call(functools.partial(route_kernel, n_pairs, top_k, experts, c...  66 us
    pallas_call x1, Pallas kernels, scatter_rows(): pl.pallas_call(functools.partial(scatter_kernel, exp_local, capacity, chu...  50.6 us
  transfers between devices with their start and end apart: 33, of which 14 were waited for; matrix products, arithmetic and copies ran while one was open for 5% of the time, Pallas kernels for 33%

commit v1 on v0

--- a/solution.py
+++ b/solution.py
@@ -10,9 +10,11 @@
 
 CAP_FACTOR = 3
 CHUNKS = 4
-GROUPS = (3, 3, 3, 3, 2, 2)
+GROUPS = (4, 4, 2, 2, 2, 1, 1)
+STAGES = ((0, 1), (2, 3, 4, 5, 6))
 PAD = 8
 LANES = 128
+N_OWN = 4
 SUB = 8
 INTERPRET = False
 VMEM_BYTES = 67_043_328
@@ -168,7 +170,8 @@
 
 
 def expert_kernel(e0, step_rows, nt_ref, mine_ref, xg_ref, dy_ref, w1o, w1p, w3o, w3p, w2o, w2p, *refs):
-    dx_ref, dr_ref, dw1_ref, dw3_ref, dw2_ref, h1, h3, da, hid, dh1, dh3, dw2t = refs[-12:]
+    *dx_refs, dr_ref = refs[len(refs) - 10 - 1 - N_OWN:-10]
+    dw1_ref, dw3_ref, dw2_ref, h1, h3, da, hid, dh1, dh3, dw2t = refs[-10:]
     e = pl.program_id(0)
     t = pl.program_id(1)
     region, j = t // CHUNKS, t % CHUNKS
@@ -213,12 +216,13 @@
         dyp = dy_ref[0, 0, :, pl.ds(other, half)].astype(jnp.float32)
         prod = dyo * dot(hid[...], w2o[0], NN) + dyp * dot(hid[...], w2p[0], NN)
         dr = jnp.sum(prod, axis=1, keepdims=True)
-        lane = lax.broadcasted_iota(jnp.int32, dr_ref.shape[2:], 1)
-        dr_ref[0, 0] = jnp.where(lane == e0 + e, dr, 0.0)
-        dxo = dot(dh1[...], w1o[0], NT) + dot(dh3[...], w3o[0], NT)
-        dx_ref[0, 0, :, pl.ds(mine, half)] = dxo.astype(jnp.bfloat16)
-        dxp = dot(dh1[...], w1p[0], NT) + dot(dh3[...], w3p[0], NT)
-        dx_ref[0, 0, :, pl.ds(other, half)] = dxp.astype(jnp.bfloat16)
+        dr_ref[0, 0] = jnp.broadcast_to(dr, (dr.shape[0], LANES)).T[:1]
+        dxo = (dot(dh1[...], w1o[0], NT) + dot(dh3[...], w3o[0], NT)).astype(jnp.bfloat16)
+        dxp = (dot(dh1[...], w1p[0], NT) + dot(dh3[...], w3p[0], NT)).astype(jnp.bfloat16)
+        chunk = dx_refs[0].shape[2]
+        for k, dx_ref in enumerate(dx_refs):
+            dx_ref[0, 0, :, pl.ds(mine, half)] = dxo[k * chunk:(k + 1) * chunk]
+            dx_ref[0, 0, :, pl.ds(other, half)] = dxp[k * chunk:(k + 1) * chunk]
 
     @pl.when(t == pl.num_programs(1) - 1)
     def _():
@@ -229,9 +233,13 @@
     exp_local, _, _, tile_rows, width = xg.shape
     half, d_ff = own[0].shape[1:]
     step_rows = 16
+    chunk = tile_rows // N_OWN
 
     def own_tile(e, t, nt_ref, _):
         return (e0 + e, jnp.minimum(jnp.where(t < CHUNKS, t, CHUNKS - 1), nt_ref[(e0 + e) * 2] - 1), 0, 0)
+
+    def own_rows(e, t, nt_ref, _):
+        return (e, jnp.minimum(jnp.where(t < CHUNKS, t, CHUNKS - 1), nt_ref[(e0 + e) * 2] - 1), 0, 0)
 
     def xg_tile(e, t, nt_ref, _):
         region = t // CHUNKS
@@ -242,8 +250,8 @@
     up = lambda at: pl.BlockSpec((1, half, d_ff), at)
     down = lambda at: pl.BlockSpec((1, d_ff, half), at)
     out_shape = [
-        jax.ShapeDtypeStruct((exp_local, CHUNKS, tile_rows, width // 2), jnp.bfloat16),
-        jax.ShapeDtypeStruct((exp_local, CHUNKS, tile_rows, LANES), jnp.float32),
+        *[jax.ShapeDtypeStruct((count, CHUNKS, chunk, width // 2), jnp.bfloat16)] * N_OWN,
+        jax.ShapeDtypeStruct((exp_local, CHUNKS, 1, tile_rows), jnp.float32),
         jax.ShapeDtypeStruct((exp_local, half, d_ff), jnp.float32),
         jax.ShapeDtypeStruct((exp_local, half, d_ff), jnp.float32),
         jax.ShapeDtypeStruct((exp_local, d_ff, half), jnp.float32),
@@ -261,8 +269,8 @@
                 up(at_own), up(at_peer), up(at_own), up(at_peer), down(at_own), down(at_peer),
             ] + [pl.BlockSpec(memory_space=pl.ANY)] * len(carried),
             out_specs=[
-                pl.BlockSpec((1, 1, tile_rows, width // 2), own_tile),
-                pl.BlockSpec((1, 1, tile_rows, LANES), own_tile),
+                *[pl.BlockSpec((1, 1, chunk, width // 2), own_rows)] * N_OWN,
+                pl.BlockSpec((1, 1, 1, tile_rows), own_tile),
                 up(at_own), up(at_own), down(at_own),
             ],
             scratch_shapes=[
@@ -275,103 +283,146 @@
                 pltpu.VMEM((half, d_ff), jnp.float32),
             ]),
         out_shape=out_shape,
-        input_output_aliases={n_in + k: k for k in range(len(carried))},
+        input_output_aliases={n_in + k: N_OWN + k for k in range(len(carried))},
         compiler_params=pltpu.CompilerParams(
             dimension_semantics=("arbitrary", "arbitrary"), vmem_limit_bytes=VMEM_BYTES),
         interpret=INTERPRET,
     )(nt.reshape(-1), mine, xg, dy, own[0], peer[0], own[1], peer[1], own[2], peer[2], *carried)
 
 
-def scatter_kernel(exp_local, capacity, chunk, tok_ref, dx_hbm, dr_hbm,
-                   dx_out, dr_out, acc, tmp, dx_v, dr_v, dx_sem, dr_sem):
+def combine_kernel(stage, counts, e0, exp_local, capacity, chunk, tok_ref, dr_ref, *refs):
+    stride = capacity + PAD
+    n_exp = sum(counts)
+    rows_hbm = refs[:N_OWN * len(counts)]
+    refs = refs[N_OWN * len(counts):]
+    first, last = stage == 0, stage == len(STAGES) - 1
+    if not first:
+        acc_in, refs = refs[0], refs[1:]
+    if last:
+        gx_out, dr_out, acc, tmp, rows_v, sem, acc_sem = refs
+    else:
+        acc_out, acc, tmp, rows_v, sem, acc_sem = refs
     src = pl.program_id(0)
-    stride = capacity + PAD
-    tok_dev = dx_out.shape[1]
-
-    def copies(e, j):
-        k = e * CHUNKS + j
-        rows = pl.ds(src * chunk, chunk)
-        return (pltpu.make_async_copy(dx_hbm.at[e, j, rows], dx_v.at[k], dx_sem.at[k]),
-                pltpu.make_async_copy(dr_hbm.at[e, j, rows], dr_v.at[k], dr_sem.at[k]))
-
-    def each(fn):
-        def per_expert(e, carry):
-            n = tok_ref[0, 0, e * stride + capacity + 1]
-            lax.fori_loop(0, (n + chunk - 1) // chunk, lambda j, c: fn(e, j, n, c), 0)
-            return carry
-
-        lax.fori_loop(0, exp_local, per_expert, 0)
-
-    def start(e, j, n, carry):
-        for copy in copies(e, j):
-            copy.start()
-        return carry
-
-    each(start)
-    acc[...] = jnp.zeros_like(acc)
-
-    def add(e, j, n, carry):
-        k = e * CHUNKS + j
-        for copy in copies(e, j):
-            copy.wait()
-        for c in range(SUB // 2):
-            tmp[pl.ds(c, chunk, stride=SUB), :] = dx_v[k, :, c * LANES:(c + 1) * LANES].astype(jnp.float32)
-        tmp[pl.ds(SUB // 2, chunk, stride=SUB), :] = dr_v[k]
-
-        def rows(r8, c):
-            r0 = r8 * 8
-            toks = [jnp.where(j * chunk + r0 + u < n, tok_ref[0, 0, e * stride + j * chunk + r0 + u], tok_dev)
+    tok_dev = acc.shape[0] // SUB - 1
+
+    def count_of(k, e):
+        return tok_ref[(k * exp_local + e0 + e) * stride + capacity + 1]
+
+    def tiles(n):
+        return (n + chunk - 1) // chunk
+
+    def start(k):
+        base = 0
+        for g, count in enumerate(counts):
+            ref = rows_hbm[g * N_OWN + k]
+
+            def per_expert(e, carry, ref=ref, base=base):
+                def one(j, c):
+                    at = (base + e) * CHUNKS + j
+                    pltpu.make_async_copy(ref.at[e, j], rows_v.at[k % 2, at], sem.at[k % 2, at]).start()
+                    return c
+
+                return lax.fori_loop(0, tiles(count_of(k, base + e)), one, carry)
+
+            lax.fori_loop(0, count, per_expert, 0)
+            base += count
+
+    @pl.when(src == 0)
+    def _():
+        if not first:
+            load = pltpu.make_async_copy(acc_in, acc, acc_sem)
+            load.start()
+        start(0)
+        tmp[...] = jnp.zeros_like(tmp)
+        if first:
+            acc[...] = jnp.zeros_like(acc)
+        else:
+            load.wait()
+
+    for k in range(1, N_OWN):
+        @pl.when(src == k - 1)
+        def _(k=k):
+            start(k)
+
+    buf = lax.rem(src, 2)
+    sub = lax.broadcasted_iota(jnp.int32, (SUB, LANES), 0)
+    lane = lax.broadcasted_iota(jnp.int32, (SUB, LANES), 1)
+
+    def per_expert(e, carry):
+        n = count_of(src, e)
+        here = (sub == SUB // 2) & (lane == src * exp_local + e0 + e)
+
+        def one(j, c):
+            at = e * CHUNKS + j
+            pltpu.make_async_copy(rows_hbm[0].at[0, 0], rows_v.at[buf, at], sem.at[buf, at]).wait()
+            for c4 in range(SUB // 2):
+                tmp[pl.ds(c4, chunk, stride=SUB), :] = rows_v[
+                    buf, at, :, c4 * LANES:(c4 + 1) * LANES].astype(jnp.float32)
+            slots = (src * exp_local + e0 + e) * stride + j * chunk
+            drs = (src * n_exp + e) * capacity + j * chunk
+
+            def rows(r8, c):
+                r0 = r8 * 8
+                toks = [jnp.where(j * chunk + r0 + u < n, tok_ref[slots + r0 + u], tok_dev) for u in range(8)]
+                ats = [pl.ds(pl.multiple_of(t * SUB, SUB), SUB) for t in toks]
+                sums = [acc[ats[u], :] + jnp.where(
+                    here, dr_ref[drs + r0 + u], tmp[pl.ds(pl.multiple_of((r0 + u) * SUB, SUB), SUB), :])
                     for u in range(8)]
-            ats = [pl.ds(pl.multiple_of(t * SUB, SUB), SUB) for t in toks]
-            sums = [acc[ats[u], :] + tmp[pl.ds(pl.multiple_of((r0 + u) * SUB, SUB), SUB), :] for u in range(8)]
-            for u in range(8):
-                acc[ats[u], :] = sums[u]
+                for u in range(8):
+                    acc[ats[u], :] = sums[u]
+                return c
+
+            lax.fori_loop(0, (jnp.minimum(n - j * chunk, chunk) + 7) // 8, rows, 0)
             return c
 
-        lax.fori_loop(0, (jnp.minimum(n - j * chunk, chunk) + 7) // 8, rows, 0)
-        return carry
-
-    each(add)
-    for c in range(SUB // 2):
-        dx_out[0, :, c * LANES:(c + 1) * LANES] = acc[pl.ds(c, tok_dev, stride=SUB), :]
-    dr_out[0] = acc[pl.ds(SUB // 2, tok_dev, stride=SUB), :]
-
-
-def scatter_rows(dx_rows, dr_rows, slot_tok, capacity, tok_dev):
-    exp_local, _, tile_rows, d_model = dx_rows.shape
-    chunk = capacity // CHUNKS
-    n_own = tile_rows // chunk
+        return lax.fori_loop(0, tiles(n), one, carry)
+
+    lax.fori_loop(0, n_exp, per_expert, 0)
+
+    @pl.when(src == N_OWN - 1)
+    def _():
+        if last:
+            for c in range(SUB // 2):
+                gx_out[:, c * LANES:(c + 1) * LANES] = acc[pl.ds(c, tok_dev, stride=SUB), :].astype(jnp.bfloat16)
+            dr_out[...] = acc[pl.ds(SUB // 2, tok_dev, stride=SUB), :]
+        else:
+            store = pltpu.make_async_copy(acc, acc_out, acc_sem)
+            store.start()
+            store.wait()
+
+
+def combine(stage, slot_home, dr, rows, carried, exp_local, capacity, tok_dev):
+    counts = [GROUPS[g] for g in STAGES[stage]]
+    e0 = sum(GROUPS[:STAGES[stage][0]])
+    n_exp = sum(counts)
+    chunk, d_model = rows[0].shape[2:]
+    smem = pl.BlockSpec(memory_space=pltpu.SMEM)
     hbm = pl.BlockSpec(memory_space=pl.ANY)
+    acc_shape = ((tok_dev + 1) * SUB, LANES)
+    if stage == len(STAGES) - 1:
+        out_specs = [pl.BlockSpec((tok_dev, d_model), lambda s: (0, 0)), pl.BlockSpec((tok_dev, LANES), lambda s: (0, 0))]
+        out_shape = [jax.ShapeDtypeStruct((tok_dev, d_model), jnp.bfloat16),
+                     jax.ShapeDtypeStruct((tok_dev, LANES), jnp.float32)]
+    else:
+        out_specs = [hbm]
+        out_shape = [jax.ShapeDtypeStruct(acc_shape, jnp.float32)]
     return pl.pallas_call(
-        functools.partial(scatter_kernel, exp_local, capacity, chunk),
-        grid_spec=pltpu.PrefetchScalarGridSpec(
-            num_scalar_prefetch=0,
-            grid=(n_own,),
-            in_specs=[
-                pl.BlockSpec((1, 1, slot_tok.shape[2]), lambda s, *_: (s, 0, 0), memory_space=pltpu.SMEM),
-                hbm, hbm,
-            ],
-            out_specs=[
-                pl.BlockSpec((1, tok_dev, d_model), lambda s, *_: (s, 0, 0)),
-                pl.BlockSpec((1, tok_dev, LANES), lambda s, *_: (s, 0, 0)),
-            ],
-            scratch_shapes=[
-                pltpu.VMEM(((tok_dev + 1) * SUB, LANES), jnp.float32),
-                pltpu.VMEM((chunk * SUB, LANES), jnp.float32),
-                pltpu.VMEM((exp_local * CHUNKS, chunk, d_model), jnp.bfloat16),
-                pltpu.VMEM((exp_local * CHUNKS, chunk, LANES), jnp.float32),
-                pltpu.SemaphoreType.DMA((exp_local * CHUNKS,)),
-                pltpu.SemaphoreType.DMA((exp_local * CHUNKS,)),
-            ]),
-        out_shape=[
-            jax.ShapeDtypeStruct((n_own, tok_dev, d_model), jnp.float32),
-            jax.ShapeDtypeStruct((n_own, tok_dev, LANES), jnp.float32),
+        functools.partial(combine_kernel, stage, counts, e0, exp_local, capacity, chunk),
+        grid=(N_OWN,),
+        in_specs=[smem, smem] + [hbm] * (len(rows) + len(carried)),
+        out_specs=out_specs,
+        out_shape=out_shape,
+        scratch_shapes=[
+            pltpu.VMEM(acc_shape, jnp.float32),
+            pltpu.VMEM((chunk * SUB, LANES), jnp.float32),
+            pltpu.VMEM((2, n_exp * CHUNKS, chunk, d_model), jnp.bfloat16),
+            pltpu.SemaphoreType.DMA((2, n_exp * CHUNKS)),
+            pltpu.SemaphoreType.DMA,
         ],
         compiler_params=pltpu.CompilerParams(
             dimension_semantics=("arbitrary",), vmem_limit_bytes=VMEM_BYTES),
-        name="scatter_rows",
         interpret=INTERPRET,
-    )(slot_tok, dx_rows, dr_rows)
+    )(slot_home, dr, *rows, *carried)
 
 
 def solution(mesh):
@@ -406,6 +457,9 @@
 
         slot_tok, slot_gate = route_slots(
             expert_ids.reshape(-1), route_w.reshape(-1), top_k, experts, capacity)
+        slot_home = slot_tok.reshape(n_ep, -1)
+        slot_home = jnp.stack(
+            [lax.dynamic_index_in_dim(slot_home, my_ep ^ b, axis=0, keepdims=False) for b in range(n_ep)]).reshape(-1)
         slot_tok = lax.all_gather(slot_tok, ("fsdp", "ep"), axis=0, tiled=False)
         slot_gate = lax.all_gather(slot_gate, ("fsdp", "ep"), axis=0, tiled=False)
 
@@ -425,28 +479,28 @@
 
         own = (w_gate, w_up, w_down)
         mine = my_fsdp.astype(jnp.int32).reshape(1)
-        carried = ()
+        carried, sums = (), ()
         e0 = 0
-        for count in GROUPS:
+        rows = []
+        for g, count in enumerate(GROUPS):
             peer = [swap(w[e0:e0 + count], "fsdp", 1) for w in own]
-            carried = expert_group(e0, count, xg, dy, nt, mine, own, peer, carried)
+            out = expert_group(e0, count, xg, dy, nt, mine, own, peer, carried)
+            dx_g, carried = out[:n_ep], out[n_ep:]
+            rows += [dx_g[0]] + [swap(dx_g[b], "ep", b) for b in range(1, n_ep)]
             e0 += count
-        dx_rows, dr_rows, grad_w_gate, grad_w_up, grad_w_down = carried
-
-        part, dr_part = scatter_rows(dx_rows, dr_rows, slot_tok[:n_ep], capacity, tok_dev)
-        from_core_near = swap(part[1], "ep", 1)
-        from_core_far = swap(part[3], "ep", 1)
-        far = part[2] + from_core_far
-        near = part[0] + from_core_near
-        grad_x = (near + swap(far, "ep", 2)).astype(jnp.bfloat16)
-        dr_mine = dr_part[:, :, :exp_local]
-        by_ep = jnp.stack([dr_mine[0]] + [swap(dr_mine[b], "ep", b) for b in range(1, n_ep)])
-        rel = (expert_ids // exp_local) ^ my_ep
-        loc = expert_ids % exp_local
-        hit = ((rel[:, :, None, None] == jnp.arange(n_ep)[None, None, :, None])
-               & (loc[:, :, None, None] == jnp.arange(exp_local)[None, None, None, :]))
-        dense = jnp.transpose(by_ep, (1, 0, 2))[:, None]
-        route_grad = jnp.sum(jnp.where(hit, dense, 0.0), axis=(2, 3))
+            for stage, groups in enumerate(STAGES):
+                if g == groups[-1]:
+                    dr = carried[0][e0 - sum(GROUPS[k] for k in groups):e0].reshape(-1, CHUNKS, n_ep, chunk)
+                    dr = dr.transpose(2, 0, 1, 3).reshape(n_ep, -1)
+                    dr = jnp.concatenate(
+                        [dr[0]] + [swap(dr[b], "ep", b) for b in range(1, n_ep)])
+                    sums = combine(stage, slot_home, dr, rows, sums, exp_local, capacity, tok_dev)
+                    rows = []
+        _, grad_w_gate, grad_w_up, grad_w_down = carried
+        grad_x, dr_tok = sums
+        place = ((expert_ids // exp_local) ^ my_ep) * exp_local + expert_ids % exp_local
+        hit = place[:, :, None] == jnp.arange(LANES, dtype=jnp.int32)
+        route_grad = jnp.sum(jnp.where(hit, dr_tok[:, None, :], 0.0), axis=2)
         return grad_x, route_grad, grad_w_gate, grad_w_up, grad_w_down
 
     return jax.shard_map(

time: 1630 us -> 1980 us (1.21)
  waiting for transfers between devices: 721 us -> 1060 us
    ppermute x31 -> x55, waiting for transfers between devices: 712 us -> 1060 us  [swap(): return lax.ppermute(value, axis, [(k, k ^ mask) for k in range(size)])]
    pallas_call x1 -> x2, Pallas kernels: 50.6 us -> 60.4 us  [combine(): pl.pallas_call(functools.partial(combine_kernel, stage, counts, e0, exp_l...]
    pallas_call x6 -> x7, Pallas kernels: 449 us -> 455 us  [expert_group(): pl.pallas_call(functools.partial(expert_kernel, e0, step_rows), grid_spec...]
    ppermute x31 -> x55, starting transfers between devices: 92.9 us -> 99.5 us  [swap(): return lax.ppermute(value, axis, [(k, k ^ mask) for k in range(size)])]
  transfers between devices with their start and end apart: 33 -> 57, of which waited for: 14 -> 27; matrix products, arithmetic and copies ran while one was open for 5% -> 4% of each run, Pallas kernels for 33% -> 30%
where the time goes in v1:
time: 1980 us
  waiting for transfers between devices  1060 us (54%)
  Pallas kernels  717 us (36%)
  starting transfers between devices  99.9 us (5%)
  local copies, waits for them, and re-layouts  58.1 us (3%)
  other arithmetic  25.4 us (1%)
    ppermute x55, waiting for transfers between devices, swap(): return lax.ppermute(value, axis, [(k, k ^ mask) for k in range(size)])  1060 us
    pallas_call x7, Pallas kernels, expert_group(): pl.pallas_call(functools.partial(expert_kernel, e0, step_rows), grid_spec...  455 us
    pallas_call x2, Pallas kernels, gather_rows(): pl.pallas_call(functools.partial(gather_kernel, n_src, with_dy, region, e...  135 us
    ppermute x55, starting transfers between devices, swap(): return lax.ppermute(value, axis, [(k, k ^ mask) for k in range(size)])  99.5 us
    pallas_call x1, Pallas kernels, route_slots(): pl.pallas_call(functools.partial(route_kernel, n_pairs, top_k, experts, c...  66 us
    pallas_call x2, Pallas kernels, combine(): pl.pallas_call(functools.partial(combine_kernel, stage, counts, e0, exp_l...  60.4 us
  transfers between devices with their start and end apart: 57, of which 27 were waited for; matrix products, arithmetic and copies ran while one was open for 4% of the time, Pallas kernels for 30%

profile of v1, /device:TPU:0, one launch (start us, length us, event | category | flops | bytes accessed | tf_op | source)
XLA Modules:
  0.0 1976.8 jit_solution(11461006666017342074)
XLA Ops:
  12.4 66.0 %route.1 = (s32[37376]{0:T(1024)}, f32[37376]{0:T(1024)}) custom-call(s32[12288]{0:T(1024)} %reshape.106.ids_ref, f32[12288]{0:T(1024)} %reshape.107.gate_ref), custom_call_target="tpu_custom_call" | custom-call | tf_op jit(solution)/shard_map/route/pallas_call | solution.py:52
  132.2 165.8 %collective-permute-done.10.w1p = bf16[1,256,1408]{2,1,0:T(8,128)(2,1)S(1)} collective-permute-done((bf16[1,256,1408]{2,1,0:T(8,128)(2,1)}, bf16[1,256,1408]{2,1,0:T(8,128)(2,1)S(1)}, u32[]{:S(2)}, u32[]{:S(2)}) %collective-permute-start.10) | collective-permute-done | bytes 720928 | tf_op jit(solution)/shard_map/ppermute | solution.py:437
  302.2 30.6 %collective-permute-done.16.w1p = bf16[2,256,1408]{2,1,0:T(8,128)(2,1)} collective-permute-done((bf16[2,256,1408]{2,1,0:T(8,128)(2,1)}, bf16[2,256,1408]{2,1,0:T(8,128)(2,1)}, u32[]{:S(2)}, u32[]{:S(2)}) %collective-permute-start.16) | collective-permute-done | bytes 1441824 | tf_op jit(solution)/shard_map/ppermute | solution.py:437
  333.7 30.0 %collective-permute-done.17.w3p = bf16[2,256,1408]{2,1,0:T(8,128)(2,1)} collective-permute-done((bf16[2,256,1408]{2,1,0:T(8,128)(2,1)}, bf16[2,256,1408]{2,1,0:T(8,128)(2,1)}, u32[]{:S(2)}, u32[]{:S(2)}) %collective-permute-start.17) | collective-permute-done | bytes 1441824 | tf_op jit(solution)/shard_map/ppermute | solution.py:437
  365.2 29.3 %collective-permute-done.18.w2p = bf16[2,1408,256]{2,1,0:T(8,128)(2,1)} collective-permute-done((bf16[2,1408,256]{2,1,0:T(8,128)(2,1)}, bf16[2,1408,256]{2,1,0:T(8,128)(2,1)}, u32[]{:S(2)}, u32[]{:S(2)}) %collective-permute-start.18) | collective-permute-done | bytes 1441824 | tf_op jit(solution)/shard_map/ppermute | solution.py:437
  395.5 30.0 %collective-permute-done.13.w1p = bf16[2,256,1408]{2,1,0:T(8,128)(2,1)} collective-permute-done((bf16[2,256,1408]{2,1,0:T(8,128)(2,1)}, bf16[2,256,1408]{2,1,0:T(8,128)(2,1)}, u32[]{:S(2)}, u32[]{:S(2)}) %collective-permute-start.13) | collective-permute-done | bytes 1441824 | tf_op jit(solution)/shard_map/ppermute | solution.py:437
  427.0 91.1 %collective-permute-done.14.w3p = bf16[2,256,1408]{2,1,0:T(8,128)(2,1)} collective-permute-done((bf16[2,256,1408]{2,1,0:T(8,128)(2,1)}, bf16[2,256,1408]{2,1,0:T(8,128)(2,1)}, u32[]{:S(2)}, u32[]{:S(2)}) %collective-permute-start.14) | collective-permute-done | bytes 1441824 | tf_op jit(solution)/shard_map/ppermute | solution.py:437
  520.3 89.4 %collective-permute-done.15.w2p = bf16[2,1408,256]{2,1,0:T(8,128)(2,1)} collective-permute-done((bf16[2,1408,256]{2,1,0:T(8,128)(2,1)}, bf16[2,1408,256]{2,1,0:T(8,128)(2,1)}, u32[]{:S(2)}, u32[]{:S(2)}) %collective-permute-start.15) | collective-permute-done | bytes 1441824 | tf_op jit(solution)/shard_map/ppermute | solution.py:437
  621.2 54.1 %collective-permute-done.27.w2p = bf16[4,1408,256]{2,1,0:T(8,128)(2,1)} collective-permute-done((bf16[4,1408,256]{2,1,0:T(8,128)(2,1)}, bf16[4,1408,256]{2,1,0:T(8,128)(2,1)}, u32[]{:S(2)}, u32[]{:S(2)}) %collective-permute-start.27) | collective-permute-done | bytes 2883616 | tf_op jit(solution)/shard_map/ppermute | solution.py:437
  675.3 61.8 %collective-permute-done.22.w1p = bf16[4,256,1408]{2,1,0:T(8,128)(2,1)} collective-permute-done((bf16[4,256,1408]{2,1,0:T(8,128)(2,1)}, bf16[4,256,1408]{2,1,0:T(8,128)(2,1)}, u32[]{:S(2)}, u32[]{:S(2)}) %collective-permute-start.22) | collective-permute-done | bytes 2883616 | tf_op jit(solution)/shard_map/ppermute | solution.py:437
  739.3 57.6 %collective-permute-done.23.w3p = bf16[4,256,1408]{2,1,0:T(8,128)(2,1)} collective-permute-done((bf16[4,256,1408]{2,1,0:T(8,128)(2,1)}, bf16[4,256,1408]{2,1,0:T(8,128)(2,1)}, u32[]{:S(2)}, u32[]{:S(2)}) %collective-permute-start.23) | collective-permute-done | bytes 2883616 | tf_op jit(solution)/shard_map/ppermute | solution.py:437
  800.2 59.4 %collective-permute-done.24.w2p = bf16[4,1408,256]{2,1,0:T(8,128)(2,1)} collective-permute-done((bf16[4,1408,256]{2,1,0:T(8,128)(2,1)}, bf16[4,1408,256]{2,1,0:T(8,128)(2,1)}, u32[]{:S(2)}, u32[]{:S(2)}) %collective-permute-start.24) | collective-permute-done | bytes 2883616 | tf_op jit(solution)/shard_map/ppermute | solution.py:437
  864.6 68.4 %shard_map.110 = (bf16[16,2,4,576,1024]{4,3,2,1,0:T(8,128)(2,1)}, bf16[16,4,576,512]{3,2,1,0:T(8,128)(2,1)}) custom-call(s32[32]{0:T(128)} %reshape.112.nt_ref, s32[4,1,9344]{2,1,0:T(1,128)} %pad_add_fusion.2.tok_ref, f32[4,1,9344]{2,1,0:T(1,128)} %pad_maximum_fusion.1.gate_ref, bf16[2048,8,128]{2,1,0:T(8,128)(2,1)} %bitcast.6.refs_0_, ...), custom_call_target="tpu_custom_call" | custom-call | tf_op jit(solution)/shard_map/pallas_call | solution.py:141
  933.1 66.5 %shard_map.111.xg_ref = bf16[16,2,4,576,1024]{4,3,2,1,0:T(8,128)(2,1)} custom-call(s32[32]{0:T(128)} %reshape.112.nt_ref, s32[4,1,9344]{2,1,0:T(1,128)} %pad_add_fusion.1.tok_ref, f32[4,1,9344]{2,1,0:T(1,128)} %pad_maximum_fusion.gate_ref, bf16[2048,8,128]{2,1,0:T(8,128)(2,1)} %collective-permute-done.refs_0_, ...), custom_call_target="tpu_custom_call", output_to_operand_aliasing={{}: (7, {})} | custom-call | tf_op jit(solution)/shard_map/pallas_call | solution.py:141
  999.6 98.9 %shard_map.112 = (bf16[4,4,144,512]{3,2,1,0:T(8,128)(2,1)}, bf16[4,4,144,512]{3,2,1,0:T(8,128)(2,1)}, bf16[4,4,144,512]{3,2,1,0:T(8,128)(2,1)}, bf16[4,4,144,512...) custom-call(s32[32]{0:T(128)} %reshape.112.nt_ref, ...), custom_call_target="tpu_custom_call" | custom-call | tf_op jit(solution)/shard_map/pallas_call | solution.py:261
  1098.5 152.3 %shard_map.113 = (bf16[4,4,144,512]{3,2,1,0:T(8,128)(2,1)}, bf16[4,4,144,512]{3,2,1,0:T(8,128)(2,1)}, bf16[4,4,144,512]{3,2,1,0:T(8,128)(2,1)}, bf16[4,4,144,512...) custom-call(s32[32]{0:T(128)} %reshape.112.nt_ref, ...), custom_call_target="tpu_custom_call", output_to_operand_aliasing={{4}: (10, {}), {5}: (11, {}), {6}: (12, {}), {7}: (13, {})} | custom-call | tf_op jit(solution)/shard_map/pallas_call | solution.py:261
  1252.5 50.6 %shard_map.114 = (bf16[2,4,144,512]{3,2,1,0:T(8,128)(2,1)}, bf16[2,4,144,512]{3,2,1,0:T(8,128)(2,1)}, bf16[2,4,144,512]{3,2,1,0:T(8,128)(2,1)}, bf16[2,4,144,512...) custom-call(s32[32]{0:T(128)} %reshape.112.nt_ref, ...), custom_call_target="tpu_custom_call", output_to_operand_aliasing={{4}: (10, {}), {5}: (11, {}), {6}: (12, {}), {7}: (13, {})} | custom-call | tf_op jit(solution)/shard_map/pallas_call | solution.py:261
  1303.1 50.7 %shard_map.115 = (bf16[2,4,144,512]{3,2,1,0:T(8,128)(2,1)}, bf16[2,4,144,512]{3,2,1,0:T(8,128)(2,1)}, bf16[2,4,144,512]{3,2,1,0:T(8,128)(2,1)}, bf16[2,4,144,512...) custom-call(s32[32]{0:T(128)} %reshape.112.nt_ref, ...), custom_call_target="tpu_custom_call", output_to_operand_aliasing={{4}: (10, {}), {5}: (11, {}), {6}: (12, {}), {7}: (13, {})} | custom-call | tf_op jit(solution)/shard_map/pallas_call | solution.py:261
  1353.8 50.7 %shard_map.116 = (bf16[2,4,144,512]{3,2,1,0:T(8,128)(2,1)}, bf16[2,4,144,512]{3,2,1,0:T(8,128)(2,1)}, bf16[2,4,144,512]{3,2,1,0:T(8,128)(2,1)}, bf16[2,4,144,512...) custom-call(s32[32]{0:T(128)} %reshape.112.nt_ref, ...), custom_call_target="tpu_custom_call", output_to_operand_aliasing={{4}: (10, {}), {5}: (11, {}), {6}: (12, {}), {7}: (13, {})} | custom-call | tf_op jit(solution)/shard_map/pallas_call | solution.py:261
  1404.5 25.9 %shard_map.117 = (bf16[1,4,144,512]{3,2,1,0:T(8,128)(2,1)}, bf16[1,4,144,512]{3,2,1,0:T(8,128)(2,1)}, bf16[1,4,144,512]{3,2,1,0:T(8,128)(2,1)}, bf16[1,4,144,512...) custom-call(s32[32]{0:T(128)} %reshape.112.nt_ref, ...), custom_call_target="tpu_custom_call", output_to_operand_aliasing={{4}: (10, {}), {5}: (11, {}), {6}: (12, {}), {7}: (13, {})} | custom-call | tf_op jit(solution)/shard_map/pallas_call | solution.py:261
  1430.5 26.1 %shard_map.118 = (bf16[1,4,144,512]{3,2,1,0:T(8,128)(2,1)}, bf16[1,4,144,512]{3,2,1,0:T(8,128)(2,1)}, bf16[1,4,144,512]{3,2,1,0:T(8,128)(2,1)}, bf16[1,4,144,512...) custom-call(s32[32]{0:T(128)} %reshape.112.nt_ref, ...), custom_call_target="tpu_custom_call", output_to_operand_aliasing={{4}: (10, {}), {5}: (11, {}), {6}: (12, {}), {7}: (13, {})} | custom-call | tf_op jit(solution)/shard_map/pallas_call | solution.py:261
  1456.7 61.6 %collective-permute-start.43 = (bf16[1,4,144,512]{3,2,1,0:T(8,128)(2,1)}, bf16[1,4,144,512]{3,2,1,0:T(8,128)(2,1)S(1)}, u32[]{:S(2)}, u32[]{:S(2)}) collective-permute-start(bf16[1,4,144,512]{3,2,1,0:T(8,128)(2,1)} %get-tuple-element.113), channel_id=1, source_target_pairs={{0,1},{1,0},{2,3},{3,2},{4,5},{5,4},{6,7},{7,6}} | collective-permute-start | bytes 1769480 | tf_op jit(solution)/shard_map/ppermute | solution.py:437
  1580.0 23.9 %collective-permute-done.38.refs_10_ = bf16[2,4,144,512]{3,2,1,0:T(8,128)(2,1)} collective-permute-done((bf16[2,4,144,512]{3,2,1,0:T(8,128)(2,1)}, bf16[2,4,144,512]{3,2,1,0:T(8,128)(2,1)}, u32[]{:S(2)}, u32[]{:S(2)}) %collective-permute-start.38) | collective-permute-done | bytes 1179680 | tf_op jit(solution)/shard_map/ppermute | solution.py:437
  1604.5 25.6 %collective-permute-done.39.refs_11_ = bf16[2,4,144,512]{3,2,1,0:T(8,128)(2,1)} collective-permute-done((bf16[2,4,144,512]{3,2,1,0:T(8,128)(2,1)}, bf16[2,4,144,512]{3,2,1,0:T(8,128)(2,1)}, u32[]{:S(2)}, u32[]{:S(2)}) %collective-permute-start.39) | collective-permute-done | bytes 1179680 | tf_op jit(solution)/shard_map/ppermute | solution.py:437
  1633.1 46.6 %collective-permute-done.53.refs_6_ = bf16[4,4,144,512]{3,2,1,0:T(8,128)(2,1)} collective-permute-done((bf16[4,4,144,512]{3,2,1,0:T(8,128)(2,1)}, bf16[4,4,144,512]{3,2,1,0:T(8,128)(2,1)}, u32[]{:S(2)}, u32[]{:S(2)}) %collective-permute-start.53) | collective-permute-done | bytes 2359328 | tf_op jit(solution)/shard_map/ppermute | solution.py:437
  1681.2 50.0 %collective-permute-done.54.refs_7_ = bf16[4,4,144,512]{3,2,1,0:T(8,128)(2,1)} collective-permute-done((bf16[4,4,144,512]{3,2,1,0:T(8,128)(2,1)}, bf16[4,4,144,512]{3,2,1,0:T(8,128)(2,1)}, u32[]{:S(2)}, u32[]{:S(2)}) %collective-permute-start.54) | collective-permute-done | bytes 2359328 | tf_op jit(solution)/shard_map/ppermute | solution.py:437
  1731.3 49.5 %collective-permute-done.50.refs_2_ = bf16[4,4,144,512]{3,2,1,0:T(8,128)(2,1)} collective-permute-done((bf16[4,4,144,512]{3,2,1,0:T(8,128)(2,1)}, bf16[4,4,144,512]{3,2,1,0:T(8,128)(2,1)}, u32[]{:S(2)}, u32[]{:S(2)}) %collective-permute-start.50) | collective-permute-done | bytes 2359328 | tf_op jit(solution)/shard_map/ppermute | solution.py:437
  1782.4 50.0 %collective-permute-done.51.refs_3_ = bf16[4,4,144,512]{3,2,1,0:T(8,128)(2,1)} collective-permute-done((bf16[4,4,144,512]{3,2,1,0:T(8,128)(2,1)}, bf16[4,4,144,512]{3,2,1,0:T(8,128)(2,1)}, u32[]{:S(2)}, u32[]{:S(2)}) %collective-permute-start.51) | collective-permute-done | bytes 2359328 | tf_op jit(solution)/shard_map/ppermute | solution.py:437
  1835.4 30.5 %shard_map.119.refs_20_ = f32[16392,128]{1,0:T(8,128)} custom-call(s32[37376]{0:T(1024)} %reshape.109.tok_ref, f32[18432]{0:T(1024)} %pad_maximum_fusion.3.dr_ref, bf16[4,4,144,512]{3,2,1,0:T(8,128)(2,1)} %get-tuple-element.116.refs_0_, bf16[4,4,144,512]{3,2,1,0:T(8,128)(2,1)} %collective-permute-done.49.refs_1_, ...), custom_call_target="tpu_custom_call" | custom-call | tf_op jit(solution)/shard_map/pallas_call | solution.py:409
  1882.9 24.3 %collective-permute-done.32.refs_2_ = bf16[2,4,144,512]{3,2,1,0:T(8,128)(2,1)} collective-permute-done((bf16[2,4,144,512]{3,2,1,0:T(8,128)(2,1)}, bf16[2,4,144,512]{3,2,1,0:T(8,128)(2,1)}, u32[]{:S(2)}, u32[]{:S(2)}) %collective-permute-start.32) | collective-permute-done | bytes 1179680 | tf_op jit(solution)/shard_map/ppermute | solution.py:437
  1907.3 25.7 %collective-permute-done.33.refs_3_ = bf16[2,4,144,512]{3,2,1,0:T(8,128)(2,1)} collective-permute-done((bf16[2,4,144,512]{3,2,1,0:T(8,128)(2,1)}, bf16[2,4,144,512]{3,2,1,0:T(8,128)(2,1)}, u32[]{:S(2)}, u32[]{:S(2)}) %collective-permute-start.33) | collective-permute-done | bytes 1179680 | tf_op jit(solution)/shard_map/ppermute | solution.py:437
  1933.0 29.9 %shard_map.120 = (bf16[2048,512]{1,0:T(8,128)(2,1)}, f32[2048,128]{1,0:T(8,128)}) custom-call(s32[37376]{0:T(1024)} %reshape.109.tok_ref, f32[18432]{0:T(1024)} %pad_maximum_fusion.2.dr_ref, bf16[2,4,144,512]{3,2,1,0:T(8,128)(2,1)} %get-tuple-element.96.refs_0_, bf16[2,4,144,512]{3,2,1,0:T(8,128)(2,1)} %collective-permute-done.31.refs_1_, ...), custom_call_target="tpu_custom_call" | custom-call | tf_op jit(solution)/shard_map/pallas_call | solution.py:409
  (183 shorter events, 189.1 us)
Async XLA Ops:
  7.2 120.3 %all-gather.7.cloned.1.call-start = ((), (), s32[]{:S(2)}) async-start(), calls=%async_computation | async-start | bytes 1345536 | tf_op jit(solution)/shard_map/all_gather | solution.py:463
  80.1 533.2 %all-gather.9.cloned.1.call-start = ((), (), s32[]{:S(2)}) async-start(), calls=%async_computation.1 | async-start | bytes 1345536 | tf_op jit(solution)/shard_map/all_gather | solution.py:464
  86.9 432.7 %collective-permute-start = (bf16[2048,8,128]{2,1,0:T(8,128)(2,1)}, bf16[2048,8,128]{2,1,0:T(8,128)(2,1)}, u32[]{:S(2)}, u32[]{:S(2)}) collective-permute-start(bf16[2048,8,128]{2,1,0:T(8,128)(2,1)} %bitcast.6.refs_0_), channel_id=1, source_target_pairs={{0,4},{4,0},{1,5},{5,1},{2,6},{6,2},{3,7},{7,3}} | collective-permute-start | bytes 12582920 | tf_op jit(solution)/shard_map/ppermute | solution.py:437
  92.4 206.5 %collective-permute-start.19 = (bf16[2,256,1408]{2,1,0:T(8,128)(2,1)}, bf16[2,256,1408]{2,1,0:T(8,128)(2,1)}, u32[]{:S(2)}, u32[]{:S(2)}) collective-permute-start(bf16[2,256,1408]{2,1,0:T(8,128)(2,1)} %get-tuple-element.165), channel_id=1, source_target_pairs={{0,4},{4,0},{1,5},{5,1},{2,6},{6,2},{3,7},{7,3}} | collective-permute-start | bytes 4325384 | tf_op jit(solution)/shard_map/ppermute | solution.py:437
  96.8 203.3 %collective-permute-start.20 = (bf16[2,256,1408]{2,1,0:T(8,128)(2,1)}, bf16[2,256,1408]{2,1,0:T(8,128)(2,1)}, u32[]{:S(2)}, u32[]{:S(2)}) collective-permute-start(bf16[2,256,1408]{2,1,0:T(8,128)(2,1)} %get-tuple-element.162), channel_id=1, source_target_pairs={{0,4},{4,0},{1,5},{5,1},{2,6},{6,2},{3,7},{7,3}} | collective-permute-start | bytes 4325384 | tf_op jit(solution)/shard_map/ppermute | solution.py:437
  103.3 197.7 %collective-permute-start.21 = (bf16[2,1408,256]{2,1,0:T(8,128)(2,1)}, bf16[2,1408,256]{2,1,0:T(8,128)(2,1)}, u32[]{:S(2)}, u32[]{:S(2)}) collective-permute-start(bf16[2,1408,256]{2,1,0:T(8,128)(2,1)} %get-tuple-element.159), channel_id=1, source_target_pairs={{0,4},{4,0},{1,5},{5,1},{2,6},{6,2},{3,7},{7,3}} | collective-permute-start | bytes 4325384 | tf_op jit(solution)/shard_map/ppermute | solution.py:437
  104.5 193.5 %collective-permute-start.10 = (bf16[1,256,1408]{2,1,0:T(8,128)(2,1)}, bf16[1,256,1408]{2,1,0:T(8,128)(2,1)S(1)}, u32[]{:S(2)}, u32[]{:S(2)}) collective-permute-start(bf16[1,256,1408]{2,1,0:T(8,128)(2,1)} %get-tuple-element.172), channel_id=1, source_target_pairs={{0,4},{4,0},{1,5},{5,1},{2,6},{6,2},{3,7},{7,3}} | collective-permute-start | bytes 2162696 | tf_op jit(solution)/shard_map/ppermute | solution.py:437
  301.0 124.5 %collective-permute-start.13 = (bf16[2,256,1408]{2,1,0:T(8,128)(2,1)}, bf16[2,256,1408]{2,1,0:T(8,128)(2,1)}, u32[]{:S(2)}, u32[]{:S(2)}) collective-permute-start(bf16[2,256,1408]{2,1,0:T(8,128)(2,1)} %get-tuple-element.167), channel_id=1, source_target_pairs={{0,4},{4,0},{1,5},{5,1},{2,6},{6,2},{3,7},{7,3}} | collective-permute-start | bytes 4325384 | tf_op jit(solution)/shard_map/ppermute | solution.py:437
  332.8 277.2 %collective-permute-start.25 = (bf16[4,256,1408]{2,1,0:T(8,128)(2,1)}, bf16[4,256,1408]{2,1,0:T(8,128)(2,1)}, u32[]{:S(2)}, u32[]{:S(2)}) collective-permute-start(bf16[4,256,1408]{2,1,0:T(8,128)(2,1)} %get-tuple-element.157), channel_id=1, source_target_pairs={{0,4},{4,0},{1,5},{5,1},{2,6},{6,2},{3,7},{7,3}} | collective-permute-start | bytes 8650760 | tf_op jit(solution)/shard_map/ppermute | solution.py:437
  363.7 154.5 %collective-permute-start.14 = (bf16[2,256,1408]{2,1,0:T(8,128)(2,1)}, bf16[2,256,1408]{2,1,0:T(8,128)(2,1)}, u32[]{:S(2)}, u32[]{:S(2)}) collective-permute-start(bf16[2,256,1408]{2,1,0:T(8,128)(2,1)} %get-tuple-element.164), channel_id=1, source_target_pairs={{0,4},{4,0},{1,5},{5,1},{2,6},{6,2},{3,7},{7,3}} | collective-permute-start | bytes 4325384 | tf_op jit(solution)/shard_map/ppermute | solution.py:437
  394.6 217.8 %collective-permute-start.26 = (bf16[4,256,1408]{2,1,0:T(8,128)(2,1)}, bf16[4,256,1408]{2,1,0:T(8,128)(2,1)}, u32[]{:S(2)}, u32[]{:S(2)}) collective-permute-start(bf16[4,256,1408]{2,1,0:T(8,128)(2,1)} %get-tuple-element.155), channel_id=1, source_target_pairs={{0,4},{4,0},{1,5},{5,1},{2,6},{6,2},{3,7},{7,3}} | collective-permute-start | bytes 8650760 | tf_op jit(solution)/shard_map/ppermute | solution.py:437
  425.5 184.2 %collective-permute-start.15 = (bf16[2,1408,256]{2,1,0:T(8,128)(2,1)}, bf16[2,1408,256]{2,1,0:T(8,128)(2,1)}, u32[]{:S(2)}, u32[]{:S(2)}) collective-permute-start(bf16[2,1408,256]{2,1,0:T(8,128)(2,1)} %get-tuple-element.161), channel_id=1, source_target_pairs={{0,4},{4,0},{1,5},{5,1},{2,6},{6,2},{3,7},{7,3}} | collective-permute-start | bytes 4325384 | tf_op jit(solution)/shard_map/ppermute | solution.py:437
  518.2 219.0 %collective-permute-start.5 = (bf16[2048,8,128]{2,1,0:T(8,128)(2,1)}, bf16[2048,8,128]{2,1,0:T(8,128)(2,1)}, u32[]{:S(2)}, u32[]{:S(2)}) collective-permute-start(bf16[2048,8,128]{2,1,0:T(8,128)(2,1)} %bitcast.6.refs_0_), channel_id=1, source_target_pairs={{0,2},{1,3},{2,0},{3,1},{4,6},{5,7},{6,4},{7,5}} | collective-permute-start | bytes 12582920 | tf_op jit(solution)/shard_map/ppermute | solution.py:437
  519.6 218.0 %collective-permute-start.2 = (bf16[2048,8,128]{2,1,0:T(8,128)(2,1)}, bf16[2048,8,128]{2,1,0:T(8,128)(2,1)}, u32[]{:S(2)}, u32[]{:S(2)}) collective-permute-start(bf16[2048,8,128]{2,1,0:T(8,128)(2,1)} %collective-permute-done.refs_0_), channel_id=1, source_target_pairs={{0,2},{1,3},{2,0},{3,1},{4,6},{5,7},{6,4},{7,5}} | collective-permute-start | bytes 12582920 | tf_op jit(solution)/shard_map/ppermute | solution.py:437
  609.9 127.2 %collective-permute-start.22 = (bf16[4,256,1408]{2,1,0:T(8,128)(2,1)}, bf16[4,256,1408]{2,1,0:T(8,128)(2,1)}, u32[]{:S(2)}, u32[]{:S(2)}) collective-permute-start(bf16[4,256,1408]{2,1,0:T(8,128)(2,1)} %get-tuple-element.158), channel_id=1, source_target_pairs={{0,4},{4,0},{1,5},{5,1},{2,6},{6,2},{3,7},{7,3}} | collective-permute-start | bytes 8650760 | tf_op jit(solution)/shard_map/ppermute | solution.py:437
  612.4 184.5 %collective-permute-start.23 = (bf16[4,256,1408]{2,1,0:T(8,128)(2,1)}, bf16[4,256,1408]{2,1,0:T(8,128)(2,1)}, u32[]{:S(2)}, u32[]{:S(2)}) collective-permute-start(bf16[4,256,1408]{2,1,0:T(8,128)(2,1)} %get-tuple-element.156), channel_id=1, source_target_pairs={{0,4},{4,0},{1,5},{5,1},{2,6},{6,2},{3,7},{7,3}} | collective-permute-start | bytes 8650760 | tf_op jit(solution)/shard_map/ppermute | solution.py:437
  675.3 184.6 %collective-permute-start.4 = (bf16[2048,8,128]{2,1,0:T(8,128)(2,1)}, bf16[2048,8,128]{2,1,0:T(8,128)(2,1)}, u32[]{:S(2)}, u32[]{:S(2)}) collective-permute-start(bf16[2048,8,128]{2,1,0:T(8,128)(2,1)} %bitcast.6.refs_0_), channel_id=1, source_target_pairs={{0,1},{1,0},{2,3},{3,2},{4,5},{5,4},{6,7},{7,6}} | collective-permute-start | bytes 12582920 | tf_op jit(solution)/shard_map/ppermute | solution.py:437
  737.1 124.8 %collective-permute-start.1 = (bf16[2048,8,128]{2,1,0:T(8,128)(2,1)}, bf16[2048,8,128]{2,1,0:T(8,128)(2,1)}, u32[]{:S(2)}, u32[]{:S(2)}) collective-permute-start(bf16[2048,8,128]{2,1,0:T(8,128)(2,1)} %collective-permute-done.refs_0_), channel_id=1, source_target_pairs={{0,1},{1,0},{2,3},{3,2},{4,5},{5,4},{6,7},{7,6}} | collective-permute-start | bytes 12582920 | tf_op jit(solution)/shard_map/ppermute | solution.py:437
  737.1 124.5 %collective-permute-start.6 = (bf16[2048,8,128]{2,1,0:T(8,128)(2,1)}, bf16[2048,8,128]{2,1,0:T(8,128)(2,1)}, u32[]{:S(2)}, u32[]{:S(2)}) collective-permute-start(bf16[2048,8,128]{2,1,0:T(8,128)(2,1)} %collective-permute-done.5.refs_2_), channel_id=1, source_target_pairs={{0,1},{1,0},{2,3},{3,2},{4,5},{5,4},{6,7},{7,6}} | collective-permute-start | bytes 12582920 | tf_op jit(solution)/shard_map/ppermute | solution.py:437
  737.6 126.0 %collective-permute-start.3 = (bf16[2048,8,128]{2,1,0:T(8,128)(2,1)}, bf16[2048,8,128]{2,1,0:T(8,128)(2,1)}, u32[]{:S(2)}, u32[]{:S(2)}) collective-permute-start(bf16[2048,8,128]{2,1,0:T(8,128)(2,1)} %collective-permute-done.2.refs_2_), channel_id=1, source_target_pairs={{0,1},{1,0},{2,3},{3,2},{4,5},{5,4},{6,7},{7,6}} | collective-permute-start | bytes 12582920 | tf_op jit(solution)/shard_map/ppermute | solution.py:437
  859.6 544.9 %collective-permute-start.11 = (bf16[1,256,1408]{2,1,0:T(8,128)(2,1)}, bf16[1,256,1408]{2,1,0:T(8,128)(2,1)}, u32[]{:S(2)}, u32[]{:S(2)}) collective-permute-start(bf16[1,256,1408]{2,1,0:T(8,128)(2,1)} %get-tuple-element.170), channel_id=1, source_target_pairs={{0,4},{4,0},{1,5},{5,1},{2,6},{6,2},{3,7},{7,3}} | collective-permute-start | bytes 2162696 | tf_op jit(solution)/shard_map/ppermute | solution.py:437
  859.9 544.6 %collective-permute-start.12 = (bf16[1,1408,256]{2,1,0:T(8,128)(2,1)}, bf16[1,1408,256]{2,1,0:T(8,128)(2,1)}, u32[]{:S(2)}, u32[]{:S(2)}) collective-permute-start(bf16[1,1408,256]{2,1,0:T(8,128)(2,1)} %get-tuple-element.168), channel_id=1, source_target_pairs={{0,4},{4,0},{1,5},{5,1},{2,6},{6,2},{3,7},{7,3}} | collective-permute-start | bytes 2162696 | tf_op jit(solution)/shard_map/ppermute | solution.py:437
  861.6 568.8 %collective-permute-start.7 = (bf16[1,256,1408]{2,1,0:T(8,128)(2,1)}, bf16[1,256,1408]{2,1,0:T(8,128)(2,1)}, u32[]{:S(2)}, u32[]{:S(2)}) collective-permute-start(bf16[1,256,1408]{2,1,0:T(8,128)(2,1)} %get-tuple-element.173), channel_id=1, source_target_pairs={{0,4},{4,0},{1,5},{5,1},{2,6},{6,2},{3,7},{7,3}} | collective-permute-start | bytes 2162696 | tf_op jit(solution)/shard_map/ppermute | solution.py:437
  861.9 568.6 %collective-permute-start.8 = (bf16[1,256,1408]{2,1,0:T(8,128)(2,1)}, bf16[1,256,1408]{2,1,0:T(8,128)(2,1)}, u32[]{:S(2)}, u32[]{:S(2)}) collective-permute-start(bf16[1,256,1408]{2,1,0:T(8,128)(2,1)} %get-tuple-element.171), channel_id=1, source_target_pairs={{0,4},{4,0},{1,5},{5,1},{2,6},{6,2},{3,7},{7,3}} | collective-permute-start | bytes 2162696 | tf_op jit(solution)/shard_map/ppermute | solution.py:437
  863.7 566.8 %collective-permute-start.9 = (bf16[1,1408,256]{2,1,0:T(8,128)(2,1)}, bf16[1,1408,256]{2,1,0:T(8,128)(2,1)}, u32[]{:S(2)}, u32[]{:S(2)}) collective-permute-start(bf16[1,1408,256]{2,1,0:T(8,128)(2,1)} %get-tuple-element.169), channel_id=1, source_target_pairs={{0,4},{4,0},{1,5},{5,1},{2,6},{6,2},{3,7},{7,3}} | collective-permute-start | bytes 2162696 | tf_op jit(solution)/shard_map/ppermute | solution.py:437
  1603.9 127.3 %collective-permute-start.54 = (bf16[4,4,144,512]{3,2,1,0:T(8,128)(2,1)}, bf16[4,4,144,512]{3,2,1,0:T(8,128)(2,1)}, u32[]{:S(2)}, u32[]{:S(2)}) collective-permute-start(bf16[4,4,144,512]{3,2,1,0:T(8,128)(2,1)} %get-tuple-element.123), channel_id=1, source_target_pairs={{0,3},{1,2},{2,1},{3,0},{4,7},{5,6},{6,5},{7,4}} | collective-permute-start | bytes 7077896 | tf_op jit(solution)/shard_map/ppermute | solution.py:437
  1630.1 150.7 %collective-permute-start.50 = (bf16[4,4,144,512]{3,2,1,0:T(8,128)(2,1)}, bf16[4,4,144,512]{3,2,1,0:T(8,128)(2,1)}, u32[]{:S(2)}, u32[]{:S(2)}) collective-permute-start(bf16[4,4,144,512]{3,2,1,0:T(8,128)(2,1)} %get-tuple-element.118), channel_id=1, source_target_pairs={{0,2},{1,3},{2,0},{3,1},{4,6},{5,7},{6,4},{7,5}} | collective-permute-start | bytes 7077896 | tf_op jit(solution)/shard_map/ppermute | solution.py:437
  1630.5 201.8 %collective-permute-start.51 = (bf16[4,4,144,512]{3,2,1,0:T(8,128)(2,1)}, bf16[4,4,144,512]{3,2,1,0:T(8,128)(2,1)}, u32[]{:S(2)}, u32[]{:S(2)}) collective-permute-start(bf16[4,4,144,512]{3,2,1,0:T(8,128)(2,1)} %get-tuple-element.119), channel_id=1, source_target_pairs={{0,3},{1,2},{2,1},{3,0},{4,7},{5,6},{6,5},{7,4}} | collective-permute-start | bytes 7077896 | tf_op jit(solution)/shard_map/ppermute | solution.py:437
  1679.7 186.2 %collective-permute-start.35 = (bf16[2,4,144,512]{3,2,1,0:T(8,128)(2,1)}, bf16[2,4,144,512]{3,2,1,0:T(8,128)(2,1)}, u32[]{:S(2)}, u32[]{:S(2)}) collective-permute-start(bf16[2,4,144,512]{3,2,1,0:T(8,128)(2,1)} %get-tuple-element.102), channel_id=1, source_target_pairs={{0,2},{1,3},{2,0},{3,1},{4,6},{5,7},{6,4},{7,5}} | collective-permute-start | bytes 3538952 | tf_op jit(solution)/shard_map/ppermute | solution.py:437
  1731.2 151.7 %collective-permute-start.36 = (bf16[2,4,144,512]{3,2,1,0:T(8,128)(2,1)}, bf16[2,4,144,512]{3,2,1,0:T(8,128)(2,1)}, u32[]{:S(2)}, u32[]{:S(2)}) collective-permute-start(bf16[2,4,144,512]{3,2,1,0:T(8,128)(2,1)} %get-tuple-element.103), channel_id=1, source_target_pairs={{0,3},{1,2},{2,1},{3,0},{4,7},{5,6},{6,5},{7,4}} | collective-permute-start | bytes 3538952 | tf_op jit(solution)/shard_map/ppermute | solution.py:437
  1731.2 151.7 %collective-permute-start.31 = (bf16[2,4,144,512]{3,2,1,0:T(8,128)(2,1)}, bf16[2,4,144,512]{3,2,1,0:T(8,128)(2,1)}, u32[]{:S(2)}, u32[]{:S(2)}) collective-permute-start(bf16[2,4,144,512]{3,2,1,0:T(8,128)(2,1)} %get-tuple-element.97), channel_id=1, source_target_pairs={{0,1},{1,0},{2,3},{3,2},{4,5},{5,4},{6,7},{7,6}} | collective-permute-start | bytes 3538952 | tf_op jit(solution)/shard_map/ppermute | solution.py:437
  1780.9 126.4 %collective-permute-start.32 = (bf16[2,4,144,512]{3,2,1,0:T(8,128)(2,1)}, bf16[2,4,144,512]{3,2,1,0:T(8,128)(2,1)}, u32[]{:S(2)}, u32[]{:S(2)}) collective-permute-start(bf16[2,4,144,512]{3,2,1,0:T(8,128)(2,1)} %get-tuple-element.98), channel_id=1, source_target_pairs={{0,2},{1,3},{2,0},{3,1},{4,6},{5,7},{6,4},{7,5}} | collective-permute-start | bytes 3538952 | tf_op jit(solution)/shard_map/ppermute | solution.py:437
  (37 other events, 2854.5 us)
Sparse Core Ops, SparseCore 0:
  80.2 25.0 all-gather.6
  107.5 23.4 all-gather.8

commit v2 on v1

--- a/solution.py
+++ b/solution.py
@@ -11,7 +11,7 @@
 CAP_FACTOR = 3
 CHUNKS = 4
 GROUPS = (4, 4, 2, 2, 2, 1, 1)
-STAGES = ((0, 1), (2, 3, 4, 5, 6))
+STAGES = ((0, 1, 2), (3, 4, 5, 6))
 PAD = 8
 LANES = 128
 N_OWN = 4
@@ -82,9 +82,10 @@
             out.append(pltpu.make_async_copy(dy_v.at[slot], dy_hbm.at[e, j, at], dy_sem.at[slot]))
         return out
 
+    is_x = lax.broadcasted_iota(jnp.int32, (SUB, LANES), 0) < SUB // 2
+    from_g = buf_g if with_dy else buf_x
+
     def one_expert(e, done):
-        n = tok_ref[0, 0, e * stride + capacity + 1]
-
         def one_chunk(j, done):
             slot = lax.rem(done, 2)
 
@@ -94,14 +95,17 @@
                     copy.wait()
 
             def rows(r8, carry):
-                at0 = j * chunk + r8 * 8
-                toks = [jnp.where(at0 + u < n, tok_ref[0, 0, e * stride + at0 + u], 0) for u in range(8)]
-                gates = [jnp.where(at0 + u < n, gate_ref[0, 0, e * stride + at0 + u], 0.0) for u in range(8)]
+                at0 = e * stride + j * chunk + r8 * 8
+                toks = [tok_ref[0, 0, at0 + u] for u in range(8)]
+                gates = [gate_ref[0, 0, at0 + u] for u in range(8)]
                 loaded = [rows_v[t].astype(jnp.float32) for t in toks]
                 for u in range(8):
                     at = pl.ds(pl.multiple_of((r8 * 8 + u) * SUB, SUB), SUB)
-                    buf_x[at, :] = loaded[u]
-                    buf_g[at, :] = loaded[u] * gates[u]
+                    if with_dy:
+                        buf_x[at, :] = loaded[u]
+                        buf_g[at, :] = loaded[u] * gates[u]
+                    else:
+                        buf_x[at, :] = loaded[u] * jnp.where(is_x, 1.0, gates[u])
                 return carry
 
             lax.fori_loop(0, chunk // 8, rows, 0)
@@ -110,7 +114,7 @@
                 lanes = slice(c * LANES, (c + 1) * LANES)
                 g_lanes = slice((half + c) * LANES, (half + c + 1) * LANES)
                 xg_v[slot, :, lanes] = buf_x[pl.ds(c, chunk, stride=SUB), :].astype(jnp.bfloat16)
-                xg_v[slot, :, g_lanes] = buf_g[pl.ds(half + c, chunk, stride=SUB), :].astype(jnp.bfloat16)
+                xg_v[slot, :, g_lanes] = from_g[pl.ds(half + c, chunk, stride=SUB), :].astype(jnp.bfloat16)
                 if with_dy:
                     dy_v[slot, :, lanes] = buf_x[pl.ds(half + c, chunk, stride=SUB), :].astype(jnp.bfloat16)
             for copy in copies(e, j, slot):
@@ -169,29 +173,28 @@
 NN, NT, TN = ((1,), (0,)), ((1,), (1,)), ((0,), (0,))
 
 
-def expert_kernel(e0, step_rows, nt_ref, mine_ref, xg_ref, dy_ref, w1o, w1p, w3o, w3p, w2o, w2p, *refs):
+def expert_kernel(step_rows, nt_ref, steps_ref, meta_ref, xg_ref, dy_ref, w1o, w1p, w3o, w3p, w2o, w2p, *refs):
     *dx_refs, dr_ref = refs[len(refs) - 10 - 1 - N_OWN:-10]
     dw1_ref, dw3_ref, dw2_ref, h1, h3, da, hid, dh1, dh3, dw2t = refs[-10:]
-    e = pl.program_id(0)
-    t = pl.program_id(1)
-    region, j = t // CHUNKS, t % CHUNKS
+    step = pl.program_id(0)
+    code = steps_ref[meta_ref[1] + step]
+    e, j = code // CHUNKS, code % CHUNKS
     half = w1o.shape[1]
     d_model = 2 * half
-    mine = pl.multiple_of(mine_ref[0] * half, half)
-    other = pl.multiple_of(half - mine_ref[0] * half, half)
-
-    @pl.when(t == 0)
+    mine = pl.multiple_of(meta_ref[0] * half, half)
+    other = pl.multiple_of(half - meta_ref[0] * half, half)
+
+    @pl.when((step < meta_ref[2]) & (j == 0))
     def _():
         dw1_ref[...] = jnp.zeros_like(dw1_ref)
         dw3_ref[...] = jnp.zeros_like(dw3_ref)
         dw2t[...] = jnp.zeros_like(dw2t)
 
-    @pl.when(j < nt_ref[(e0 + e) * 2 + region])
-    def _():
-        xo = xg_ref[0, 0, 0, :, pl.ds(mine, half)]
-        xp = xg_ref[0, 0, 0, :, pl.ds(other, half)]
-        go = xg_ref[0, 0, 0, :, pl.ds(d_model + mine, half)]
-        gp = xg_ref[0, 0, 0, :, pl.ds(d_model + other, half)]
+    def tile(region):
+        xo = xg_ref[0, region, 0, :, pl.ds(mine, half)]
+        xp = xg_ref[0, region, 0, :, pl.ds(other, half)]
+        go = xg_ref[0, region, 0, :, pl.ds(d_model + mine, half)]
+        gp = xg_ref[0, region, 0, :, pl.ds(d_model + other, half)]
         h1[...] = dot(xo, w1o[0], NN) + dot(xp, w1p[0], NN)
         h3[...] = dot(xo, w3o[0], NN) + dot(xp, w3p[0], NN)
         da[...] = dot(go, w2o[0], NT) + dot(gp, w2p[0], NT)
@@ -210,43 +213,62 @@
         dw3_ref[0] += dot(xo, dh3[...], TN)
         dw2t[...] += dot(go, hid[...], TN)
 
-    @pl.when((region == 0) & (j < nt_ref[(e0 + e) * 2]))
-    def _():
-        dyo = dy_ref[0, 0, :, pl.ds(mine, half)].astype(jnp.float32)
-        dyp = dy_ref[0, 0, :, pl.ds(other, half)].astype(jnp.float32)
-        prod = dyo * dot(hid[...], w2o[0], NN) + dyp * dot(hid[...], w2p[0], NN)
-        dr = jnp.sum(prod, axis=1, keepdims=True)
-        dr_ref[0, 0] = jnp.broadcast_to(dr, (dr.shape[0], LANES)).T[:1]
-        dxo = (dot(dh1[...], w1o[0], NT) + dot(dh3[...], w3o[0], NT)).astype(jnp.bfloat16)
-        dxp = (dot(dh1[...], w1p[0], NT) + dot(dh3[...], w3p[0], NT)).astype(jnp.bfloat16)
-        chunk = dx_refs[0].shape[2]
-        for k, dx_ref in enumerate(dx_refs):
-            dx_ref[0, 0, :, pl.ds(mine, half)] = dxo[k * chunk:(k + 1) * chunk]
-            dx_ref[0, 0, :, pl.ds(other, half)] = dxp[k * chunk:(k + 1) * chunk]
-
-    @pl.when(t == pl.num_programs(1) - 1)
+        @pl.when(region == 0)
+        def _():
+            dyo = dy_ref[0, 0, :, pl.ds(mine, half)].astype(jnp.float32)
+            dyp = dy_ref[0, 0, :, pl.ds(other, half)].astype(jnp.float32)
+            prod = dyo * dot(hid[...], w2o[0], NN) + dyp * dot(hid[...], w2p[0], NN)
+            dr = jnp.sum(prod, axis=1, keepdims=True)
+            dr_ref[0, 0] = jnp.broadcast_to(dr, (dr.shape[0], LANES)).T[:1]
+            dxo = (dot(dh1[...], w1o[0], NT) + dot(dh3[...], w3o[0], NT)).astype(jnp.bfloat16)
+            dxp = (dot(dh1[...], w1p[0], NT) + dot(dh3[...], w3p[0], NT)).astype(jnp.bfloat16)
+            chunk = dx_refs[0].shape[2]
+            for k, dx_ref in enumerate(dx_refs):
+                dx_ref[0, 0, :, pl.ds(mine, half)] = dxo[k * chunk:(k + 1) * chunk]
+                dx_ref[0, 0, :, pl.ds(other, half)] = dxp[k * chunk:(k + 1) * chunk]
+
+    def one_region(region, carry):
+        @pl.when((step < meta_ref[2]) & (j < nt_ref[e * 2 + region]))
+        def _():
+            tile(region)
+
+        return carry
+
+    lax.fori_loop(0, 2, one_region, 0)
+
+    @pl.when((step < meta_ref[2]) & (j == jnp.maximum(nt_ref[e * 2], nt_ref[e * 2 + 1]) - 1))
     def _():
         dw2_ref[0] = dw2t[...].T
 
 
-def expert_group(e0, count, xg, dy, nt, mine, own, peer, carried):
+def expert_group(e0, count, xg, dy, nt, steps, meta, own, peer, carried):
     exp_local, _, _, tile_rows, width = xg.shape
     half, d_ff = own[0].shape[1:]
     step_rows = 16
     chunk = tile_rows // N_OWN
 
-    def own_tile(e, t, nt_ref, _):
-        return (e0 + e, jnp.minimum(jnp.where(t < CHUNKS, t, CHUNKS - 1), nt_ref[(e0 + e) * 2] - 1), 0, 0)
-
-    def own_rows(e, t, nt_ref, _):
-        return (e, jnp.minimum(jnp.where(t < CHUNKS, t, CHUNKS - 1), nt_ref[(e0 + e) * 2] - 1), 0, 0)
-
-    def xg_tile(e, t, nt_ref, _):
-        region = t // CHUNKS
-        return (e0 + e, region, jnp.minimum(t % CHUNKS, nt_ref[(e0 + e) * 2 + region] - 1), 0, 0)
-
-    at_own = lambda e, t, *_: (e0 + e, 0, 0)
-    at_peer = lambda e, t, *_: (e, 0, 0)
+    def place(s, steps_ref, meta_ref):
+        code = steps_ref[meta_ref[1] + jnp.minimum(s, meta_ref[2] - 1)]
+        return code // CHUNKS, code % CHUNKS
+
+    def own_tile(s, nt_ref, steps_ref, meta_ref):
+        e, j = place(s, steps_ref, meta_ref)
+        return (e, jnp.minimum(j, nt_ref[e * 2] - 1), 0, 0)
+
+    def own_rows(s, nt_ref, steps_ref, meta_ref):
+        e, j = place(s, steps_ref, meta_ref)
+        return (e - e0, jnp.minimum(j, nt_ref[e * 2] - 1), 0, 0)
+
+    def xg_tile(s, nt_ref, steps_ref, meta_ref):
+        e, j = place(s, steps_ref, meta_ref)
+        return (e, 0, j, 0, 0)
+
+    def at_own(s, nt_ref, steps_ref, meta_ref):
+        return (place(s, steps_ref, meta_ref)[0], 0, 0)
+
+    def at_peer(s, nt_ref, steps_ref, meta_ref):
+        return (place(s, steps_ref, meta_ref)[0] - e0, 0, 0)
+
     up = lambda at: pl.BlockSpec((1, half, d_ff), at)
     down = lambda at: pl.BlockSpec((1, d_ff, half), at)
     out_shape = [
@@ -256,15 +278,15 @@
         jax.ShapeDtypeStruct((exp_local, half, d_ff), jnp.float32),
         jax.ShapeDtypeStruct((exp_local, d_ff, half), jnp.float32),
     ]
-    n_in = 2 + 8
+    n_in = 3 + 8
     carried = list(carried)
     return pl.pallas_call(
-        functools.partial(expert_kernel, e0, step_rows),
+        functools.partial(expert_kernel, step_rows),
         grid_spec=pltpu.PrefetchScalarGridSpec(
-            num_scalar_prefetch=2,
-            grid=(count, 2 * CHUNKS),
+            num_scalar_prefetch=3,
+            grid=(count * CHUNKS,),
             in_specs=[
-                pl.BlockSpec((1, 1, 1, tile_rows, width), xg_tile),
+                pl.BlockSpec((1, 2, 1, tile_rows, width), xg_tile),
                 pl.BlockSpec((1, 1, tile_rows, width // 2), own_tile),
                 up(at_own), up(at_peer), up(at_own), up(at_peer), down(at_own), down(at_peer),
             ] + [pl.BlockSpec(memory_space=pl.ANY)] * len(carried),
@@ -285,9 +307,9 @@
         out_shape=out_shape,
         input_output_aliases={n_in + k: N_OWN + k for k in range(len(carried))},
         compiler_params=pltpu.CompilerParams(
-            dimension_semantics=("arbitrary", "arbitrary"), vmem_limit_bytes=VMEM_BYTES),
+            dimension_semantics=("arbitrary",), vmem_limit_bytes=VMEM_BYTES),
         interpret=INTERPRET,
-    )(nt.reshape(-1), mine, xg, dy, own[0], peer[0], own[1], peer[1], own[2], peer[2], *carried)
+    )(nt.reshape(-1), steps, meta, xg, dy, own[0], peer[0], own[1], peer[1], own[2], peer[2], *carried)
 
 
 def combine_kernel(stage, counts, e0, exp_local, capacity, chunk, tok_ref, dr_ref, *refs):
@@ -299,7 +321,7 @@
     if not first:
         acc_in, refs = refs[0], refs[1:]
     if last:
-        gx_out, dr_out, acc, tmp, rows_v, sem, acc_sem = refs
+        place_ref, gx_out, rg_out, acc, tmp, rows_v, sem, acc_sem = refs
     else:
         acc_out, acc, tmp, rows_v, sem, acc_sem = refs
     src = pl.program_id(0)
@@ -363,7 +385,7 @@
 
             def rows(r8, c):
                 r0 = r8 * 8
-                toks = [jnp.where(j * chunk + r0 + u < n, tok_ref[slots + r0 + u], tok_dev) for u in range(8)]
+                toks = [tok_ref[slots + r0 + u] for u in range(8)]
                 ats = [pl.ds(pl.multiple_of(t * SUB, SUB), SUB) for t in toks]
                 sums = [acc[ats[u], :] + jnp.where(
                     here, dr_ref[drs + r0 + u], tmp[pl.ds(pl.multiple_of((r0 + u) * SUB, SUB), SUB), :])
@@ -384,14 +406,18 @@
         if last:
             for c in range(SUB // 2):
                 gx_out[:, c * LANES:(c + 1) * LANES] = acc[pl.ds(c, tok_dev, stride=SUB), :].astype(jnp.bfloat16)
-            dr_out[...] = acc[pl.ds(SUB // 2, tok_dev, stride=SUB), :]
+            by_expert = acc[pl.ds(SUB // 2, tok_dev, stride=SUB), :].T[:N_OWN * exp_local]
+            lane_of = lax.broadcasted_iota(jnp.int32, by_expert.shape, 0)
+            for k in range(place_ref.shape[0]):
+                mine = jnp.where(lane_of == place_ref[k:k + 1, :], by_expert, 0.0)
+                rg_out[k:k + 1, :] = jnp.sum(mine, axis=0, keepdims=True)
         else:
             store = pltpu.make_async_copy(acc, acc_out, acc_sem)
             store.start()
             store.wait()
 
 
-def combine(stage, slot_home, dr, rows, carried, exp_local, capacity, tok_dev):
+def combine(stage, slot_home, dr, rows, carried, place, exp_local, capacity, tok_dev):
     counts = [GROUPS[g] for g in STAGES[stage]]
     e0 = sum(GROUPS[:STAGES[stage][0]])
     n_exp = sum(counts)
@@ -400,16 +426,18 @@
     hbm = pl.BlockSpec(memory_space=pl.ANY)
     acc_shape = ((tok_dev + 1) * SUB, LANES)
     if stage == len(STAGES) - 1:
-        out_specs = [pl.BlockSpec((tok_dev, d_model), lambda s: (0, 0)), pl.BlockSpec((tok_dev, LANES), lambda s: (0, 0))]
+        out_specs = [pl.BlockSpec((tok_dev, d_model), lambda s: (0, 0)), pl.BlockSpec(place.shape, lambda s: (0, 0))]
         out_shape = [jax.ShapeDtypeStruct((tok_dev, d_model), jnp.bfloat16),
-                     jax.ShapeDtypeStruct((tok_dev, LANES), jnp.float32)]
+                     jax.ShapeDtypeStruct(place.shape, jnp.float32)]
+        extra, extra_specs = [place], [pl.BlockSpec(place.shape, lambda s: (0, 0))]
     else:
+        extra, extra_specs = [], []
         out_specs = [hbm]
         out_shape = [jax.ShapeDtypeStruct(acc_shape, jnp.float32)]
     return pl.pallas_call(
         functools.partial(combine_kernel, stage, counts, e0, exp_local, capacity, chunk),
         grid=(N_OWN,),
-        in_specs=[smem, smem] + [hbm] * (len(rows) + len(carried)),
+        in_specs=[smem, smem] + [hbm] * (len(rows) + len(carried)) + extra_specs,
         out_specs=out_specs,
         out_shape=out_shape,
         scratch_shapes=[
@@ -422,7 +450,7 @@
         compiler_params=pltpu.CompilerParams(
             dimension_semantics=("arbitrary",), vmem_limit_bytes=VMEM_BYTES),
         interpret=INTERPRET,
-    )(slot_home, dr, *rows, *carried)
+    )(slot_home, dr, *rows, *carried, *extra)
 
 
 def solution(mesh):
@@ -469,22 +497,44 @@
             order = [(my_fsdp ^ a) * n_ep + (my_ep ^ b) for a in range(n_fsdp) for b in range(n_ep)]
             return jnp.stack([lax.dynamic_index_in_dim(v, k, axis=0, keepdims=True) for k in order])
 
-        slot_tok, slot_gate = for_me(slot_tok), for_me(slot_gate)
-        cnt = slot_tok.reshape(n_fsdp, n_ep, exp_local, capacity + PAD)[..., capacity + 1]
+        stride = capacity + PAD
+        word = jnp.arange(stride, dtype=jnp.int32)
+
+        def filled(tok, empty):
+            tok = tok.reshape(-1, exp_local, stride)
+            held = word < tok[..., capacity + 1:capacity + 2]
+            return jnp.where(held | (word == capacity + 1), tok, empty), held
+
+        slot_tok, held = filled(for_me(slot_tok), 0)
+        slot_gate = jnp.where(held, for_me(slot_gate).reshape(held.shape), 0.0)
+        slot_home = filled(slot_home, tok_dev)[0].reshape(-1)
+        cnt = slot_tok[..., capacity + 1].reshape(n_fsdp, n_ep, exp_local)
+        slot_tok = slot_tok.reshape(n_fsdp * n_ep, 1, -1)
+        slot_gate = slot_gate.reshape(n_fsdp * n_ep, 1, -1)
         most = jnp.max(cnt, axis=1)
         nt = jnp.maximum((most + chunk - 1) // chunk, 1).T
+        per_expert = jnp.max(nt, axis=1)
+        active = (jnp.arange(CHUNKS, dtype=jnp.int32) < per_expert[:, None]).reshape(-1)
+        code = jnp.arange(active.shape[0], dtype=jnp.int32)
+        before = jnp.sum(jnp.where((code[None, :] < code[:, None]) & active[None, :], 1, 0), axis=1)
+        steps = jnp.sum(jnp.where((before[None, :] == code[:, None]) & active[None, :], code[None, :], 0), axis=1)
+        first = [sum(GROUPS[:g]) for g in range(len(GROUPS))]
+        n_steps = [jnp.sum(per_expert[first[g]:first[g] + GROUPS[g]]) for g in range(len(GROUPS))]
+        starts = [jnp.sum(per_expert[:first[g]]) for g in range(len(GROUPS))]
 
         xg, dy = gather_rows(all_tokens[:n_ep], slot_tok[:n_ep], slot_gate[:n_ep], nt, 0, capacity)
         xg, = gather_rows(all_tokens[n_ep:], slot_tok[n_ep:], slot_gate[n_ep:], nt, 1, capacity, (xg,))
 
         own = (w_gate, w_up, w_down)
-        mine = my_fsdp.astype(jnp.int32).reshape(1)
+        mine = my_fsdp.astype(jnp.int32)
+        place = (((expert_ids // exp_local) ^ my_ep) * exp_local + expert_ids % exp_local).T
         carried, sums = (), ()
         e0 = 0
         rows = []
         for g, count in enumerate(GROUPS):
             peer = [swap(w[e0:e0 + count], "fsdp", 1) for w in own]
-            out = expert_group(e0, count, xg, dy, nt, mine, own, peer, carried)
+            meta = jnp.stack([mine, starts[g], n_steps[g]])
+            out = expert_group(e0, count, xg, dy, nt, steps, meta, own, peer, carried)
             dx_g, carried = out[:n_ep], out[n_ep:]
             rows += [dx_g[0]] + [swap(dx_g[b], "ep", b) for b in range(1, n_ep)]
             e0 += count
@@ -494,13 +544,10 @@
                     dr = dr.transpose(2, 0, 1, 3).reshape(n_ep, -1)
                     dr = jnp.concatenate(
                         [dr[0]] + [swap(dr[b], "ep", b) for b in range(1, n_ep)])
-                    sums = combine(stage, slot_home, dr, rows, sums, exp_local, capacity, tok_dev)
+                    sums = combine(stage, slot_home, dr, rows, sums, place, exp_local, capacity, tok_dev)
                     rows = []
         _, grad_w_gate, grad_w_up, grad_w_down = carried
-        grad_x, dr_tok = sums
-        place = ((expert_ids // exp_local) ^ my_ep) * exp_local + expert_ids % exp_local
-        hit = place[:, :, None] == jnp.arange(LANES, dtype=jnp.int32)
-        route_grad = jnp.sum(jnp.where(hit, dr_tok[:, None, :], 0.0), axis=2)
+        grad_x, route_grad = sums[0], sums[1].T
         return grad_x, route_grad, grad_w_gate, grad_w_up, grad_w_down
 
     return jax.shard_map(

time: 1980 us -> 1860 us (0.939)
  waiting for transfers between devices: 1060 us -> 975 us
  Pallas kernels: 717 us -> 663 us
    ppermute x55, waiting for transfers between devices: 1060 us -> 975 us  [swap(): return lax.ppermute(value, axis, [(k, k ^ mask) for k in range(size)])]
    pallas_call x7, Pallas kernels: 455 us -> 420 us  [expert_group(): pl.pallas_call(functools.partial(expert_kernel, step_rows), grid_spec=plt...]
  transfers between devices with their start and end apart: 57 -> 57, of which waited for: 27 -> 26; matrix products, arithmetic and copies ran while one was open for 4% -> 5% of each run, Pallas kernels for 30% -> 33%
where the time goes in v2:
time: 1860 us; the launch traced here: 1850 us
  waiting for transfers between devices  975 us (52%)
  Pallas kernels  663 us (36%)
  starting transfers between devices  105 us (6%)
  local copies, waits for them, and re-layouts  58 us (3%)
  other arithmetic  35.9 us (2%)
    ppermute x55, waiting for transfers between devices, swap(): return lax.ppermute(value, axis, [(k, k ^ mask) for k in range(size)])  975 us
    pallas_call x7, Pallas kernels, expert_group(): pl.pallas_call(functools.partial(expert_kernel, step_rows), grid_spec=plt...  420 us
    pallas_call x2, Pallas kernels, gather_rows(): pl.pallas_call(functools.partial(gather_kernel, n_src, with_dy, region, e...  124 us
    ppermute x55, starting transfers between devices, swap(): return lax.ppermute(value, axis, [(k, k ^ mask) for k in range(size)])  105 us
    pallas_call x1, Pallas kernels, route_slots(): pl.pallas_call(functools.partial(route_kernel, n_pairs, top_k, experts, c...  66 us
    pallas_call x2, Pallas kernels, combine(): pl.pallas_call(functools.partial(combine_kernel, stage, counts, e0, exp_l...  53.2 us
  transfers between devices with their start and end apart: 57, of which 26 were waited for; matrix products, arithmetic and copies ran while one was open for 5% of the time, Pallas kernels for 33%

profile of v2, /device:TPU:0, one launch (start us, length us, event | category | flops | bytes accessed | tf_op | source)
XLA Modules:
  0.0 1852.0 jit_solution(6593246554120313631)
XLA Ops:
  31.2 185.3 %collective-permute-done.10.w1p = bf16[1,256,1408]{2,1,0:T(8,128)(2,1)S(1)} collective-permute-done((bf16[1,256,1408]{2,1,0:T(8,128)(2,1)S(1)}, bf16[1,256,1408]{2,1,0:T(8,128)(2,1)S(1)}, u32[]{:S(2)}, u32[]{:S(2)}) %collective-permute-start.10) | collective-permute-done | bytes 720928 | tf_op jit(solution)/shard_map/ppermute | solution.py:465
  223.6 27.5 %collective-permute-done.16.w1p = bf16[2,256,1408]{2,1,0:T(8,128)(2,1)S(1)} collective-permute-done((bf16[2,256,1408]{2,1,0:T(8,128)(2,1)}, bf16[2,256,1408]{2,1,0:T(8,128)(2,1)S(1)}, u32[]{:S(2)}, u32[]{:S(2)}) %collective-permute-start.16) | collective-permute-done | bytes 1441824 | tf_op jit(solution)/shard_map/ppermute | solution.py:465
  252.9 29.2 %collective-permute-done.17.w3p = bf16[2,256,1408]{2,1,0:T(8,128)(2,1)S(1)} collective-permute-done((bf16[2,256,1408]{2,1,0:T(8,128)(2,1)}, bf16[2,256,1408]{2,1,0:T(8,128)(2,1)S(1)}, u32[]{:S(2)}, u32[]{:S(2)}) %collective-permute-start.17) | collective-permute-done | bytes 1441824 | tf_op jit(solution)/shard_map/ppermute | solution.py:465
  286.9 26.2 %collective-permute-done.18.w2p = bf16[2,1408,256]{2,1,0:T(8,128)(2,1)} collective-permute-done((bf16[2,1408,256]{2,1,0:T(8,128)(2,1)}, bf16[2,1408,256]{2,1,0:T(8,128)(2,1)}, u32[]{:S(2)}, u32[]{:S(2)}) %collective-permute-start.18) | collective-permute-done | bytes 1441824 | tf_op jit(solution)/shard_map/ppermute | solution.py:465
  314.8 29.2 %collective-permute-done.13.w1p = bf16[2,256,1408]{2,1,0:T(8,128)(2,1)} collective-permute-done((bf16[2,256,1408]{2,1,0:T(8,128)(2,1)}, bf16[2,256,1408]{2,1,0:T(8,128)(2,1)}, u32[]{:S(2)}, u32[]{:S(2)}) %collective-permute-start.13) | collective-permute-done | bytes 1441824 | tf_op jit(solution)/shard_map/ppermute | solution.py:465
  345.7 90.8 %collective-permute-done.14.w3p = bf16[2,256,1408]{2,1,0:T(8,128)(2,1)S(1)} collective-permute-done((bf16[2,256,1408]{2,1,0:T(8,128)(2,1)}, bf16[2,256,1408]{2,1,0:T(8,128)(2,1)S(1)}, u32[]{:S(2)}, u32[]{:S(2)}) %collective-permute-start.14) | collective-permute-done | bytes 1441824 | tf_op jit(solution)/shard_map/ppermute | solution.py:465
  442.7 66.0 %route.1 = (s32[37376]{0:T(1024)}, f32[37376]{0:T(1024)}) custom-call(s32[12288]{0:T(1024)} %reshape.150.ids_ref, f32[12288]{0:T(1024)} %reshape.151.gate_ref), custom_call_target="tpu_custom_call" | custom-call | tf_op jit(solution)/shard_map/route/pallas_call | solution.py:52
  516.7 16.2 collective-permute-done.15.w2p
  548.7 54.7 %collective-permute-done.27.w2p = bf16[4,1408,256]{2,1,0:T(8,128)(2,1)} collective-permute-done((bf16[4,1408,256]{2,1,0:T(8,128)(2,1)}, bf16[4,1408,256]{2,1,0:T(8,128)(2,1)}, u32[]{:S(2)}, u32[]{:S(2)}) %collective-permute-start.27) | collective-permute-done | bytes 2883616 | tf_op jit(solution)/shard_map/ppermute | solution.py:465
  603.4 61.8 %collective-permute-done.22.w1p = bf16[4,256,1408]{2,1,0:T(8,128)(2,1)} collective-permute-done((bf16[4,256,1408]{2,1,0:T(8,128)(2,1)}, bf16[4,256,1408]{2,1,0:T(8,128)(2,1)}, u32[]{:S(2)}, u32[]{:S(2)}) %collective-permute-start.22) | collective-permute-done | bytes 2883616 | tf_op jit(solution)/shard_map/ppermute | solution.py:465
  669.1 54.8 %collective-permute-done.23.w3p = bf16[4,256,1408]{2,1,0:T(8,128)(2,1)} collective-permute-done((bf16[4,256,1408]{2,1,0:T(8,128)(2,1)}, bf16[4,256,1408]{2,1,0:T(8,128)(2,1)}, u32[]{:S(2)}, u32[]{:S(2)}) %collective-permute-start.23) | collective-permute-done | bytes 2883616 | tf_op jit(solution)/shard_map/ppermute | solution.py:465
  740.9 45.7 %collective-permute-done.24.w2p = bf16[4,1408,256]{2,1,0:T(8,128)(2,1)} collective-permute-done((bf16[4,1408,256]{2,1,0:T(8,128)(2,1)}, bf16[4,1408,256]{2,1,0:T(8,128)(2,1)}, u32[]{:S(2)}, u32[]{:S(2)}) %collective-permute-start.24) | collective-permute-done | bytes 2883616 | tf_op jit(solution)/shard_map/ppermute | solution.py:465
  803.4 63.3 %shard_map.110 = (bf16[16,2,4,576,1024]{4,3,2,1,0:T(8,128)(2,1)}, bf16[16,4,576,512]{3,2,1,0:T(8,128)(2,1)}) custom-call(s32[32]{0:T(128)} %reshape.154.nt_ref, s32[4,1,9344]{2,1,0:T(1,128)} %slice.181.tok_ref, f32[4,1,9344]{2,1,0:T(1,128)} %slice.183.gate_ref, bf16[2048,8,128]{2,1,0:T(8,128)(2,1)} %bitcast.19.refs_0_, ...), custom_call_target="tpu_custom_call" | custom-call | tf_op jit(solution)/shard_map/pallas_call | solution.py:145
  866.7 60.5 %shard_map.111.xg_ref = bf16[16,2,4,576,1024]{4,3,2,1,0:T(8,128)(2,1)} custom-call(s32[32]{0:T(128)} %reshape.154.nt_ref, s32[4,1,9344]{2,1,0:T(1,128)} %slice.177.tok_ref, f32[4,1,9344]{2,1,0:T(1,128)} %slice.179.gate_ref, bf16[2048,8,128]{2,1,0:T(8,128)(2,1)} %collective-permute-done.refs_0_, ...), custom_call_target="tpu_custom_call", output_to_operand_aliasing={{}: (7, {})} | custom-call | tf_op jit(solution)/shard_map/pallas_call | solution.py:145
  927.2 85.9 %shard_map.112 = (bf16[4,4,144,512]{3,2,1,0:T(8,128)(2,1)}, bf16[4,4,144,512]{3,2,1,0:T(8,128)(2,1)}, bf16[4,4,144,512]{3,2,1,0:T(8,128)(2,1)}, bf16[4,4,144,512...) custom-call(s32[32]{0:T(128)} %reshape.154.nt_ref, ...), custom_call_target="tpu_custom_call" | custom-call | tf_op jit(solution)/shard_map/pallas_call | solution.py:283
  1013.1 143.5 %shard_map.113 = (bf16[4,4,144,512]{3,2,1,0:T(8,128)(2,1)}, bf16[4,4,144,512]{3,2,1,0:T(8,128)(2,1)}, bf16[4,4,144,512]{3,2,1,0:T(8,128)(2,1)}, bf16[4,4,144,512...) custom-call(s32[32]{0:T(128)} %reshape.154.nt_ref, ...), custom_call_target="tpu_custom_call", output_to_operand_aliasing={{4}: (11, {}), {5}: (12, {}), {6}: (13, {}), {7}: (14, {})} | custom-call | tf_op jit(solution)/shard_map/pallas_call | solution.py:283
  1156.6 46.1 %shard_map.114 = (bf16[2,4,144,512]{3,2,1,0:T(8,128)(2,1)}, bf16[2,4,144,512]{3,2,1,0:T(8,128)(2,1)}, bf16[2,4,144,512]{3,2,1,0:T(8,128)(2,1)}, bf16[2,4,144,512...) custom-call(s32[32]{0:T(128)} %reshape.154.nt_ref, ...), custom_call_target="tpu_custom_call", output_to_operand_aliasing={{4}: (11, {}), {5}: (12, {}), {6}: (13, {}), {7}: (14, {})} | custom-call | tf_op jit(solution)/shard_map/pallas_call | solution.py:283
  1204.5 46.1 %shard_map.115 = (bf16[2,4,144,512]{3,2,1,0:T(8,128)(2,1)}, bf16[2,4,144,512]{3,2,1,0:T(8,128)(2,1)}, bf16[2,4,144,512]{3,2,1,0:T(8,128)(2,1)}, bf16[2,4,144,512...) custom-call(s32[32]{0:T(128)} %reshape.154.nt_ref, ...), custom_call_target="tpu_custom_call", output_to_operand_aliasing={{4}: (11, {}), {5}: (12, {}), {6}: (13, {}), {7}: (14, {})} | custom-call | tf_op jit(solution)/shard_map/pallas_call | solution.py:283
  1250.6 46.3 %shard_map.116 = (bf16[2,4,144,512]{3,2,1,0:T(8,128)(2,1)}, bf16[2,4,144,512]{3,2,1,0:T(8,128)(2,1)}, bf16[2,4,144,512]{3,2,1,0:T(8,128)(2,1)}, bf16[2,4,144,512...) custom-call(s32[32]{0:T(128)} %reshape.154.nt_ref, ...), custom_call_target="tpu_custom_call", output_to_operand_aliasing={{4}: (11, {}), {5}: (12, {}), {6}: (13, {}), {7}: (14, {})} | custom-call | tf_op jit(solution)/shard_map/pallas_call | solution.py:283
  1297.0 25.9 %shard_map.117 = (bf16[1,4,144,512]{3,2,1,0:T(8,128)(2,1)}, bf16[1,4,144,512]{3,2,1,0:T(8,128)(2,1)}, bf16[1,4,144,512]{3,2,1,0:T(8,128)(2,1)}, bf16[1,4,144,512...) custom-call(s32[32]{0:T(128)} %reshape.154.nt_ref, ...), custom_call_target="tpu_custom_call", output_to_operand_aliasing={{4}: (11, {}), {5}: (12, {}), {6}: (13, {}), {7}: (14, {})} | custom-call | tf_op jit(solution)/shard_map/pallas_call | solution.py:283
  1323.0 26.0 %shard_map.118 = (bf16[1,4,144,512]{3,2,1,0:T(8,128)(2,1)}, bf16[1,4,144,512]{3,2,1,0:T(8,128)(2,1)}, bf16[1,4,144,512]{3,2,1,0:T(8,128)(2,1)}, bf16[1,4,144,512...) custom-call(s32[32]{0:T(128)} %reshape.154.nt_ref, ...), custom_call_target="tpu_custom_call", output_to_operand_aliasing={{4}: (11, {}), {5}: (12, {}), {6}: (13, {}), {7}: (14, {})} | custom-call | tf_op jit(solution)/shard_map/pallas_call | solution.py:283
  1348.9 57.2 %collective-permute-start.40 = (bf16[1,4,144,512]{3,2,1,0:T(8,128)(2,1)}, bf16[1,4,144,512]{3,2,1,0:T(8,128)(2,1)S(1)}, u32[]{:S(2)}, u32[]{:S(2)}) collective-permute-start(bf16[1,4,144,512]{3,2,1,0:T(8,128)(2,1)} %get-tuple-element.109), channel_id=1, source_target_pairs={{0,1},{1,0},{2,3},{3,2},{4,5},{5,4},{6,7},{7,6}} | collective-permute-start | bytes 1769480 | tf_op jit(solution)/shard_map/ppermute | solution.py:465
  1473.1 20.6 %collective-permute-done.53.refs_10_ = bf16[2,4,144,512]{3,2,1,0:T(8,128)(2,1)S(1)} collective-permute-done((bf16[2,4,144,512]{3,2,1,0:T(8,128)(2,1)}, bf16[2,4,144,512]{3,2,1,0:T(8,128)(2,1)S(1)}, u32[]{:S(2)}, u32[]{:S(2)}) %collective-permute-start.53) | collective-permute-done | bytes 1179680 | tf_op jit(solution)/shard_map/ppermute | solution.py:465
  1495.0 25.9 %collective-permute-done.54.refs_11_ = bf16[2,4,144,512]{3,2,1,0:T(8,128)(2,1)} collective-permute-done((bf16[2,4,144,512]{3,2,1,0:T(8,128)(2,1)}, bf16[2,4,144,512]{3,2,1,0:T(8,128)(2,1)}, u32[]{:S(2)}, u32[]{:S(2)}) %collective-permute-start.54) | collective-permute-done | bytes 1179680 | tf_op jit(solution)/shard_map/ppermute | solution.py:465
  1525.6 43.9 %collective-permute-done.50.refs_6_ = bf16[4,4,144,512]{3,2,1,0:T(8,128)(2,1)} collective-permute-done((bf16[4,4,144,512]{3,2,1,0:T(8,128)(2,1)}, bf16[4,4,144,512]{3,2,1,0:T(8,128)(2,1)}, u32[]{:S(2)}, u32[]{:S(2)}) %collective-permute-start.50) | collective-permute-done | bytes 2359328 | tf_op jit(solution)/shard_map/ppermute | solution.py:465
  1572.0 50.0 %collective-permute-done.51.refs_7_ = bf16[4,4,144,512]{3,2,1,0:T(8,128)(2,1)} collective-permute-done((bf16[4,4,144,512]{3,2,1,0:T(8,128)(2,1)}, bf16[4,4,144,512]{3,2,1,0:T(8,128)(2,1)}, u32[]{:S(2)}, u32[]{:S(2)}) %collective-permute-start.51) | collective-permute-done | bytes 2359328 | tf_op jit(solution)/shard_map/ppermute | solution.py:465
  1622.0 48.6 %collective-permute-done.47.refs_2_ = bf16[4,4,144,512]{3,2,1,0:T(8,128)(2,1)} collective-permute-done((bf16[4,4,144,512]{3,2,1,0:T(8,128)(2,1)}, bf16[4,4,144,512]{3,2,1,0:T(8,128)(2,1)}, u32[]{:S(2)}, u32[]{:S(2)}) %collective-permute-start.47) | collective-permute-done | bytes 2359328 | tf_op jit(solution)/shard_map/ppermute | solution.py:465
  1673.1 50.0 %collective-permute-done.48.refs_3_ = bf16[4,4,144,512]{3,2,1,0:T(8,128)(2,1)} collective-permute-done((bf16[4,4,144,512]{3,2,1,0:T(8,128)(2,1)}, bf16[4,4,144,512]{3,2,1,0:T(8,128)(2,1)}, u32[]{:S(2)}, u32[]{:S(2)}) %collective-permute-start.48) | collective-permute-done | bytes 2359328 | tf_op jit(solution)/shard_map/ppermute | solution.py:465
  1729.8 31.2 %shard_map.119.refs_16_ = f32[16392,128]{1,0:T(8,128)} custom-call(s32[37376]{0:T(1024)} %broadcast_select_fusion.tok_ref, f32[23040]{0:T(1024)} %pad_maximum_fusion.dr_ref, bf16[4,4,144,512]{3,2,1,0:T(8,128)(2,1)} %get-tuple-element.112.refs_0_, bf16[4,4,144,512]{3,2,1,0:T(8,128)(2,1)} %collective-permute-done.46.refs_1_, ...), custom_call_target="tpu_custom_call" | custom-call | tf_op jit(solution)/shard_map/pallas_call | solution.py:437
  1773.7 23.4 %collective-permute-done.32.refs_2_ = bf16[2,4,144,512]{3,2,1,0:T(8,128)(2,1)} collective-permute-done((bf16[2,4,144,512]{3,2,1,0:T(8,128)(2,1)}, bf16[2,4,144,512]{3,2,1,0:T(8,128)(2,1)}, u32[]{:S(2)}, u32[]{:S(2)}) %collective-permute-start.32) | collective-permute-done | bytes 1179680 | tf_op jit(solution)/shard_map/ppermute | solution.py:465
  1797.0 25.9 %collective-permute-done.33.refs_3_ = bf16[2,4,144,512]{3,2,1,0:T(8,128)(2,1)} collective-permute-done((bf16[2,4,144,512]{3,2,1,0:T(8,128)(2,1)}, bf16[2,4,144,512]{3,2,1,0:T(8,128)(2,1)}, u32[]{:S(2)}, u32[]{:S(2)}) %collective-permute-start.33) | collective-permute-done | bytes 1179680 | tf_op jit(solution)/shard_map/ppermute | solution.py:465
  1822.9 22.0 %shard_map.120 = (bf16[2048,512]{1,0:T(8,128)(2,1)}, f32[6,2048]{1,0:T(8,128)}) custom-call(s32[37376]{0:T(1024)} %broadcast_select_fusion.tok_ref, f32[13824]{0:T(1024)} %pad_maximum_fusion.1.dr_ref, bf16[2,4,144,512]{3,2,1,0:T(8,128)(2,1)} %get-tuple-element.96.refs_0_, bf16[2,4,144,512]{3,2,1,0:T(8,128)(2,1)} %collective-permute-done.31.refs_1_, ...), custom_call_target="tpu_custom_call" | custom-call | tf_op jit(solution)/shard_map/pallas_call | solution.py:437
  (262 shorter events, 207.3 us)
Async XLA Ops:
  7.2 535.0 %all-gather.7.cloned.1.call-start = ((), (), s32[]{:S(2)}) async-start(), calls=%async_computation | async-start | bytes 1345536 | tf_op jit(solution)/shard_map/all_gather | solution.py:491
  14.2 424.0 %collective-permute-start = (bf16[2048,8,128]{2,1,0:T(8,128)(2,1)}, bf16[2048,8,128]{2,1,0:T(8,128)(2,1)}, u32[]{:S(2)}, u32[]{:S(2)}) collective-permute-start(bf16[2048,8,128]{2,1,0:T(8,128)(2,1)} %bitcast.19.refs_0_), channel_id=1, source_target_pairs={{0,4},{4,0},{1,5},{5,1},{2,6},{6,2},{3,7},{7,3}} | collective-permute-start | bytes 12582920 | tf_op jit(solution)/shard_map/ppermute | solution.py:465
  19.5 198.7 %collective-permute-start.19 = (bf16[2,256,1408]{2,1,0:T(8,128)(2,1)S(1)}, bf16[2,256,1408]{2,1,0:T(8,128)(2,1)}, u32[]{:S(2)}, u32[]{:S(2)}) collective-permute-start(bf16[2,256,1408]{2,1,0:T(8,128)(2,1)S(1)} %get-tuple-element.172), channel_id=1, source_target_pairs={{0,4},{4,0},{1,5},{5,1},{2,6},{6,2},{3,7},{7,3}} | collective-permute-start | bytes 4325384 | tf_op jit(solution)/shard_map/ppermute | solution.py:465
  21.4 197.1 %collective-permute-start.20 = (bf16[2,256,1408]{2,1,0:T(8,128)(2,1)S(1)}, bf16[2,256,1408]{2,1,0:T(8,128)(2,1)}, u32[]{:S(2)}, u32[]{:S(2)}) collective-permute-start(bf16[2,256,1408]{2,1,0:T(8,128)(2,1)S(1)} %get-tuple-element.169), channel_id=1, source_target_pairs={{0,4},{4,0},{1,5},{5,1},{2,6},{6,2},{3,7},{7,3}} | collective-permute-start | bytes 4325384 | tf_op jit(solution)/shard_map/ppermute | solution.py:465
  28.2 192.0 %collective-permute-start.21 = (bf16[2,1408,256]{2,1,0:T(8,128)(2,1)S(1)}, bf16[2,1408,256]{2,1,0:T(8,128)(2,1)}, u32[]{:S(2)}, u32[]{:S(2)}) collective-permute-start(bf16[2,1408,256]{2,1,0:T(8,128)(2,1)S(1)} %get-tuple-element.166), channel_id=1, source_target_pairs={{0,4},{4,0},{1,5},{5,1},{2,6},{6,2},{3,7},{7,3}} | collective-permute-start | bytes 4325384 | tf_op jit(solution)/shard_map/ppermute | solution.py:465
  29.2 187.3 %collective-permute-start.10 = (bf16[1,256,1408]{2,1,0:T(8,128)(2,1)S(1)}, bf16[1,256,1408]{2,1,0:T(8,128)(2,1)S(1)}, u32[]{:S(2)}, u32[]{:S(2)}) collective-permute-start(bf16[1,256,1408]{2,1,0:T(8,128)(2,1)S(1)} %get-tuple-element.179), channel_id=1, source_target_pairs={{0,4},{4,0},{1,5},{5,1},{2,6},{6,2},{3,7},{7,3}} | collective-permute-start | bytes 2162696 | tf_op jit(solution)/shard_map/ppermute | solution.py:465
  220.2 123.7 %collective-permute-start.13 = (bf16[2,256,1408]{2,1,0:T(8,128)(2,1)}, bf16[2,256,1408]{2,1,0:T(8,128)(2,1)}, u32[]{:S(2)}, u32[]{:S(2)}) collective-permute-start(bf16[2,256,1408]{2,1,0:T(8,128)(2,1)} %get-tuple-element.174), channel_id=1, source_target_pairs={{0,4},{4,0},{1,5},{5,1},{2,6},{6,2},{3,7},{7,3}} | collective-permute-start | bytes 4325384 | tf_op jit(solution)/shard_map/ppermute | solution.py:465
  251.1 283.0 %collective-permute-start.25 = (bf16[4,256,1408]{2,1,0:T(8,128)(2,1)}, bf16[4,256,1408]{2,1,0:T(8,128)(2,1)}, u32[]{:S(2)}, u32[]{:S(2)}) collective-permute-start(bf16[4,256,1408]{2,1,0:T(8,128)(2,1)} %get-tuple-element.164), channel_id=1, source_target_pairs={{0,4},{4,0},{1,5},{5,1},{2,6},{6,2},{3,7},{7,3}} | collective-permute-start | bytes 8650760 | tf_op jit(solution)/shard_map/ppermute | solution.py:465
  282.0 154.5 %collective-permute-start.14 = (bf16[2,256,1408]{2,1,0:T(8,128)(2,1)}, bf16[2,256,1408]{2,1,0:T(8,128)(2,1)S(1)}, u32[]{:S(2)}, u32[]{:S(2)}) collective-permute-start(bf16[2,256,1408]{2,1,0:T(8,128)(2,1)} %get-tuple-element.171), channel_id=1, source_target_pairs={{0,4},{4,0},{1,5},{5,1},{2,6},{6,2},{3,7},{7,3}} | collective-permute-start | bytes 4325384 | tf_op jit(solution)/shard_map/ppermute | solution.py:465
  313.0 222.7 %collective-permute-start.26 = (bf16[4,256,1408]{2,1,0:T(8,128)(2,1)}, bf16[4,256,1408]{2,1,0:T(8,128)(2,1)}, u32[]{:S(2)}, u32[]{:S(2)}) collective-permute-start(bf16[4,256,1408]{2,1,0:T(8,128)(2,1)} %get-tuple-element.162), channel_id=1, source_target_pairs={{0,4},{4,0},{1,5},{5,1},{2,6},{6,2},{3,7},{7,3}} | collective-permute-start | bytes 8650760 | tf_op jit(solution)/shard_map/ppermute | solution.py:465
  343.9 189.0 %collective-permute-start.15 = (bf16[2,1408,256]{2,1,0:T(8,128)(2,1)}, bf16[2,1408,256]{2,1,0:T(8,128)(2,1)S(1)}, u32[]{:S(2)}, u32[]{:S(2)}) collective-permute-start(bf16[2,1408,256]{2,1,0:T(8,128)(2,1)} %get-tuple-element.168), channel_id=1, source_target_pairs={{0,4},{4,0},{1,5},{5,1},{2,6},{6,2},{3,7},{7,3}} | collective-permute-start | bytes 4325384 | tf_op jit(solution)/shard_map/ppermute | solution.py:465
  436.5 228.7 %collective-permute-start.5 = (bf16[2048,8,128]{2,1,0:T(8,128)(2,1)}, bf16[2048,8,128]{2,1,0:T(8,128)(2,1)}, u32[]{:S(2)}, u32[]{:S(2)}) collective-permute-start(bf16[2048,8,128]{2,1,0:T(8,128)(2,1)} %bitcast.19.refs_0_), channel_id=1, source_target_pairs={{0,2},{1,3},{2,0},{3,1},{4,6},{5,7},{6,4},{7,5}} | collective-permute-start | bytes 12582920 | tf_op jit(solution)/shard_map/ppermute | solution.py:465
  438.2 227.5 %collective-permute-start.2 = (bf16[2048,8,128]{2,1,0:T(8,128)(2,1)}, bf16[2048,8,128]{2,1,0:T(8,128)(2,1)}, u32[]{:S(2)}, u32[]{:S(2)}) collective-permute-start(bf16[2048,8,128]{2,1,0:T(8,128)(2,1)} %collective-permute-done.refs_0_), channel_id=1, source_target_pairs={{0,2},{1,3},{2,0},{3,1},{4,6},{5,7},{6,4},{7,5}} | collective-permute-start | bytes 12582920 | tf_op jit(solution)/shard_map/ppermute | solution.py:465
  510.4 216.7 %all-gather.9.cloned.1.call-start = ((), (), s32[]{:S(2)}) async-start(), calls=%async_computation.1 | async-start | bytes 1345536 | tf_op jit(solution)/shard_map/all_gather | solution.py:492
  534.1 131.0 %collective-permute-start.22 = (bf16[4,256,1408]{2,1,0:T(8,128)(2,1)}, bf16[4,256,1408]{2,1,0:T(8,128)(2,1)}, u32[]{:S(2)}, u32[]{:S(2)}) collective-permute-start(bf16[4,256,1408]{2,1,0:T(8,128)(2,1)} %get-tuple-element.165), channel_id=1, source_target_pairs={{0,4},{4,0},{1,5},{5,1},{2,6},{6,2},{3,7},{7,3}} | collective-permute-start | bytes 8650760 | tf_op jit(solution)/shard_map/ppermute | solution.py:465
  535.7 188.2 %collective-permute-start.23 = (bf16[4,256,1408]{2,1,0:T(8,128)(2,1)}, bf16[4,256,1408]{2,1,0:T(8,128)(2,1)}, u32[]{:S(2)}, u32[]{:S(2)}) collective-permute-start(bf16[4,256,1408]{2,1,0:T(8,128)(2,1)} %get-tuple-element.163), channel_id=1, source_target_pairs={{0,4},{4,0},{1,5},{5,1},{2,6},{6,2},{3,7},{7,3}} | collective-permute-start | bytes 8650760 | tf_op jit(solution)/shard_map/ppermute | solution.py:465
  603.4 184.5 %collective-permute-start.4 = (bf16[2048,8,128]{2,1,0:T(8,128)(2,1)}, bf16[2048,8,128]{2,1,0:T(8,128)(2,1)}, u32[]{:S(2)}, u32[]{:S(2)}) collective-permute-start(bf16[2048,8,128]{2,1,0:T(8,128)(2,1)} %bitcast.19.refs_0_), channel_id=1, source_target_pairs={{0,1},{1,0},{2,3},{3,2},{4,5},{5,4},{6,7},{7,6}} | collective-permute-start | bytes 12582920 | tf_op jit(solution)/shard_map/ppermute | solution.py:465
  665.2 124.7 %collective-permute-start.1 = (bf16[2048,8,128]{2,1,0:T(8,128)(2,1)}, bf16[2048,8,128]{2,1,0:T(8,128)(2,1)}, u32[]{:S(2)}, u32[]{:S(2)}) collective-permute-start(bf16[2048,8,128]{2,1,0:T(8,128)(2,1)} %collective-permute-done.refs_0_), channel_id=1, source_target_pairs={{0,1},{1,0},{2,3},{3,2},{4,5},{5,4},{6,7},{7,6}} | collective-permute-start | bytes 12582920 | tf_op jit(solution)/shard_map/ppermute | solution.py:465
  665.2 123.4 %collective-permute-start.6 = (bf16[2048,8,128]{2,1,0:T(8,128)(2,1)}, bf16[2048,8,128]{2,1,0:T(8,128)(2,1)}, u32[]{:S(2)}, u32[]{:S(2)}) collective-permute-start(bf16[2048,8,128]{2,1,0:T(8,128)(2,1)} %collective-permute-done.5.refs_2_), channel_id=1, source_target_pairs={{0,1},{1,0},{2,3},{3,2},{4,5},{5,4},{6,7},{7,6}} | collective-permute-start | bytes 12582920 | tf_op jit(solution)/shard_map/ppermute | solution.py:465
  665.7 125.0 %collective-permute-start.3 = (bf16[2048,8,128]{2,1,0:T(8,128)(2,1)}, bf16[2048,8,128]{2,1,0:T(8,128)(2,1)}, u32[]{:S(2)}, u32[]{:S(2)}) collective-permute-start(bf16[2048,8,128]{2,1,0:T(8,128)(2,1)} %collective-permute-done.2.refs_2_), channel_id=1, source_target_pairs={{0,1},{1,0},{2,3},{3,2},{4,5},{5,4},{6,7},{7,6}} | collective-permute-start | bytes 12582920 | tf_op jit(solution)/shard_map/ppermute | solution.py:465
  786.6 510.4 %collective-permute-start.11 = (bf16[1,256,1408]{2,1,0:T(8,128)(2,1)}, bf16[1,256,1408]{2,1,0:T(8,128)(2,1)}, u32[]{:S(2)}, u32[]{:S(2)}) collective-permute-start(bf16[1,256,1408]{2,1,0:T(8,128)(2,1)} %get-tuple-element.177), channel_id=1, source_target_pairs={{0,4},{4,0},{1,5},{5,1},{2,6},{6,2},{3,7},{7,3}} | collective-permute-start | bytes 2162696 | tf_op jit(solution)/shard_map/ppermute | solution.py:465
  787.8 509.2 %collective-permute-start.12 = (bf16[1,1408,256]{2,1,0:T(8,128)(2,1)}, bf16[1,1408,256]{2,1,0:T(8,128)(2,1)}, u32[]{:S(2)}, u32[]{:S(2)}) collective-permute-start(bf16[1,1408,256]{2,1,0:T(8,128)(2,1)} %get-tuple-element.175), channel_id=1, source_target_pairs={{0,4},{4,0},{1,5},{5,1},{2,6},{6,2},{3,7},{7,3}} | collective-permute-start | bytes 2162696 | tf_op jit(solution)/shard_map/ppermute | solution.py:465
  788.6 534.3 %collective-permute-start.7 = (bf16[1,256,1408]{2,1,0:T(8,128)(2,1)}, bf16[1,256,1408]{2,1,0:T(8,128)(2,1)}, u32[]{:S(2)}, u32[]{:S(2)}) collective-permute-start(bf16[1,256,1408]{2,1,0:T(8,128)(2,1)} %get-tuple-element.180), channel_id=1, source_target_pairs={{0,4},{4,0},{1,5},{5,1},{2,6},{6,2},{3,7},{7,3}} | collective-permute-start | bytes 2162696 | tf_op jit(solution)/shard_map/ppermute | solution.py:465
  789.8 533.1 %collective-permute-start.8 = (bf16[1,256,1408]{2,1,0:T(8,128)(2,1)}, bf16[1,256,1408]{2,1,0:T(8,128)(2,1)}, u32[]{:S(2)}, u32[]{:S(2)}) collective-permute-start(bf16[1,256,1408]{2,1,0:T(8,128)(2,1)} %get-tuple-element.178), channel_id=1, source_target_pairs={{0,4},{4,0},{1,5},{5,1},{2,6},{6,2},{3,7},{7,3}} | collective-permute-start | bytes 2162696 | tf_op jit(solution)/shard_map/ppermute | solution.py:465
  790.6 532.3 %collective-permute-start.9 = (bf16[1,1408,256]{2,1,0:T(8,128)(2,1)}, bf16[1,1408,256]{2,1,0:T(8,128)(2,1)}, u32[]{:S(2)}, u32[]{:S(2)}) collective-permute-start(bf16[1,1408,256]{2,1,0:T(8,128)(2,1)} %get-tuple-element.176), channel_id=1, source_target_pairs={{0,4},{4,0},{1,5},{5,1},{2,6},{6,2},{3,7},{7,3}} | collective-permute-start | bytes 2162696 | tf_op jit(solution)/shard_map/ppermute | solution.py:465
  1493.7 128.3 %collective-permute-start.51 = (bf16[4,4,144,512]{3,2,1,0:T(8,128)(2,1)}, bf16[4,4,144,512]{3,2,1,0:T(8,128)(2,1)}, u32[]{:S(2)}, u32[]{:S(2)}) collective-permute-start(bf16[4,4,144,512]{3,2,1,0:T(8,128)(2,1)} %get-tuple-element.119), channel_id=1, source_target_pairs={{0,3},{1,2},{2,1},{3,0},{4,7},{5,6},{6,5},{7,4}} | collective-permute-start | bytes 7077896 | tf_op jit(solution)/shard_map/ppermute | solution.py:465
  1520.9 149.8 %collective-permute-start.47 = (bf16[4,4,144,512]{3,2,1,0:T(8,128)(2,1)}, bf16[4,4,144,512]{3,2,1,0:T(8,128)(2,1)}, u32[]{:S(2)}, u32[]{:S(2)}) collective-permute-start(bf16[4,4,144,512]{3,2,1,0:T(8,128)(2,1)} %get-tuple-element.114), channel_id=1, source_target_pairs={{0,2},{1,3},{2,0},{3,1},{4,6},{5,7},{6,4},{7,5}} | collective-permute-start | bytes 7077896 | tf_op jit(solution)/shard_map/ppermute | solution.py:465
  1521.3 201.8 %collective-permute-start.48 = (bf16[4,4,144,512]{3,2,1,0:T(8,128)(2,1)}, bf16[4,4,144,512]{3,2,1,0:T(8,128)(2,1)}, u32[]{:S(2)}, u32[]{:S(2)}) collective-permute-start(bf16[4,4,144,512]{3,2,1,0:T(8,128)(2,1)} %get-tuple-element.115), channel_id=1, source_target_pairs={{0,3},{1,2},{2,1},{3,0},{4,7},{5,6},{6,5},{7,4}} | collective-permute-start | bytes 7077896 | tf_op jit(solution)/shard_map/ppermute | solution.py:465
  1569.5 191.5 %collective-permute-start.35 = (bf16[2,4,144,512]{3,2,1,0:T(8,128)(2,1)}, bf16[2,4,144,512]{3,2,1,0:T(8,128)(2,1)}, u32[]{:S(2)}, u32[]{:S(2)}) collective-permute-start(bf16[2,4,144,512]{3,2,1,0:T(8,128)(2,1)} %get-tuple-element.102), channel_id=1, source_target_pairs={{0,2},{1,3},{2,0},{3,1},{4,6},{5,7},{6,4},{7,5}} | collective-permute-start | bytes 3538952 | tf_op jit(solution)/shard_map/ppermute | solution.py:465
  1622.0 151.7 %collective-permute-start.36 = (bf16[2,4,144,512]{3,2,1,0:T(8,128)(2,1)}, bf16[2,4,144,512]{3,2,1,0:T(8,128)(2,1)}, u32[]{:S(2)}, u32[]{:S(2)}) collective-permute-start(bf16[2,4,144,512]{3,2,1,0:T(8,128)(2,1)} %get-tuple-element.103), channel_id=1, source_target_pairs={{0,3},{1,2},{2,1},{3,0},{4,7},{5,6},{6,5},{7,4}} | collective-permute-start | bytes 3538952 | tf_op jit(solution)/shard_map/ppermute | solution.py:465
  1622.0 151.7 %collective-permute-start.31 = (bf16[2,4,144,512]{3,2,1,0:T(8,128)(2,1)}, bf16[2,4,144,512]{3,2,1,0:T(8,128)(2,1)}, u32[]{:S(2)}, u32[]{:S(2)}) collective-permute-start(bf16[2,4,144,512]{3,2,1,0:T(8,128)(2,1)} %get-tuple-element.97), channel_id=1, source_target_pairs={{0,1},{1,0},{2,3},{3,2},{4,5},{5,4},{6,7},{7,6}} | collective-permute-start | bytes 3538952 | tf_op jit(solution)/shard_map/ppermute | solution.py:465
  1670.6 126.4 %collective-permute-start.32 = (bf16[2,4,144,512]{3,2,1,0:T(8,128)(2,1)}, bf16[2,4,144,512]{3,2,1,0:T(8,128)(2,1)}, u32[]{:S(2)}, u32[]{:S(2)}) collective-permute-start(bf16[2,4,144,512]{3,2,1,0:T(8,128)(2,1)} %get-tuple-element.98), channel_id=1, source_target_pairs={{0,2},{1,3},{2,0},{3,1},{4,6},{5,7},{6,4},{7,5}} | collective-permute-start | bytes 3538952 | tf_op jit(solution)/shard_map/ppermute | solution.py:465
  (50 other events, 2011.2 us)
Sparse Core Ops, SparseCore 0:
  510.5 23.8 all-gather.6
  536.8 23.4 all-gather.8

commit v3 on v2

--- a/solution.py
+++ b/solution.py
@@ -10,8 +10,8 @@
 
 CAP_FACTOR = 3
 CHUNKS = 4
-GROUPS = (4, 4, 2, 2, 2, 1, 1)
-STAGES = ((0, 1, 2), (3, 4, 5, 6))
+GROUPS = (4, 2, 2, 2, 2, 2, 1, 1)
+STAGES = ((0, 1, 2, 3), (4, 5, 6, 7))
 PAD = 8
 LANES = 128
 N_OWN = 4
@@ -178,7 +178,7 @@
     dw1_ref, dw3_ref, dw2_ref, h1, h3, da, hid, dh1, dh3, dw2t = refs[-10:]
     step = pl.program_id(0)
     code = steps_ref[meta_ref[1] + step]
-    e, j = code // CHUNKS, code % CHUNKS
+    e, j = meta_ref[3 + code // CHUNKS], code % CHUNKS
     half = w1o.shape[1]
     d_model = 2 * half
     mine = pl.multiple_of(meta_ref[0] * half, half)
@@ -249,22 +249,26 @@
 
     def place(s, steps_ref, meta_ref):
         code = steps_ref[meta_ref[1] + jnp.minimum(s, meta_ref[2] - 1)]
-        return code // CHUNKS, code % CHUNKS
-
-    def own_tile(s, nt_ref, steps_ref, meta_ref):
-        e, j = place(s, steps_ref, meta_ref)
+        return code // CHUNKS, meta_ref[3 + code // CHUNKS], code % CHUNKS
+
+    def dy_tile(s, nt_ref, steps_ref, meta_ref):
+        _, e, j = place(s, steps_ref, meta_ref)
         return (e, jnp.minimum(j, nt_ref[e * 2] - 1), 0, 0)
 
-    def own_rows(s, nt_ref, steps_ref, meta_ref):
-        e, j = place(s, steps_ref, meta_ref)
-        return (e - e0, jnp.minimum(j, nt_ref[e * 2] - 1), 0, 0)
+    def dr_tile(s, nt_ref, steps_ref, meta_ref):
+        k, e, j = place(s, steps_ref, meta_ref)
+        return (k, jnp.minimum(j, nt_ref[e * 2] - 1), 0, 0)
+
+    def dx_tile(s, nt_ref, steps_ref, meta_ref):
+        k, e, j = place(s, steps_ref, meta_ref)
+        return (k - e0, jnp.minimum(j, nt_ref[e * 2] - 1), 0, 0)
 
     def xg_tile(s, nt_ref, steps_ref, meta_ref):
-        e, j = place(s, steps_ref, meta_ref)
+        _, e, j = place(s, steps_ref, meta_ref)
         return (e, 0, j, 0, 0)
 
     def at_own(s, nt_ref, steps_ref, meta_ref):
-        return (place(s, steps_ref, meta_ref)[0], 0, 0)
+        return (place(s, steps_ref, meta_ref)[1], 0, 0)
 
     def at_peer(s, nt_ref, steps_ref, meta_ref):
         return (place(s, steps_ref, meta_ref)[0] - e0, 0, 0)
@@ -287,12 +291,12 @@
             grid=(count * CHUNKS,),
             in_specs=[
                 pl.BlockSpec((1, 2, 1, tile_rows, width), xg_tile),
-                pl.BlockSpec((1, 1, tile_rows, width // 2), own_tile),
+                pl.BlockSpec((1, 1, tile_rows, width // 2), dy_tile),
                 up(at_own), up(at_peer), up(at_own), up(at_peer), down(at_own), down(at_peer),
             ] + [pl.BlockSpec(memory_space=pl.ANY)] * len(carried),
             out_specs=[
-                *[pl.BlockSpec((1, 1, chunk, width // 2), own_rows)] * N_OWN,
-                pl.BlockSpec((1, 1, 1, tile_rows), own_tile),
+                *[pl.BlockSpec((1, 1, chunk, width // 2), dx_tile)] * N_OWN,
+                pl.BlockSpec((1, 1, 1, tile_rows), dr_tile),
                 up(at_own), up(at_own), down(at_own),
             ],
             scratch_shapes=[
@@ -312,7 +316,7 @@
     )(nt.reshape(-1), steps, meta, xg, dy, own[0], peer[0], own[1], peer[1], own[2], peer[2], *carried)
 
 
-def combine_kernel(stage, counts, e0, exp_local, capacity, chunk, tok_ref, dr_ref, *refs):
+def combine_kernel(stage, counts, e0, exp_local, capacity, chunk, order_ref, tok_ref, dr_ref, *refs):
     stride = capacity + PAD
     n_exp = sum(counts)
     rows_hbm = refs[:N_OWN * len(counts)]
@@ -327,8 +331,11 @@
     src = pl.program_id(0)
     tok_dev = acc.shape[0] // SUB - 1
 
+    def expert(k, e):
+        return order_ref[k * exp_local + e0 + e]
+
     def count_of(k, e):
-        return tok_ref[(k * exp_local + e0 + e) * stride + capacity + 1]
+        return tok_ref[(k * exp_local + expert(k, e)) * stride + capacity + 1]
 
     def tiles(n):
         return (n + chunk - 1) // chunk
@@ -372,7 +379,7 @@
 
     def per_expert(e, carry):
         n = count_of(src, e)
-        here = (sub == SUB // 2) & (lane == src * exp_local + e0 + e)
+        here = (sub == SUB // 2) & (lane == src * exp_local + expert(src, e))
 
         def one(j, c):
             at = e * CHUNKS + j
@@ -380,7 +387,7 @@
             for c4 in range(SUB // 2):
                 tmp[pl.ds(c4, chunk, stride=SUB), :] = rows_v[
                     buf, at, :, c4 * LANES:(c4 + 1) * LANES].astype(jnp.float32)
-            slots = (src * exp_local + e0 + e) * stride + j * chunk
+            slots = (src * exp_local + expert(src, e)) * stride + j * chunk
             drs = (src * n_exp + e) * capacity + j * chunk
 
             def rows(r8, c):
@@ -417,7 +424,7 @@
             store.wait()
 
 
-def combine(stage, slot_home, dr, rows, carried, place, exp_local, capacity, tok_dev):
+def combine(stage, order, slot_home, dr, rows, carried, place, exp_local, capacity, tok_dev):
     counts = [GROUPS[g] for g in STAGES[stage]]
     e0 = sum(GROUPS[:STAGES[stage][0]])
     n_exp = sum(counts)
@@ -437,7 +444,7 @@
     return pl.pallas_call(
         functools.partial(combine_kernel, stage, counts, e0, exp_local, capacity, chunk),
         grid=(N_OWN,),
-        in_specs=[smem, smem] + [hbm] * (len(rows) + len(carried)) + extra_specs,
+        in_specs=[smem, smem, smem] + [hbm] * (len(rows) + len(carried)) + extra_specs,
         out_specs=out_specs,
         out_shape=out_shape,
         scratch_shapes=[
@@ -450,7 +457,7 @@
         compiler_params=pltpu.CompilerParams(
             dimension_semantics=("arbitrary",), vmem_limit_bytes=VMEM_BYTES),
         interpret=INTERPRET,
-    )(slot_home, dr, *rows, *carried, *extra)
+    )(order, slot_home, dr, *rows, *carried, *extra)
 
 
 def solution(mesh):
@@ -498,6 +505,18 @@
             return jnp.stack([lax.dynamic_index_in_dim(v, k, axis=0, keepdims=True) for k in order])
 
         stride = capacity + PAD
+        totals = jnp.sum(slot_tok.reshape(-1, n_ep, exp_local, stride)[..., capacity + 1], axis=0)
+        totals = jnp.repeat(jnp.sum(totals.reshape(n_ep, -1, 2), axis=2), 2, axis=1)
+        index = jnp.arange(exp_local, dtype=jnp.int32)
+        key = jnp.where(index < GROUPS[0], 2 * n_fsdp * n_ep * capacity + 1, totals)
+        ahead = (key[:, None, :] > key[:, :, None]) | (
+            (key[:, None, :] == key[:, :, None]) & (index[None, None, :] < index[None, :, None]))
+        rank = jnp.sum(ahead.astype(jnp.int32), axis=2)
+        orders = jnp.sum(jnp.where(rank[:, None, :] == index[None, :, None], index[None, None, :], 0), axis=2)
+        order_home = jnp.stack(
+            [lax.dynamic_index_in_dim(orders, my_ep ^ b, axis=0, keepdims=False) for b in range(n_ep)])
+        order = order_home[0]
+        order_home = order_home.reshape(-1)
         word = jnp.arange(stride, dtype=jnp.int32)
 
         def filled(tok, empty):
@@ -514,6 +533,7 @@
         most = jnp.max(cnt, axis=1)
         nt = jnp.maximum((most + chunk - 1) // chunk, 1).T
         per_expert = jnp.max(nt, axis=1)
+        per_expert = jnp.sum(jnp.where(order[:, None] == index[None, :], per_expert[None, :], 0), axis=1)
         active = (jnp.arange(CHUNKS, dtype=jnp.int32) < per_expert[:, None]).reshape(-1)
         code = jnp.arange(active.shape[0], dtype=jnp.int32)
         before = jnp.sum(jnp.where((code[None, :] < code[:, None]) & active[None, :], 1, 0), axis=1)
@@ -532,8 +552,9 @@
         e0 = 0
         rows = []
         for g, count in enumerate(GROUPS):
-            peer = [swap(w[e0:e0 + count], "fsdp", 1) for w in own]
-            meta = jnp.stack([mine, starts[g], n_steps[g]])
+            part = [w[:count] if g == 0 else lax.dynamic_slice_in_dim(w, order[e0], count, axis=0) for w in own]
+            peer = [swap(w, "fsdp", 1) for w in part]
+            meta = jnp.concatenate([jnp.stack([mine, starts[g], n_steps[g]]), order])
             out = expert_group(e0, count, xg, dy, nt, steps, meta, own, peer, carried)
             dx_g, carried = out[:n_ep], out[n_ep:]
             rows += [dx_g[0]] + [swap(dx_g[b], "ep", b) for b in range(1, n_ep)]
@@ -544,7 +565,7 @@
                     dr = dr.transpose(2, 0, 1, 3).reshape(n_ep, -1)
                     dr = jnp.concatenate(
                         [dr[0]] + [swap(dr[b], "ep", b) for b in range(1, n_ep)])
-                    sums = combine(stage, slot_home, dr, rows, sums, place, exp_local, capacity, tok_dev)
+                    sums = combine(stage, order_home, slot_home, dr, rows, sums, place, exp_local, capacity, tok_dev)
                     rows = []
         _, grad_w_gate, grad_w_up, grad_w_down = carried
         grad_x, route_grad = sums[0], sums[1].T

time: 1860 us -> 1940 us (1.043)
  waiting for transfers between devices: 975 us -> 1020 us
    ppermute x55 -> x61, waiting for transfers between devices: 975 us -> 1020 us  [swap(): return lax.ppermute(value, axis, [(k, k ^ mask) for k in range(size)])]
    dynamic_slice x0 -> x7, local copies, waits for them, and re-layouts: none -> 21.7 us  [the longest x6 21.1 us: per_device(): lax.dynamic_slice_in_dim(w, order[e0], count, axis=0)]
    ppermute x55 -> x61, starting transfers between devices: 105 us -> 117 us  [swap(): return lax.ppermute(value, axis, [(k, k ^ mask) for k in range(size)])]
    pallas_call x7 -> x8, Pallas kernels: 420 us -> 428 us  [expert_group(): pl.pallas_call(functools.partial(expert_kernel, step_rows), grid_spec=plt...]
  transfers between devices with their start and end apart: 57 -> 63, of which waited for: 26 -> 32; matrix products, arithmetic and copies ran while one was open for 5% -> 5% of each run, Pallas kernels for 33% -> 29%
where the time goes in v3:
time: 1940 us
  waiting for transfers between devices  1020 us (53%)
  Pallas kernels  673 us (35%)
  starting transfers between devices  118 us (6%)
  local copies, waits for them, and re-layouts  65.6 us (3%)
  other arithmetic  32.6 us (2%)
  between operations  28.6 us (1%)
    ppermute x61, waiting for transfers between devices, swap(): return lax.ppermute(value, axis, [(k, k ^ mask) for k in range(size)])  1020 us
    pallas_call x8, Pallas kernels, expert_group(): pl.pallas_call(functools.partial(expert_kernel, step_rows), grid_spec=plt...  428 us
    pallas_call x2, Pallas kernels, gather_rows(): pl.pallas_call(functools.partial(gather_kernel, n_src, with_dy, region, e...  124 us
    ppermute x61, starting transfers between devices, swap(): return lax.ppermute(value, axis, [(k, k ^ mask) for k in range(size)])  117 us
    pallas_call x1, Pallas kernels, route_slots(): pl.pallas_call(functools.partial(route_kernel, n_pairs, top_k, experts, c...  66 us
    pallas_call x2, Pallas kernels, combine(): pl.pallas_call(functools.partial(combine_kernel, stage, counts, e0, exp_l...  54.8 us
  transfers between devices with their start and end apart: 63, of which 32 were waited for; matrix products, arithmetic and copies ran while one was open for 5% of the time, Pallas kernels for 29%

profile of v3, /device:TPU:0, one launch (start us, length us, event | category | flops | bytes accessed | tf_op | source)
XLA Modules:
  0.0 1937.9 jit_solution(10012715408575920875)
XLA Ops:
  11.4 66.0 %route.1 = (s32[37376]{0:T(1024)}, f32[37376]{0:T(1024)}) custom-call(s32[12288]{0:T(1024)} %reshape.224.ids_ref, f32[12288]{0:T(1024)} %reshape.225.gate_ref), custom_call_target="tpu_custom_call" | custom-call | tf_op jit(solution)/shard_map/route/pallas_call | solution.py:52
  140.2 243.0 %collective-permute-done.10.w1p = bf16[1,256,1408]{2,1,0:T(8,128)(2,1)S(1)} collective-permute-done((bf16[1,256,1408]{2,1,0:T(8,128)(2,1)S(1)}, bf16[1,256,1408]{2,1,0:T(8,128)(2,1)S(1)}, u32[]{:S(2)}, u32[]{:S(2)}) %collective-permute-start.10) | collective-permute-done | bytes 720928 | tf_op jit(solution)/shard_map/ppermute | solution.py:472
  389.4 28.3 %collective-permute-done.25.w1p = bf16[2,256,1408]{2,1,0:T(8,128)(2,1)} collective-permute-done((bf16[2,256,1408]{2,1,0:T(8,128)(2,1)S(1)}, bf16[2,256,1408]{2,1,0:T(8,128)(2,1)}, u32[]{:S(2)}, u32[]{:S(2)}) %collective-permute-start.25) | collective-permute-done | bytes 1441824 | tf_op jit(solution)/shard_map/ppermute | solution.py:472
  419.5 29.2 %collective-permute-done.26.w3p = bf16[2,256,1408]{2,1,0:T(8,128)(2,1)} collective-permute-done((bf16[2,256,1408]{2,1,0:T(8,128)(2,1)S(1)}, bf16[2,256,1408]{2,1,0:T(8,128)(2,1)}, u32[]{:S(2)}, u32[]{:S(2)}) %collective-permute-start.26) | collective-permute-done | bytes 1441824 | tf_op jit(solution)/shard_map/ppermute | solution.py:472
  450.4 29.2 %collective-permute-done.27.w2p = bf16[2,1408,256]{2,1,0:T(8,128)(2,1)} collective-permute-done((bf16[2,1408,256]{2,1,0:T(8,128)(2,1)S(1)}, bf16[2,1408,256]{2,1,0:T(8,128)(2,1)}, u32[]{:S(2)}, u32[]{:S(2)}) %collective-permute-start.27) | collective-permute-done | bytes 1441824 | tf_op jit(solution)/shard_map/ppermute | solution.py:472
  481.6 28.9 %collective-permute-done.22.w1p = bf16[2,256,1408]{2,1,0:T(8,128)(2,1)} collective-permute-done((bf16[2,256,1408]{2,1,0:T(8,128)(2,1)S(1)}, bf16[2,256,1408]{2,1,0:T(8,128)(2,1)}, u32[]{:S(2)}, u32[]{:S(2)}) %collective-permute-start.22) | collective-permute-done | bytes 1441824 | tf_op jit(solution)/shard_map/ppermute | solution.py:472
  512.2 29.2 %collective-permute-done.23.w3p = bf16[2,256,1408]{2,1,0:T(8,128)(2,1)} collective-permute-done((bf16[2,256,1408]{2,1,0:T(8,128)(2,1)S(1)}, bf16[2,256,1408]{2,1,0:T(8,128)(2,1)}, u32[]{:S(2)}, u32[]{:S(2)}) %collective-permute-start.23) | collective-permute-done | bytes 1441824 | tf_op jit(solution)/shard_map/ppermute | solution.py:472
  543.1 29.2 %collective-permute-done.24.w2p = bf16[2,1408,256]{2,1,0:T(8,128)(2,1)} collective-permute-done((bf16[2,1408,256]{2,1,0:T(8,128)(2,1)S(1)}, bf16[2,1408,256]{2,1,0:T(8,128)(2,1)}, u32[]{:S(2)}, u32[]{:S(2)}) %collective-permute-start.24) | collective-permute-done | bytes 1441824 | tf_op jit(solution)/shard_map/ppermute | solution.py:472
  574.8 33.1 %collective-permute-done.19.w1p = bf16[2,256,1408]{2,1,0:T(8,128)(2,1)S(1)} collective-permute-done((bf16[2,256,1408]{2,1,0:T(8,128)(2,1)}, bf16[2,256,1408]{2,1,0:T(8,128)(2,1)S(1)}, u32[]{:S(2)}, u32[]{:S(2)}) %collective-permute-start.19) | collective-permute-done | bytes 1441824 | tf_op jit(solution)/shard_map/ppermute | solution.py:472
  609.6 29.3 %collective-permute-done.20.w3p = bf16[2,256,1408]{2,1,0:T(8,128)(2,1)} collective-permute-done((bf16[2,256,1408]{2,1,0:T(8,128)(2,1)}, bf16[2,256,1408]{2,1,0:T(8,128)(2,1)}, u32[]{:S(2)}, u32[]{:S(2)}) %collective-permute-start.20) | collective-permute-done | bytes 1441824 | tf_op jit(solution)/shard_map/ppermute | solution.py:472
  640.6 29.2 %collective-permute-done.21.w2p = bf16[2,1408,256]{2,1,0:T(8,128)(2,1)} collective-permute-done((bf16[2,1408,256]{2,1,0:T(8,128)(2,1)}, bf16[2,1408,256]{2,1,0:T(8,128)(2,1)}, u32[]{:S(2)}, u32[]{:S(2)}) %collective-permute-start.21) | collective-permute-done | bytes 1441824 | tf_op jit(solution)/shard_map/ppermute | solution.py:472
  673.8 26.8 %collective-permute-done.16.w1p = bf16[2,256,1408]{2,1,0:T(8,128)(2,1)} collective-permute-done((bf16[2,256,1408]{2,1,0:T(8,128)(2,1)}, bf16[2,256,1408]{2,1,0:T(8,128)(2,1)}, u32[]{:S(2)}, u32[]{:S(2)}) %collective-permute-start.16) | collective-permute-done | bytes 1441824 | tf_op jit(solution)/shard_map/ppermute | solution.py:472
  702.8 28.7 %collective-permute-done.17.w3p = bf16[2,256,1408]{2,1,0:T(8,128)(2,1)} collective-permute-done((bf16[2,256,1408]{2,1,0:T(8,128)(2,1)}, bf16[2,256,1408]{2,1,0:T(8,128)(2,1)}, u32[]{:S(2)}, u32[]{:S(2)}) %collective-permute-start.17) | collective-permute-done | bytes 1441824 | tf_op jit(solution)/shard_map/ppermute | solution.py:472
  731.5 30.9 %collective-permute-done.18.w2p = bf16[2,1408,256]{2,1,0:T(8,128)(2,1)} collective-permute-done((bf16[2,1408,256]{2,1,0:T(8,128)(2,1)}, bf16[2,1408,256]{2,1,0:T(8,128)(2,1)}, u32[]{:S(2)}, u32[]{:S(2)}) %collective-permute-start.18) | collective-permute-done | bytes 1441824 | tf_op jit(solution)/shard_map/ppermute | solution.py:472
  798.2 26.1 %collective-permute-done.14.w3p = bf16[2,256,1408]{2,1,0:T(8,128)(2,1)S(1)} collective-permute-done((bf16[2,256,1408]{2,1,0:T(8,128)(2,1)}, bf16[2,256,1408]{2,1,0:T(8,128)(2,1)S(1)}, u32[]{:S(2)}, u32[]{:S(2)}) %collective-permute-start.14) | collective-permute-done | bytes 1441824 | tf_op jit(solution)/shard_map/ppermute | solution.py:472
  831.4 24.4 %collective-permute-done.15.w2p = bf16[2,1408,256]{2,1,0:T(8,128)(2,1)} collective-permute-done((bf16[2,1408,256]{2,1,0:T(8,128)(2,1)S(1)}, bf16[2,1408,256]{2,1,0:T(8,128)(2,1)}, u32[]{:S(2)}, u32[]{:S(2)}) %collective-permute-start.15) | collective-permute-done | bytes 1441824 | tf_op jit(solution)/shard_map/ppermute | solution.py:472
  874.5 63.5 %shard_map.110 = (bf16[16,2,4,576,1024]{4,3,2,1,0:T(8,128)(2,1)}, bf16[16,4,576,512]{3,2,1,0:T(8,128)(2,1)}) custom-call(s32[32]{0:T(128)} %reshape.232.nt_ref, s32[4,1,9344]{2,1,0:T(1,128)} %slice.179.tok_ref, f32[4,1,9344]{2,1,0:T(1,128)} %slice.181.gate_ref, bf16[2048,8,128]{2,1,0:T(8,128)(2,1)} %bitcast.31.refs_0_, ...), custom_call_target="tpu_custom_call" | custom-call | tf_op jit(solution)/shard_map/pallas_call | solution.py:145
  938.0 60.5 %shard_map.111.xg_ref = bf16[16,2,4,576,1024]{4,3,2,1,0:T(8,128)(2,1)} custom-call(s32[32]{0:T(128)} %reshape.232.nt_ref, s32[4,1,9344]{2,1,0:T(1,128)} %slice.175.tok_ref, f32[4,1,9344]{2,1,0:T(1,128)} %slice.177.gate_ref, bf16[2048,8,128]{2,1,0:T(8,128)(2,1)} %collective-permute-done.refs_0_, ...), custom_call_target="tpu_custom_call", output_to_operand_aliasing={{}: (7, {})} | custom-call | tf_op jit(solution)/shard_map/pallas_call | solution.py:145
  998.5 86.5 %shard_map.112 = (bf16[4,4,144,512]{3,2,1,0:T(8,128)(2,1)}, bf16[4,4,144,512]{3,2,1,0:T(8,128)(2,1)}, bf16[4,4,144,512]{3,2,1,0:T(8,128)(2,1)}, bf16[4,4,144,512...) custom-call(s32[32]{0:T(128)} %reshape.232.nt_ref, ...), custom_call_target="tpu_custom_call" | custom-call | tf_op jit(solution)/shard_map/pallas_call | solution.py:287
  1085.0 96.8 %shard_map.113 = (bf16[2,4,144,512]{3,2,1,0:T(8,128)(2,1)}, bf16[2,4,144,512]{3,2,1,0:T(8,128)(2,1)}, bf16[2,4,144,512]{3,2,1,0:T(8,128)(2,1)}, bf16[2,4,144,512...) custom-call(s32[32]{0:T(128)} %reshape.232.nt_ref, ...), custom_call_target="tpu_custom_call", output_to_operand_aliasing={{4}: (11, {}), {5}: (12, {}), {6}: (13, {}), {7}: (14, {})} | custom-call | tf_op jit(solution)/shard_map/pallas_call | solution.py:287
  1181.8 46.4 %shard_map.114 = (bf16[2,4,144,512]{3,2,1,0:T(8,128)(2,1)}, bf16[2,4,144,512]{3,2,1,0:T(8,128)(2,1)}, bf16[2,4,144,512]{3,2,1,0:T(8,128)(2,1)}, bf16[2,4,144,512...) custom-call(s32[32]{0:T(128)} %reshape.232.nt_ref, ...), custom_call_target="tpu_custom_call", output_to_operand_aliasing={{4}: (11, {}), {5}: (12, {}), {6}: (13, {}), {7}: (14, {})} | custom-call | tf_op jit(solution)/shard_map/pallas_call | solution.py:287
  1228.3 46.7 %shard_map.115 = (bf16[2,4,144,512]{3,2,1,0:T(8,128)(2,1)}, bf16[2,4,144,512]{3,2,1,0:T(8,128)(2,1)}, bf16[2,4,144,512]{3,2,1,0:T(8,128)(2,1)}, bf16[2,4,144,512...) custom-call(s32[32]{0:T(128)} %reshape.232.nt_ref, ...), custom_call_target="tpu_custom_call", output_to_operand_aliasing={{4}: (11, {}), {5}: (12, {}), {6}: (13, {}), {7}: (14, {})} | custom-call | tf_op jit(solution)/shard_map/pallas_call | solution.py:287
  1276.7 53.2 %shard_map.116 = (bf16[2,4,144,512]{3,2,1,0:T(8,128)(2,1)}, bf16[2,4,144,512]{3,2,1,0:T(8,128)(2,1)}, bf16[2,4,144,512]{3,2,1,0:T(8,128)(2,1)}, bf16[2,4,144,512...) custom-call(s32[32]{0:T(128)} %reshape.232.nt_ref, ...), custom_call_target="tpu_custom_call", output_to_operand_aliasing={{4}: (11, {}), {5}: (12, {}), {6}: (13, {}), {7}: (14, {})} | custom-call | tf_op jit(solution)/shard_map/pallas_call | solution.py:287
  1330.0 46.4 %shard_map.117 = (bf16[2,4,144,512]{3,2,1,0:T(8,128)(2,1)}, bf16[2,4,144,512]{3,2,1,0:T(8,128)(2,1)}, bf16[2,4,144,512]{3,2,1,0:T(8,128)(2,1)}, bf16[2,4,144,512...) custom-call(s32[32]{0:T(128)} %reshape.232.nt_ref, ...), custom_call_target="tpu_custom_call", output_to_operand_aliasing={{4}: (11, {}), {5}: (12, {}), {6}: (13, {}), {7}: (14, {})} | custom-call | tf_op jit(solution)/shard_map/pallas_call | solution.py:287
  1376.4 26.2 %shard_map.118 = (bf16[1,4,144,512]{3,2,1,0:T(8,128)(2,1)}, bf16[1,4,144,512]{3,2,1,0:T(8,128)(2,1)}, bf16[1,4,144,512]{3,2,1,0:T(8,128)(2,1)}, bf16[1,4,144,512...) custom-call(s32[32]{0:T(128)} %reshape.232.nt_ref, ...), custom_call_target="tpu_custom_call", output_to_operand_aliasing={{4}: (11, {}), {5}: (12, {}), {6}: (13, {}), {7}: (14, {})} | custom-call | tf_op jit(solution)/shard_map/pallas_call | solution.py:287
  1402.6 26.2 %shard_map.119 = (bf16[1,4,144,512]{3,2,1,0:T(8,128)(2,1)}, bf16[1,4,144,512]{3,2,1,0:T(8,128)(2,1)}, bf16[1,4,144,512]{3,2,1,0:T(8,128)(2,1)}, bf16[1,4,144,512...) custom-call(s32[32]{0:T(128)} %reshape.232.nt_ref, ...), custom_call_target="tpu_custom_call", output_to_operand_aliasing={{4}: (11, {}), {5}: (12, {}), {6}: (13, {}), {7}: (14, {})} | custom-call | tf_op jit(solution)/shard_map/pallas_call | solution.py:287
  1428.8 60.9 %collective-permute-start.43 = (bf16[1,4,144,512]{3,2,1,0:T(8,128)(2,1)}, bf16[1,4,144,512]{3,2,1,0:T(8,128)(2,1)S(1)}, u32[]{:S(2)}, u32[]{:S(2)}) collective-permute-start(bf16[1,4,144,512]{3,2,1,0:T(8,128)(2,1)} %get-tuple-element.121), channel_id=1, source_target_pairs={{0,1},{1,0},{2,3},{3,2},{4,5},{5,4},{6,7},{7,6}} | collective-permute-start | bytes 1769480 | tf_op jit(solution)/shard_map/ppermute | solution.py:472
  1579.0 25.5 %collective-permute-done.60.refs_15_ = bf16[2,4,144,512]{3,2,1,0:T(8,128)(2,1)} collective-permute-done((bf16[2,4,144,512]{3,2,1,0:T(8,128)(2,1)}, bf16[2,4,144,512]{3,2,1,0:T(8,128)(2,1)}, u32[]{:S(2)}, u32[]{:S(2)}) %collective-permute-start.60) | collective-permute-done | bytes 1179680 | tf_op jit(solution)/shard_map/ppermute | solution.py:472
  1630.2 24.8 %collective-permute-done.57.refs_11_ = bf16[2,4,144,512]{3,2,1,0:T(8,128)(2,1)} collective-permute-done((bf16[2,4,144,512]{3,2,1,0:T(8,128)(2,1)}, bf16[2,4,144,512]{3,2,1,0:T(8,128)(2,1)}, u32[]{:S(2)}, u32[]{:S(2)}) %collective-permute-start.57) | collective-permute-done | bytes 1179680 | tf_op jit(solution)/shard_map/ppermute | solution.py:472
  1681.4 124.0 %collective-permute-done.54.refs_7_ = bf16[2,4,144,512]{3,2,1,0:T(8,128)(2,1)} collective-permute-done((bf16[2,4,144,512]{3,2,1,0:T(8,128)(2,1)}, bf16[2,4,144,512]{3,2,1,0:T(8,128)(2,1)}, u32[]{:S(2)}, u32[]{:S(2)}) %collective-permute-start.54) | collective-permute-done | bytes 1179680 | tf_op jit(solution)/shard_map/ppermute | solution.py:472
  1813.1 32.5 %shard_map.120.refs_16_ = f32[16392,128]{1,0:T(8,128)} custom-call(s32[64]{0:T(128)} %reshape.229.order_ref, s32[37376]{0:T(1024)} %broadcast_select_fusion.tok_ref, f32[23040]{0:T(1024)} %pad_maximum_fusion.dr_ref, bf16[4,4,144,512]{3,2,1,0:T(8,128)(2,1)} %get-tuple-element.124.refs_0_, bf16[4,4,144,512]{3,2,1,0:T(8,128)(2,1)} %collective-permute-done.49.refs_1_, ...), custom_call_target="tpu_custom_call" | custom-call | tf_op jit(solution)/shard_map/pallas_call | solution.py:444
  1858.4 26.7 %collective-permute-done.35.refs_2_ = bf16[2,4,144,512]{3,2,1,0:T(8,128)(2,1)} collective-permute-done((bf16[2,4,144,512]{3,2,1,0:T(8,128)(2,1)}, bf16[2,4,144,512]{3,2,1,0:T(8,128)(2,1)}, u32[]{:S(2)}, u32[]{:S(2)}) %collective-permute-start.35) | collective-permute-done | bytes 1179680 | tf_op jit(solution)/shard_map/ppermute | solution.py:472
  (322 shorter events, 351.3 us)
Async XLA Ops:
  7.2 98.4 %all-gather.7.cloned.1.call-start = ((), (), s32[]{:S(2)}) async-start(), calls=%async_computation | async-start | bytes 1345536 | tf_op jit(solution)/shard_map/all_gather | solution.py:498
  79.2 683.9 %all-gather.9.cloned.1.call-start = ((), (), s32[]{:S(2)}) async-start(), calls=%async_computation.1 | async-start | bytes 1345536 | tf_op jit(solution)/shard_map/all_gather | solution.py:499
  83.4 301.5 %collective-permute-start.28 = (bf16[4,256,1408]{2,1,0:T(8,128)(2,1)}, bf16[4,256,1408]{2,1,0:T(8,128)(2,1)}, u32[]{:S(2)}, u32[]{:S(2)}) collective-permute-start(bf16[4,256,1408]{2,1,0:T(8,128)(2,1)} %slice.201), channel_id=1, source_target_pairs={{0,4},{4,0},{1,5},{5,1},{2,6},{6,2},{3,7},{7,3}} | collective-permute-start | bytes 8650760 | tf_op jit(solution)/shard_map/ppermute | solution.py:472
  90.4 297.0 %collective-permute-start.29 = (bf16[4,256,1408]{2,1,0:T(8,128)(2,1)}, bf16[4,256,1408]{2,1,0:T(8,128)(2,1)}, u32[]{:S(2)}, u32[]{:S(2)}) collective-permute-start(bf16[4,256,1408]{2,1,0:T(8,128)(2,1)} %slice.202), channel_id=1, source_target_pairs={{0,4},{4,0},{1,5},{5,1},{2,6},{6,2},{3,7},{7,3}} | collective-permute-start | bytes 8650760 | tf_op jit(solution)/shard_map/ppermute | solution.py:472
  95.2 386.1 %collective-permute-start = (bf16[2048,8,128]{2,1,0:T(8,128)(2,1)}, bf16[2048,8,128]{2,1,0:T(8,128)(2,1)}, u32[]{:S(2)}, u32[]{:S(2)}) collective-permute-start(bf16[2048,8,128]{2,1,0:T(8,128)(2,1)} %bitcast.31.refs_0_), channel_id=1, source_target_pairs={{0,4},{4,0},{1,5},{5,1},{2,6},{6,2},{3,7},{7,3}} | collective-permute-start | bytes 12582920 | tf_op jit(solution)/shard_map/ppermute | solution.py:472
  100.6 288.5 %collective-permute-start.30 = (bf16[4,1408,256]{2,1,0:T(8,128)(2,1)}, bf16[4,1408,256]{2,1,0:T(8,128)(2,1)}, u32[]{:S(2)}, u32[]{:S(2)}) collective-permute-start(bf16[4,1408,256]{2,1,0:T(8,128)(2,1)} %slice.203), channel_id=1, source_target_pairs={{0,4},{4,0},{1,5},{5,1},{2,6},{6,2},{3,7},{7,3}} | collective-permute-start | bytes 8650760 | tf_op jit(solution)/shard_map/ppermute | solution.py:472
  125.4 257.8 %collective-permute-start.10 = (bf16[1,256,1408]{2,1,0:T(8,128)(2,1)S(1)}, bf16[1,256,1408]{2,1,0:T(8,128)(2,1)S(1)}, u32[]{:S(2)}, u32[]{:S(2)}) collective-permute-start(bf16[1,256,1408]{2,1,0:T(8,128)(2,1)S(1)} %get-tuple-element.195), channel_id=1, source_target_pairs={{0,4},{4,0},{1,5},{5,1},{2,6},{6,2},{3,7},{7,3}} | collective-permute-start | bytes 2162696 | tf_op jit(solution)/shard_map/ppermute | solution.py:472
  389.1 121.3 %collective-permute-start.22 = (bf16[2,256,1408]{2,1,0:T(8,128)(2,1)S(1)}, bf16[2,256,1408]{2,1,0:T(8,128)(2,1)}, u32[]{:S(2)}, u32[]{:S(2)}) collective-permute-start(bf16[2,256,1408]{2,1,0:T(8,128)(2,1)S(1)} %get-tuple-element.187), channel_id=1, source_target_pairs={{0,4},{4,0},{1,5},{5,1},{2,6},{6,2},{3,7},{7,3}} | collective-permute-start | bytes 4325384 | tf_op jit(solution)/shard_map/ppermute | solution.py:472
  417.7 123.6 %collective-permute-start.23 = (bf16[2,256,1408]{2,1,0:T(8,128)(2,1)S(1)}, bf16[2,256,1408]{2,1,0:T(8,128)(2,1)}, u32[]{:S(2)}, u32[]{:S(2)}) collective-permute-start(bf16[2,256,1408]{2,1,0:T(8,128)(2,1)S(1)} %get-tuple-element.182), channel_id=1, source_target_pairs={{0,4},{4,0},{1,5},{5,1},{2,6},{6,2},{3,7},{7,3}} | collective-permute-start | bytes 4325384 | tf_op jit(solution)/shard_map/ppermute | solution.py:472
  448.6 123.6 %collective-permute-start.24 = (bf16[2,1408,256]{2,1,0:T(8,128)(2,1)S(1)}, bf16[2,1408,256]{2,1,0:T(8,128)(2,1)}, u32[]{:S(2)}, u32[]{:S(2)}) collective-permute-start(bf16[2,1408,256]{2,1,0:T(8,128)(2,1)S(1)} %get-tuple-element.177), channel_id=1, source_target_pairs={{0,4},{4,0},{1,5},{5,1},{2,6},{6,2},{3,7},{7,3}} | collective-permute-start | bytes 4325384 | tf_op jit(solution)/shard_map/ppermute | solution.py:472
  479.5 282.9 %collective-permute-start.5 = (bf16[2048,8,128]{2,1,0:T(8,128)(2,1)}, bf16[2048,8,128]{2,1,0:T(8,128)(2,1)}, u32[]{:S(2)}, u32[]{:S(2)}) collective-permute-start(bf16[2048,8,128]{2,1,0:T(8,128)(2,1)} %bitcast.31.refs_0_), channel_id=1, source_target_pairs={{0,2},{1,3},{2,0},{3,1},{4,6},{5,7},{6,4},{7,5}} | collective-permute-start | bytes 12582920 | tf_op jit(solution)/shard_map/ppermute | solution.py:472
  481.2 281.7 %collective-permute-start.2 = (bf16[2048,8,128]{2,1,0:T(8,128)(2,1)}, bf16[2048,8,128]{2,1,0:T(8,128)(2,1)}, u32[]{:S(2)}, u32[]{:S(2)}) collective-permute-start(bf16[2048,8,128]{2,1,0:T(8,128)(2,1)} %collective-permute-done.refs_0_), channel_id=1, source_target_pairs={{0,2},{1,3},{2,0},{3,1},{4,6},{5,7},{6,4},{7,5}} | collective-permute-start | bytes 12582920 | tf_op jit(solution)/shard_map/ppermute | solution.py:472
  510.4 97.4 %collective-permute-start.19 = (bf16[2,256,1408]{2,1,0:T(8,128)(2,1)}, bf16[2,256,1408]{2,1,0:T(8,128)(2,1)S(1)}, u32[]{:S(2)}, u32[]{:S(2)}) collective-permute-start(bf16[2,256,1408]{2,1,0:T(8,128)(2,1)} %get-tuple-element.188), channel_id=1, source_target_pairs={{0,4},{4,0},{1,5},{5,1},{2,6},{6,2},{3,7},{7,3}} | collective-permute-start | bytes 4325384 | tf_op jit(solution)/shard_map/ppermute | solution.py:472
  541.3 97.5 %collective-permute-start.20 = (bf16[2,256,1408]{2,1,0:T(8,128)(2,1)}, bf16[2,256,1408]{2,1,0:T(8,128)(2,1)}, u32[]{:S(2)}, u32[]{:S(2)}) collective-permute-start(bf16[2,256,1408]{2,1,0:T(8,128)(2,1)} %get-tuple-element.183), channel_id=1, source_target_pairs={{0,4},{4,0},{1,5},{5,1},{2,6},{6,2},{3,7},{7,3}} | collective-permute-start | bytes 4325384 | tf_op jit(solution)/shard_map/ppermute | solution.py:472
  572.2 97.5 %collective-permute-start.21 = (bf16[2,1408,256]{2,1,0:T(8,128)(2,1)}, bf16[2,1408,256]{2,1,0:T(8,128)(2,1)}, u32[]{:S(2)}, u32[]{:S(2)}) collective-permute-start(bf16[2,1408,256]{2,1,0:T(8,128)(2,1)} %get-tuple-element.178), channel_id=1, source_target_pairs={{0,4},{4,0},{1,5},{5,1},{2,6},{6,2},{3,7},{7,3}} | collective-permute-start | bytes 4325384 | tf_op jit(solution)/shard_map/ppermute | solution.py:472
  607.8 92.8 %collective-permute-start.16 = (bf16[2,256,1408]{2,1,0:T(8,128)(2,1)}, bf16[2,256,1408]{2,1,0:T(8,128)(2,1)}, u32[]{:S(2)}, u32[]{:S(2)}) collective-permute-start(bf16[2,256,1408]{2,1,0:T(8,128)(2,1)} %get-tuple-element.189), channel_id=1, source_target_pairs={{0,4},{4,0},{1,5},{5,1},{2,6},{6,2},{3,7},{7,3}} | collective-permute-start | bytes 4325384 | tf_op jit(solution)/shard_map/ppermute | solution.py:472
  731.5 126.1 %collective-permute-start.4 = (bf16[2048,8,128]{2,1,0:T(8,128)(2,1)}, bf16[2048,8,128]{2,1,0:T(8,128)(2,1)}, u32[]{:S(2)}, u32[]{:S(2)}) collective-permute-start(bf16[2048,8,128]{2,1,0:T(8,128)(2,1)} %bitcast.31.refs_0_), channel_id=1, source_target_pairs={{0,1},{1,0},{2,3},{3,2},{4,5},{5,4},{6,7},{7,6}} | collective-permute-start | bytes 12582920 | tf_op jit(solution)/shard_map/ppermute | solution.py:472
  762.4 97.2 %collective-permute-start.1 = (bf16[2048,8,128]{2,1,0:T(8,128)(2,1)}, bf16[2048,8,128]{2,1,0:T(8,128)(2,1)}, u32[]{:S(2)}, u32[]{:S(2)}) collective-permute-start(bf16[2048,8,128]{2,1,0:T(8,128)(2,1)} %collective-permute-done.refs_0_), channel_id=1, source_target_pairs={{0,1},{1,0},{2,3},{3,2},{4,5},{5,4},{6,7},{7,6}} | collective-permute-start | bytes 12582920 | tf_op jit(solution)/shard_map/ppermute | solution.py:472
  762.4 95.4 %collective-permute-start.6 = (bf16[2048,8,128]{2,1,0:T(8,128)(2,1)}, bf16[2048,8,128]{2,1,0:T(8,128)(2,1)}, u32[]{:S(2)}, u32[]{:S(2)}) collective-permute-start(bf16[2048,8,128]{2,1,0:T(8,128)(2,1)} %collective-permute-done.5.refs_2_), channel_id=1, source_target_pairs={{0,1},{1,0},{2,3},{3,2},{4,5},{5,4},{6,7},{7,6}} | collective-permute-start | bytes 12582920 | tf_op jit(solution)/shard_map/ppermute | solution.py:472
  762.9 97.0 %collective-permute-start.3 = (bf16[2048,8,128]{2,1,0:T(8,128)(2,1)}, bf16[2048,8,128]{2,1,0:T(8,128)(2,1)}, u32[]{:S(2)}, u32[]{:S(2)}) collective-permute-start(bf16[2048,8,128]{2,1,0:T(8,128)(2,1)} %collective-permute-done.2.refs_2_), channel_id=1, source_target_pairs={{0,1},{1,0},{2,3},{3,2},{4,5},{5,4},{6,7},{7,6}} | collective-permute-start | bytes 12582920 | tf_op jit(solution)/shard_map/ppermute | solution.py:472
  855.8 520.5 %collective-permute-start.11 = (bf16[1,256,1408]{2,1,0:T(8,128)(2,1)}, bf16[1,256,1408]{2,1,0:T(8,128)(2,1)}, u32[]{:S(2)}, u32[]{:S(2)}) collective-permute-start(bf16[1,256,1408]{2,1,0:T(8,128)(2,1)} %get-tuple-element.193), channel_id=1, source_target_pairs={{0,4},{4,0},{1,5},{5,1},{2,6},{6,2},{3,7},{7,3}} | collective-permute-start | bytes 2162696 | tf_op jit(solution)/shard_map/ppermute | solution.py:472
  857.6 518.8 %collective-permute-start.12 = (bf16[1,1408,256]{2,1,0:T(8,128)(2,1)}, bf16[1,1408,256]{2,1,0:T(8,128)(2,1)}, u32[]{:S(2)}, u32[]{:S(2)}) collective-permute-start(bf16[1,1408,256]{2,1,0:T(8,128)(2,1)} %get-tuple-element.191), channel_id=1, source_target_pairs={{0,4},{4,0},{1,5},{5,1},{2,6},{6,2},{3,7},{7,3}} | collective-permute-start | bytes 2162696 | tf_op jit(solution)/shard_map/ppermute | solution.py:472
  857.9 544.7 %collective-permute-start.7 = (bf16[1,256,1408]{2,1,0:T(8,128)(2,1)}, bf16[1,256,1408]{2,1,0:T(8,128)(2,1)}, u32[]{:S(2)}, u32[]{:S(2)}) collective-permute-start(bf16[1,256,1408]{2,1,0:T(8,128)(2,1)} %get-tuple-element.196), channel_id=1, source_target_pairs={{0,4},{4,0},{1,5},{5,1},{2,6},{6,2},{3,7},{7,3}} | collective-permute-start | bytes 2162696 | tf_op jit(solution)/shard_map/ppermute | solution.py:472
  859.6 543.0 %collective-permute-start.8 = (bf16[1,256,1408]{2,1,0:T(8,128)(2,1)}, bf16[1,256,1408]{2,1,0:T(8,128)(2,1)}, u32[]{:S(2)}, u32[]{:S(2)}) collective-permute-start(bf16[1,256,1408]{2,1,0:T(8,128)(2,1)} %get-tuple-element.194), channel_id=1, source_target_pairs={{0,4},{4,0},{1,5},{5,1},{2,6},{6,2},{3,7},{7,3}} | collective-permute-start | bytes 2162696 | tf_op jit(solution)/shard_map/ppermute | solution.py:472
  859.9 542.7 %collective-permute-start.9 = (bf16[1,1408,256]{2,1,0:T(8,128)(2,1)}, bf16[1,1408,256]{2,1,0:T(8,128)(2,1)}, u32[]{:S(2)}, u32[]{:S(2)}) collective-permute-start(bf16[1,1408,256]{2,1,0:T(8,128)(2,1)} %get-tuple-element.192), channel_id=1, source_target_pairs={{0,4},{4,0},{1,5},{5,1},{2,6},{6,2},{3,7},{7,3}} | collective-permute-start | bytes 2162696 | tf_op jit(solution)/shard_map/ppermute | solution.py:472
  1553.9 101.1 %collective-permute-start.57 = (bf16[2,4,144,512]{3,2,1,0:T(8,128)(2,1)}, bf16[2,4,144,512]{3,2,1,0:T(8,128)(2,1)}, u32[]{:S(2)}, u32[]{:S(2)}) collective-permute-start(bf16[2,4,144,512]{3,2,1,0:T(8,128)(2,1)} %get-tuple-element.135), channel_id=1, source_target_pairs={{0,3},{1,2},{2,1},{3,0},{4,7},{5,6},{6,5},{7,4}} | collective-permute-start | bytes 3538952 | tf_op jit(solution)/shard_map/ppermute | solution.py:472
  1606.1 200.4 %collective-permute-start.49 = (bf16[4,4,144,512]{3,2,1,0:T(8,128)(2,1)}, bf16[4,4,144,512]{3,2,1,0:T(8,128)(2,1)}, u32[]{:S(2)}, u32[]{:S(2)}) collective-permute-start(bf16[4,4,144,512]{3,2,1,0:T(8,128)(2,1)} %get-tuple-element.125), channel_id=1, source_target_pairs={{0,1},{1,0},{2,3},{3,2},{4,5},{5,4},{6,7},{7,6}} | collective-permute-start | bytes 7077896 | tf_op jit(solution)/shard_map/ppermute | solution.py:472
  1627.8 179.7 %collective-permute-start.50 = (bf16[4,4,144,512]{3,2,1,0:T(8,128)(2,1)}, bf16[4,4,144,512]{3,2,1,0:T(8,128)(2,1)}, u32[]{:S(2)}, u32[]{:S(2)}) collective-permute-start(bf16[4,4,144,512]{3,2,1,0:T(8,128)(2,1)} %get-tuple-element.126), channel_id=1, source_target_pairs={{0,2},{1,3},{2,0},{3,1},{4,6},{5,7},{6,4},{7,5}} | collective-permute-start | bytes 7077896 | tf_op jit(solution)/shard_map/ppermute | solution.py:472
  1655.0 153.6 %collective-permute-start.51 = (bf16[4,4,144,512]{3,2,1,0:T(8,128)(2,1)}, bf16[4,4,144,512]{3,2,1,0:T(8,128)(2,1)}, u32[]{:S(2)}, u32[]{:S(2)}) collective-permute-start(bf16[4,4,144,512]{3,2,1,0:T(8,128)(2,1)} %get-tuple-element.127), channel_id=1, source_target_pairs={{0,3},{1,2},{2,1},{3,0},{4,7},{5,6},{6,5},{7,4}} | collective-permute-start | bytes 7077896 | tf_op jit(solution)/shard_map/ppermute | solution.py:472
  1656.4 149.0 %collective-permute-start.54 = (bf16[2,4,144,512]{3,2,1,0:T(8,128)(2,1)}, bf16[2,4,144,512]{3,2,1,0:T(8,128)(2,1)}, u32[]{:S(2)}, u32[]{:S(2)}) collective-permute-start(bf16[2,4,144,512]{3,2,1,0:T(8,128)(2,1)} %get-tuple-element.131), channel_id=1, source_target_pairs={{0,3},{1,2},{2,1},{3,0},{4,7},{5,6},{6,5},{7,4}} | collective-permute-start | bytes 3538952 | tf_op jit(solution)/shard_map/ppermute | solution.py:472
  1678.4 128.1 %collective-permute-start.37 = (bf16[2,4,144,512]{3,2,1,0:T(8,128)(2,1)}, bf16[2,4,144,512]{3,2,1,0:T(8,128)(2,1)}, u32[]{:S(2)}, u32[]{:S(2)}) collective-permute-start(bf16[2,4,144,512]{3,2,1,0:T(8,128)(2,1)} %get-tuple-element.113), channel_id=1, source_target_pairs={{0,1},{1,0},{2,3},{3,2},{4,5},{5,4},{6,7},{7,6}} | collective-permute-start | bytes 3538952 | tf_op jit(solution)/shard_map/ppermute | solution.py:472
  1808.6 99.6 %collective-permute-start.36 = (bf16[2,4,144,512]{3,2,1,0:T(8,128)(2,1)}, bf16[2,4,144,512]{3,2,1,0:T(8,128)(2,1)}, u32[]{:S(2)}, u32[]{:S(2)}) collective-permute-start(bf16[2,4,144,512]{3,2,1,0:T(8,128)(2,1)} %get-tuple-element.111), channel_id=1, source_target_pairs={{0,3},{1,2},{2,1},{3,0},{4,7},{5,6},{6,5},{7,4}} | collective-permute-start | bytes 3538952 | tf_op jit(solution)/shard_map/ppermute | solution.py:472
  (72 other events, 6422.8 us)
Sparse Core Ops, SparseCore 0:
  79.3 26.2 all-gather.6
  574.9 23.4 all-gather.8

commit v4 on v3

--- a/solution.py
+++ b/solution.py
@@ -173,18 +173,20 @@
 NN, NT, TN = ((1,), (0,)), ((1,), (1,)), ((0,), (0,))
 
 
-def expert_kernel(step_rows, nt_ref, steps_ref, meta_ref, xg_ref, dy_ref, w1o, w1p, w3o, w3p, w2o, w2p, *refs):
+def expert_kernel(g, step_rows, nt_ref, steps_ref, meta_ref, xg_ref, dy_ref, w1o, w1p, w3o, w3p, w2o, w2p, *refs):
     *dx_refs, dr_ref = refs[len(refs) - 10 - 1 - N_OWN:-10]
     dw1_ref, dw3_ref, dw2_ref, h1, h3, da, hid, dh1, dh3, dw2t = refs[-10:]
     step = pl.program_id(0)
-    code = steps_ref[meta_ref[1] + step]
-    e, j = meta_ref[3 + code // CHUNKS], code % CHUNKS
+    n_groups = len(GROUPS)
+    n_steps = meta_ref[1 + n_groups + g]
+    code = steps_ref[meta_ref[1 + g] + step]
+    e, j = meta_ref[1 + 2 * n_groups + code // CHUNKS], code % CHUNKS
     half = w1o.shape[1]
     d_model = 2 * half
     mine = pl.multiple_of(meta_ref[0] * half, half)
     other = pl.multiple_of(half - meta_ref[0] * half, half)
 
-    @pl.when((step < meta_ref[2]) & (j == 0))
+    @pl.when((step < n_steps) & (j == 0))
     def _():
         dw1_ref[...] = jnp.zeros_like(dw1_ref)
         dw3_ref[...] = jnp.zeros_like(dw3_ref)
@@ -228,7 +230,7 @@
                 dx_ref[0, 0, :, pl.ds(other, half)] = dxp[k * chunk:(k + 1) * chunk]
 
     def one_region(region, carry):
-        @pl.when((step < meta_ref[2]) & (j < nt_ref[e * 2 + region]))
+        @pl.when((step < n_steps) & (j < nt_ref[e * 2 + region]))
         def _():
             tile(region)
 
@@ -236,20 +238,21 @@
 
     lax.fori_loop(0, 2, one_region, 0)
 
-    @pl.when((step < meta_ref[2]) & (j == jnp.maximum(nt_ref[e * 2], nt_ref[e * 2 + 1]) - 1))
+    @pl.when((step < n_steps) & (j == jnp.maximum(nt_ref[e * 2], nt_ref[e * 2 + 1]) - 1))
     def _():
         dw2_ref[0] = dw2t[...].T
 
 
-def expert_group(e0, count, xg, dy, nt, steps, meta, own, peer, carried):
+def expert_group(g, e0, count, xg, dy, nt, steps, meta, own, peer, carried):
     exp_local, _, _, tile_rows, width = xg.shape
     half, d_ff = own[0].shape[1:]
+    n_groups = len(GROUPS)
     step_rows = 16
     chunk = tile_rows // N_OWN
 
     def place(s, steps_ref, meta_ref):
-        code = steps_ref[meta_ref[1] + jnp.minimum(s, meta_ref[2] - 1)]
-        return code // CHUNKS, meta_ref[3 + code // CHUNKS], code % CHUNKS
+        code = steps_ref[meta_ref[1 + g] + jnp.minimum(s, meta_ref[1 + n_groups + g] - 1)]
+        return code // CHUNKS, meta_ref[1 + 2 * n_groups + code // CHUNKS], code % CHUNKS
 
     def dy_tile(s, nt_ref, steps_ref, meta_ref):
         _, e, j = place(s, steps_ref, meta_ref)
@@ -285,7 +288,7 @@
     n_in = 3 + 8
     carried = list(carried)
     return pl.pallas_call(
-        functools.partial(expert_kernel, step_rows),
+        functools.partial(expert_kernel, g, step_rows),
         grid_spec=pltpu.PrefetchScalarGridSpec(
             num_scalar_prefetch=3,
             grid=(count * CHUNKS,),
@@ -538,15 +541,14 @@
         code = jnp.arange(active.shape[0], dtype=jnp.int32)
         before = jnp.sum(jnp.where((code[None, :] < code[:, None]) & active[None, :], 1, 0), axis=1)
         steps = jnp.sum(jnp.where((before[None, :] == code[:, None]) & active[None, :], code[None, :], 0), axis=1)
-        first = [sum(GROUPS[:g]) for g in range(len(GROUPS))]
-        n_steps = [jnp.sum(per_expert[first[g]:first[g] + GROUPS[g]]) for g in range(len(GROUPS))]
-        starts = [jnp.sum(per_expert[:first[g]]) for g in range(len(GROUPS))]
+        bounds = jnp.array([sum(GROUPS[:g]) for g in range(len(GROUPS) + 1)], jnp.int32)
+        starts = jnp.sum(jnp.where(index[None, :] < bounds[:, None], per_expert[None, :], 0), axis=1)
 
         xg, dy = gather_rows(all_tokens[:n_ep], slot_tok[:n_ep], slot_gate[:n_ep], nt, 0, capacity)
         xg, = gather_rows(all_tokens[n_ep:], slot_tok[n_ep:], slot_gate[n_ep:], nt, 1, capacity, (xg,))
 
         own = (w_gate, w_up, w_down)
-        mine = my_fsdp.astype(jnp.int32)
+        meta = jnp.concatenate([my_fsdp.astype(jnp.int32)[None], starts[:-1], starts[1:] - starts[:-1], order])
         place = (((expert_ids // exp_local) ^ my_ep) * exp_local + expert_ids % exp_local).T
         carried, sums = (), ()
         e0 = 0
@@ -554,8 +556,7 @@
         for g, count in enumerate(GROUPS):
             part = [w[:count] if g == 0 else lax.dynamic_slice_in_dim(w, order[e0], count, axis=0) for w in own]
             peer = [swap(w, "fsdp", 1) for w in part]
-            meta = jnp.concatenate([jnp.stack([mine, starts[g], n_steps[g]]), order])
-            out = expert_group(e0, count, xg, dy, nt, steps, meta, own, peer, carried)
+            out = expert_group(g, e0, count, xg, dy, nt, steps, meta, own, peer, carried)
             dx_g, carried = out[:n_ep], out[n_ep:]
             rows += [dx_g[0]] + [swap(dx_g[b], "ep", b) for b in range(1, n_ep)]
             e0 += count

time: 1940 us -> 1940 us (level)
  transfers between devices with their start and end apart: 63 -> 63, of which waited for: 32 -> 32; matrix products, arithmetic and copies ran while one was open for 5% -> 4% of each run, Pallas kernels for 29% -> 29%
where the time goes in v4:
time: 1940 us; the launch traced here: 1930 us
  waiting for transfers between devices  1030 us (53%)
  Pallas kernels  673 us (35%)
  starting transfers between devices  117 us (6%)
  local copies, waits for them, and re-layouts  67.2 us (3%)
  between operations  28.4 us (1%)
    ppermute x61, waiting for transfers between devices, swap(): return lax.ppermute(value, axis, [(k, k ^ mask) for k in range(size)])  1020 us
    pallas_call x8, Pallas kernels, expert_group(): pl.pallas_call(functools.partial(expert_kernel, g, step_rows), grid_spec=...  428 us
    pallas_call x2, Pallas kernels, gather_rows(): pl.pallas_call(functools.partial(gather_kernel, n_src, with_dy, region, e...  124 us
    ppermute x61, starting transfers between devices, swap(): return lax.ppermute(value, axis, [(k, k ^ mask) for k in range(size)])  117 us
    pallas_call x1, Pallas kernels, route_slots(): pl.pallas_call(functools.partial(route_kernel, n_pairs, top_k, experts, c...  66 us
    pallas_call x2, Pallas kernels, combine(): pl.pallas_call(functools.partial(combine_kernel, stage, counts, e0, exp_l...  54.8 us
  transfers between devices with their start and end apart: 63, of which 32 were waited for; matrix products, arithmetic and copies ran while one was open for 4% of the time, Pallas kernels for 29%

profile of v4, /device:TPU:0, one launch (start us, length us, event | category | flops | bytes accessed | tf_op | source)
XLA Modules:
  0.0 1931.1 jit_solution(10971272199033859362)
XLA Ops:
  11.4 66.0 %route.1 = (s32[37376]{0:T(1024)}, f32[37376]{0:T(1024)}) custom-call(s32[12288]{0:T(1024)} %reshape.222.ids_ref, f32[12288]{0:T(1024)} %reshape.223.gate_ref), custom_call_target="tpu_custom_call" | custom-call | tf_op jit(solution)/shard_map/route/pallas_call | solution.py:52
  140.0 243.1 %collective-permute-done.10.w1p = bf16[1,256,1408]{2,1,0:T(8,128)(2,1)S(1)} collective-permute-done((bf16[1,256,1408]{2,1,0:T(8,128)(2,1)S(1)}, bf16[1,256,1408]{2,1,0:T(8,128)(2,1)S(1)}, u32[]{:S(2)}, u32[]{:S(2)}) %collective-permute-start.10) | collective-permute-done | bytes 720928 | tf_op jit(solution)/shard_map/ppermute | solution.py:475
  389.4 28.3 %collective-permute-done.25.w1p = bf16[2,256,1408]{2,1,0:T(8,128)(2,1)} collective-permute-done((bf16[2,256,1408]{2,1,0:T(8,128)(2,1)S(1)}, bf16[2,256,1408]{2,1,0:T(8,128)(2,1)}, u32[]{:S(2)}, u32[]{:S(2)}) %collective-permute-start.25) | collective-permute-done | bytes 1441824 | tf_op jit(solution)/shard_map/ppermute | solution.py:475
  419.4 29.2 %collective-permute-done.26.w3p = bf16[2,256,1408]{2,1,0:T(8,128)(2,1)} collective-permute-done((bf16[2,256,1408]{2,1,0:T(8,128)(2,1)S(1)}, bf16[2,256,1408]{2,1,0:T(8,128)(2,1)}, u32[]{:S(2)}, u32[]{:S(2)}) %collective-permute-start.26) | collective-permute-done | bytes 1441824 | tf_op jit(solution)/shard_map/ppermute | solution.py:475
  450.3 29.2 %collective-permute-done.27.w2p = bf16[2,1408,256]{2,1,0:T(8,128)(2,1)} collective-permute-done((bf16[2,1408,256]{2,1,0:T(8,128)(2,1)S(1)}, bf16[2,1408,256]{2,1,0:T(8,128)(2,1)}, u32[]{:S(2)}, u32[]{:S(2)}) %collective-permute-start.27) | collective-permute-done | bytes 1441824 | tf_op jit(solution)/shard_map/ppermute | solution.py:475
  481.5 28.9 %collective-permute-done.22.w1p = bf16[2,256,1408]{2,1,0:T(8,128)(2,1)} collective-permute-done((bf16[2,256,1408]{2,1,0:T(8,128)(2,1)S(1)}, bf16[2,256,1408]{2,1,0:T(8,128)(2,1)}, u32[]{:S(2)}, u32[]{:S(2)}) %collective-permute-start.22) | collective-permute-done | bytes 1441824 | tf_op jit(solution)/shard_map/ppermute | solution.py:475
  512.1 29.2 %collective-permute-done.23.w3p = bf16[2,256,1408]{2,1,0:T(8,128)(2,1)} collective-permute-done((bf16[2,256,1408]{2,1,0:T(8,128)(2,1)S(1)}, bf16[2,256,1408]{2,1,0:T(8,128)(2,1)}, u32[]{:S(2)}, u32[]{:S(2)}) %collective-permute-start.23) | collective-permute-done | bytes 1441824 | tf_op jit(solution)/shard_map/ppermute | solution.py:475
  543.0 29.2 %collective-permute-done.24.w2p = bf16[2,1408,256]{2,1,0:T(8,128)(2,1)} collective-permute-done((bf16[2,1408,256]{2,1,0:T(8,128)(2,1)S(1)}, bf16[2,1408,256]{2,1,0:T(8,128)(2,1)}, u32[]{:S(2)}, u32[]{:S(2)}) %collective-permute-start.24) | collective-permute-done | bytes 1441824 | tf_op jit(solution)/shard_map/ppermute | solution.py:475
  574.7 33.1 %collective-permute-done.19.w1p = bf16[2,256,1408]{2,1,0:T(8,128)(2,1)S(1)} collective-permute-done((bf16[2,256,1408]{2,1,0:T(8,128)(2,1)}, bf16[2,256,1408]{2,1,0:T(8,128)(2,1)S(1)}, u32[]{:S(2)}, u32[]{:S(2)}) %collective-permute-start.19) | collective-permute-done | bytes 1441824 | tf_op jit(solution)/shard_map/ppermute | solution.py:475
  609.5 29.3 %collective-permute-done.20.w3p = bf16[2,256,1408]{2,1,0:T(8,128)(2,1)} collective-permute-done((bf16[2,256,1408]{2,1,0:T(8,128)(2,1)}, bf16[2,256,1408]{2,1,0:T(8,128)(2,1)}, u32[]{:S(2)}, u32[]{:S(2)}) %collective-permute-start.20) | collective-permute-done | bytes 1441824 | tf_op jit(solution)/shard_map/ppermute | solution.py:475
  640.5 29.2 %collective-permute-done.21.w2p = bf16[2,1408,256]{2,1,0:T(8,128)(2,1)} collective-permute-done((bf16[2,1408,256]{2,1,0:T(8,128)(2,1)}, bf16[2,1408,256]{2,1,0:T(8,128)(2,1)}, u32[]{:S(2)}, u32[]{:S(2)}) %collective-permute-start.21) | collective-permute-done | bytes 1441824 | tf_op jit(solution)/shard_map/ppermute | solution.py:475
  671.4 29.2 %collective-permute-done.16.w1p = bf16[2,256,1408]{2,1,0:T(8,128)(2,1)} collective-permute-done((bf16[2,256,1408]{2,1,0:T(8,128)(2,1)}, bf16[2,256,1408]{2,1,0:T(8,128)(2,1)}, u32[]{:S(2)}, u32[]{:S(2)}) %collective-permute-start.16) | collective-permute-done | bytes 1441824 | tf_op jit(solution)/shard_map/ppermute | solution.py:475
  731.5 30.9 %collective-permute-done.18.w2p = bf16[2,1408,256]{2,1,0:T(8,128)(2,1)} collective-permute-done((bf16[2,1408,256]{2,1,0:T(8,128)(2,1)}, bf16[2,1408,256]{2,1,0:T(8,128)(2,1)}, u32[]{:S(2)}, u32[]{:S(2)}) %collective-permute-start.18) | collective-permute-done | bytes 1441824 | tf_op jit(solution)/shard_map/ppermute | solution.py:475
  763.7 28.1 %collective-permute-done.13.w1p = bf16[2,256,1408]{2,1,0:T(8,128)(2,1)} collective-permute-done((bf16[2,256,1408]{2,1,0:T(8,128)(2,1)}, bf16[2,256,1408]{2,1,0:T(8,128)(2,1)}, u32[]{:S(2)}, u32[]{:S(2)}) %collective-permute-start.13) | collective-permute-done | bytes 1441824 | tf_op jit(solution)/shard_map/ppermute | solution.py:475
  793.9 30.3 %collective-permute-done.14.w3p = bf16[2,256,1408]{2,1,0:T(8,128)(2,1)S(1)} collective-permute-done((bf16[2,256,1408]{2,1,0:T(8,128)(2,1)}, bf16[2,256,1408]{2,1,0:T(8,128)(2,1)S(1)}, u32[]{:S(2)}, u32[]{:S(2)}) %collective-permute-start.14) | collective-permute-done | bytes 1441824 | tf_op jit(solution)/shard_map/ppermute | solution.py:475
  831.3 24.4 %collective-permute-done.15.w2p = bf16[2,1408,256]{2,1,0:T(8,128)(2,1)} collective-permute-done((bf16[2,1408,256]{2,1,0:T(8,128)(2,1)S(1)}, bf16[2,1408,256]{2,1,0:T(8,128)(2,1)}, u32[]{:S(2)}, u32[]{:S(2)}) %collective-permute-start.15) | collective-permute-done | bytes 1441824 | tf_op jit(solution)/shard_map/ppermute | solution.py:475
  867.7 63.5 %shard_map.119 = (bf16[16,2,4,576,1024]{4,3,2,1,0:T(8,128)(2,1)}, bf16[16,4,576,512]{3,2,1,0:T(8,128)(2,1)}) custom-call(s32[32]{0:T(128)} %reshape.230.nt_ref, s32[4,1,9344]{2,1,0:T(1,128)} %slice.143.tok_ref, f32[4,1,9344]{2,1,0:T(1,128)} %slice.145.gate_ref, bf16[2048,8,128]{2,1,0:T(8,128)(2,1)} %bitcast.19.refs_0_, ...), custom_call_target="tpu_custom_call" | custom-call | tf_op jit(solution)/shard_map/pallas_call | solution.py:145
  931.3 60.5 %shard_map.120.xg_ref = bf16[16,2,4,576,1024]{4,3,2,1,0:T(8,128)(2,1)} custom-call(s32[32]{0:T(128)} %reshape.230.nt_ref, s32[4,1,9344]{2,1,0:T(1,128)} %slice.139.tok_ref, f32[4,1,9344]{2,1,0:T(1,128)} %slice.141.gate_ref, bf16[2048,8,128]{2,1,0:T(8,128)(2,1)} %collective-permute-done.refs_0_, ...), custom_call_target="tpu_custom_call", output_to_operand_aliasing={{}: (7, {})} | custom-call | tf_op jit(solution)/shard_map/pallas_call | solution.py:145
  991.8 86.5 %shard_map.121 = (bf16[4,4,144,512]{3,2,1,0:T(8,128)(2,1)}, bf16[4,4,144,512]{3,2,1,0:T(8,128)(2,1)}, bf16[4,4,144,512]{3,2,1,0:T(8,128)(2,1)}, bf16[4,4,144,512...) custom-call(s32[32]{0:T(128)} %reshape.230.nt_ref, ...), custom_call_target="tpu_custom_call" | custom-call | tf_op jit(solution)/shard_map/pallas_call | solution.py:290
  1078.3 96.8 %shard_map.122 = (bf16[2,4,144,512]{3,2,1,0:T(8,128)(2,1)}, bf16[2,4,144,512]{3,2,1,0:T(8,128)(2,1)}, bf16[2,4,144,512]{3,2,1,0:T(8,128)(2,1)}, bf16[2,4,144,512...) custom-call(s32[32]{0:T(128)} %reshape.230.nt_ref, ...), custom_call_target="tpu_custom_call", output_to_operand_aliasing={{4}: (11, {}), {5}: (12, {}), {6}: (13, {}), {7}: (14, {})} | custom-call | tf_op jit(solution)/shard_map/pallas_call | solution.py:290
  1175.1 46.4 %shard_map.123 = (bf16[2,4,144,512]{3,2,1,0:T(8,128)(2,1)}, bf16[2,4,144,512]{3,2,1,0:T(8,128)(2,1)}, bf16[2,4,144,512]{3,2,1,0:T(8,128)(2,1)}, bf16[2,4,144,512...) custom-call(s32[32]{0:T(128)} %reshape.230.nt_ref, ...), custom_call_target="tpu_custom_call", output_to_operand_aliasing={{4}: (11, {}), {5}: (12, {}), {6}: (13, {}), {7}: (14, {})} | custom-call | tf_op jit(solution)/shard_map/pallas_call | solution.py:290
  1221.6 46.7 %shard_map.124 = (bf16[2,4,144,512]{3,2,1,0:T(8,128)(2,1)}, bf16[2,4,144,512]{3,2,1,0:T(8,128)(2,1)}, bf16[2,4,144,512]{3,2,1,0:T(8,128)(2,1)}, bf16[2,4,144,512...) custom-call(s32[32]{0:T(128)} %reshape.230.nt_ref, ...), custom_call_target="tpu_custom_call", output_to_operand_aliasing={{4}: (11, {}), {5}: (12, {}), {6}: (13, {}), {7}: (14, {})} | custom-call | tf_op jit(solution)/shard_map/pallas_call | solution.py:290
  1270.1 53.3 %shard_map.125 = (bf16[2,4,144,512]{3,2,1,0:T(8,128)(2,1)}, bf16[2,4,144,512]{3,2,1,0:T(8,128)(2,1)}, bf16[2,4,144,512]{3,2,1,0:T(8,128)(2,1)}, bf16[2,4,144,512...) custom-call(s32[32]{0:T(128)} %reshape.230.nt_ref, ...), custom_call_target="tpu_custom_call", output_to_operand_aliasing={{4}: (11, {}), {5}: (12, {}), {6}: (13, {}), {7}: (14, {})} | custom-call | tf_op jit(solution)/shard_map/pallas_call | solution.py:290
  1323.3 46.4 %shard_map.126 = (bf16[2,4,144,512]{3,2,1,0:T(8,128)(2,1)}, bf16[2,4,144,512]{3,2,1,0:T(8,128)(2,1)}, bf16[2,4,144,512]{3,2,1,0:T(8,128)(2,1)}, bf16[2,4,144,512...) custom-call(s32[32]{0:T(128)} %reshape.230.nt_ref, ...), custom_call_target="tpu_custom_call", output_to_operand_aliasing={{4}: (11, {}), {5}: (12, {}), {6}: (13, {}), {7}: (14, {})} | custom-call | tf_op jit(solution)/shard_map/pallas_call | solution.py:290
  1369.7 26.2 %shard_map.127 = (bf16[1,4,144,512]{3,2,1,0:T(8,128)(2,1)}, bf16[1,4,144,512]{3,2,1,0:T(8,128)(2,1)}, bf16[1,4,144,512]{3,2,1,0:T(8,128)(2,1)}, bf16[1,4,144,512...) custom-call(s32[32]{0:T(128)} %reshape.230.nt_ref, ...), custom_call_target="tpu_custom_call", output_to_operand_aliasing={{4}: (11, {}), {5}: (12, {}), {6}: (13, {}), {7}: (14, {})} | custom-call | tf_op jit(solution)/shard_map/pallas_call | solution.py:290
  1395.9 26.2 %shard_map.128 = (bf16[1,4,144,512]{3,2,1,0:T(8,128)(2,1)}, bf16[1,4,144,512]{3,2,1,0:T(8,128)(2,1)}, bf16[1,4,144,512]{3,2,1,0:T(8,128)(2,1)}, bf16[1,4,144,512...) custom-call(s32[32]{0:T(128)} %reshape.230.nt_ref, ...), custom_call_target="tpu_custom_call", output_to_operand_aliasing={{4}: (11, {}), {5}: (12, {}), {6}: (13, {}), {7}: (14, {})} | custom-call | tf_op jit(solution)/shard_map/pallas_call | solution.py:290
  1422.1 60.8 %collective-permute-start.43 = (bf16[1,4,144,512]{3,2,1,0:T(8,128)(2,1)}, bf16[1,4,144,512]{3,2,1,0:T(8,128)(2,1)S(1)}, u32[]{:S(2)}, u32[]{:S(2)}) collective-permute-start(bf16[1,4,144,512]{3,2,1,0:T(8,128)(2,1)} %get-tuple-element.121), channel_id=1, source_target_pairs={{0,1},{1,0},{2,3},{3,2},{4,5},{5,4},{6,7},{7,6}} | collective-permute-start | bytes 1769480 | tf_op jit(solution)/shard_map/ppermute | solution.py:475
  1572.2 25.5 %collective-permute-done.60.refs_15_ = bf16[2,4,144,512]{3,2,1,0:T(8,128)(2,1)} collective-permute-done((bf16[2,4,144,512]{3,2,1,0:T(8,128)(2,1)}, bf16[2,4,144,512]{3,2,1,0:T(8,128)(2,1)}, u32[]{:S(2)}, u32[]{:S(2)}) %collective-permute-start.60) | collective-permute-done | bytes 1179680 | tf_op jit(solution)/shard_map/ppermute | solution.py:475
  1623.4 24.8 %collective-permute-done.57.refs_11_ = bf16[2,4,144,512]{3,2,1,0:T(8,128)(2,1)} collective-permute-done((bf16[2,4,144,512]{3,2,1,0:T(8,128)(2,1)}, bf16[2,4,144,512]{3,2,1,0:T(8,128)(2,1)}, u32[]{:S(2)}, u32[]{:S(2)}) %collective-permute-start.57) | collective-permute-done | bytes 1179680 | tf_op jit(solution)/shard_map/ppermute | solution.py:475
  1674.5 124.0 %collective-permute-done.54.refs_7_ = bf16[2,4,144,512]{3,2,1,0:T(8,128)(2,1)} collective-permute-done((bf16[2,4,144,512]{3,2,1,0:T(8,128)(2,1)}, bf16[2,4,144,512]{3,2,1,0:T(8,128)(2,1)}, u32[]{:S(2)}, u32[]{:S(2)}) %collective-permute-start.54) | collective-permute-done | bytes 1179680 | tf_op jit(solution)/shard_map/ppermute | solution.py:475
  1806.2 32.5 %shard_map.129.refs_16_ = f32[16392,128]{1,0:T(8,128)} custom-call(s32[64]{0:T(128)} %reshape.227.order_ref, s32[37376]{0:T(1024)} %broadcast_select_fusion.tok_ref, f32[23040]{0:T(1024)} %pad_maximum_fusion.dr_ref, bf16[4,4,144,512]{3,2,1,0:T(8,128)(2,1)} %get-tuple-element.124.refs_0_, bf16[4,4,144,512]{3,2,1,0:T(8,128)(2,1)} %collective-permute-done.49.refs_1_, ...), custom_call_target="tpu_custom_call" | custom-call | tf_op jit(solution)/shard_map/pallas_call | solution.py:447
  1851.6 26.7 %collective-permute-done.35.refs_2_ = bf16[2,4,144,512]{3,2,1,0:T(8,128)(2,1)} collective-permute-done((bf16[2,4,144,512]{3,2,1,0:T(8,128)(2,1)}, bf16[2,4,144,512]{3,2,1,0:T(8,128)(2,1)}, u32[]{:S(2)}, u32[]{:S(2)}) %collective-permute-start.35) | collective-permute-done | bytes 1179680 | tf_op jit(solution)/shard_map/ppermute | solution.py:475
  (314 shorter events, 338.6 us)
Async XLA Ops:
  7.2 98.4 %all-gather.7.cloned.1.call-start = ((), (), s32[]{:S(2)}) async-start(), calls=%async_computation | async-start | bytes 1345536 | tf_op jit(solution)/shard_map/all_gather | solution.py:501
  79.2 623.7 %all-gather.9.cloned.1.call-start = ((), (), s32[]{:S(2)}) async-start(), calls=%async_computation.1 | async-start | bytes 1345536 | tf_op jit(solution)/shard_map/all_gather | solution.py:502
  83.3 301.5 %collective-permute-start.28 = (bf16[4,256,1408]{2,1,0:T(8,128)(2,1)}, bf16[4,256,1408]{2,1,0:T(8,128)(2,1)}, u32[]{:S(2)}, u32[]{:S(2)}) collective-permute-start(bf16[4,256,1408]{2,1,0:T(8,128)(2,1)} %slice.153), channel_id=1, source_target_pairs={{0,4},{4,0},{1,5},{5,1},{2,6},{6,2},{3,7},{7,3}} | collective-permute-start | bytes 8650760 | tf_op jit(solution)/shard_map/ppermute | solution.py:475
  90.3 297.0 %collective-permute-start.29 = (bf16[4,256,1408]{2,1,0:T(8,128)(2,1)}, bf16[4,256,1408]{2,1,0:T(8,128)(2,1)}, u32[]{:S(2)}, u32[]{:S(2)}) collective-permute-start(bf16[4,256,1408]{2,1,0:T(8,128)(2,1)} %slice.154), channel_id=1, source_target_pairs={{0,4},{4,0},{1,5},{5,1},{2,6},{6,2},{3,7},{7,3}} | collective-permute-start | bytes 8650760 | tf_op jit(solution)/shard_map/ppermute | solution.py:475
  95.1 386.1 %collective-permute-start = (bf16[2048,8,128]{2,1,0:T(8,128)(2,1)}, bf16[2048,8,128]{2,1,0:T(8,128)(2,1)}, u32[]{:S(2)}, u32[]{:S(2)}) collective-permute-start(bf16[2048,8,128]{2,1,0:T(8,128)(2,1)} %bitcast.19.refs_0_), channel_id=1, source_target_pairs={{0,4},{4,0},{1,5},{5,1},{2,6},{6,2},{3,7},{7,3}} | collective-permute-start | bytes 12582920 | tf_op jit(solution)/shard_map/ppermute | solution.py:475
  100.5 288.6 %collective-permute-start.30 = (bf16[4,1408,256]{2,1,0:T(8,128)(2,1)}, bf16[4,1408,256]{2,1,0:T(8,128)(2,1)}, u32[]{:S(2)}, u32[]{:S(2)}) collective-permute-start(bf16[4,1408,256]{2,1,0:T(8,128)(2,1)} %slice.155), channel_id=1, source_target_pairs={{0,4},{4,0},{1,5},{5,1},{2,6},{6,2},{3,7},{7,3}} | collective-permute-start | bytes 8650760 | tf_op jit(solution)/shard_map/ppermute | solution.py:475
  125.2 257.9 %collective-permute-start.10 = (bf16[1,256,1408]{2,1,0:T(8,128)(2,1)S(1)}, bf16[1,256,1408]{2,1,0:T(8,128)(2,1)S(1)}, u32[]{:S(2)}, u32[]{:S(2)}) collective-permute-start(bf16[1,256,1408]{2,1,0:T(8,128)(2,1)S(1)} %get-tuple-element.190), channel_id=1, source_target_pairs={{0,4},{4,0},{1,5},{5,1},{2,6},{6,2},{3,7},{7,3}} | collective-permute-start | bytes 2162696 | tf_op jit(solution)/shard_map/ppermute | solution.py:475
  389.1 121.3 %collective-permute-start.22 = (bf16[2,256,1408]{2,1,0:T(8,128)(2,1)S(1)}, bf16[2,256,1408]{2,1,0:T(8,128)(2,1)}, u32[]{:S(2)}, u32[]{:S(2)}) collective-permute-start(bf16[2,256,1408]{2,1,0:T(8,128)(2,1)S(1)} %get-tuple-element.182), channel_id=1, source_target_pairs={{0,4},{4,0},{1,5},{5,1},{2,6},{6,2},{3,7},{7,3}} | collective-permute-start | bytes 4325384 | tf_op jit(solution)/shard_map/ppermute | solution.py:475
  417.7 123.6 %collective-permute-start.23 = (bf16[2,256,1408]{2,1,0:T(8,128)(2,1)S(1)}, bf16[2,256,1408]{2,1,0:T(8,128)(2,1)}, u32[]{:S(2)}, u32[]{:S(2)}) collective-permute-start(bf16[2,256,1408]{2,1,0:T(8,128)(2,1)S(1)} %get-tuple-element.177), channel_id=1, source_target_pairs={{0,4},{4,0},{1,5},{5,1},{2,6},{6,2},{3,7},{7,3}} | collective-permute-start | bytes 4325384 | tf_op jit(solution)/shard_map/ppermute | solution.py:475
  448.6 123.6 %collective-permute-start.24 = (bf16[2,1408,256]{2,1,0:T(8,128)(2,1)S(1)}, bf16[2,1408,256]{2,1,0:T(8,128)(2,1)}, u32[]{:S(2)}, u32[]{:S(2)}) collective-permute-start(bf16[2,1408,256]{2,1,0:T(8,128)(2,1)S(1)} %get-tuple-element.172), channel_id=1, source_target_pairs={{0,4},{4,0},{1,5},{5,1},{2,6},{6,2},{3,7},{7,3}} | collective-permute-start | bytes 4325384 | tf_op jit(solution)/shard_map/ppermute | solution.py:475
  479.5 282.9 %collective-permute-start.5 = (bf16[2048,8,128]{2,1,0:T(8,128)(2,1)}, bf16[2048,8,128]{2,1,0:T(8,128)(2,1)}, u32[]{:S(2)}, u32[]{:S(2)}) collective-permute-start(bf16[2048,8,128]{2,1,0:T(8,128)(2,1)} %bitcast.19.refs_0_), channel_id=1, source_target_pairs={{0,2},{1,3},{2,0},{3,1},{4,6},{5,7},{6,4},{7,5}} | collective-permute-start | bytes 12582920 | tf_op jit(solution)/shard_map/ppermute | solution.py:475
  481.2 281.7 %collective-permute-start.2 = (bf16[2048,8,128]{2,1,0:T(8,128)(2,1)}, bf16[2048,8,128]{2,1,0:T(8,128)(2,1)}, u32[]{:S(2)}, u32[]{:S(2)}) collective-permute-start(bf16[2048,8,128]{2,1,0:T(8,128)(2,1)} %collective-permute-done.refs_0_), channel_id=1, source_target_pairs={{0,2},{1,3},{2,0},{3,1},{4,6},{5,7},{6,4},{7,5}} | collective-permute-start | bytes 12582920 | tf_op jit(solution)/shard_map/ppermute | solution.py:475
  510.4 97.4 %collective-permute-start.19 = (bf16[2,256,1408]{2,1,0:T(8,128)(2,1)}, bf16[2,256,1408]{2,1,0:T(8,128)(2,1)S(1)}, u32[]{:S(2)}, u32[]{:S(2)}) collective-permute-start(bf16[2,256,1408]{2,1,0:T(8,128)(2,1)} %get-tuple-element.183), channel_id=1, source_target_pairs={{0,4},{4,0},{1,5},{5,1},{2,6},{6,2},{3,7},{7,3}} | collective-permute-start | bytes 4325384 | tf_op jit(solution)/shard_map/ppermute | solution.py:475
  541.3 97.5 %collective-permute-start.20 = (bf16[2,256,1408]{2,1,0:T(8,128)(2,1)}, bf16[2,256,1408]{2,1,0:T(8,128)(2,1)}, u32[]{:S(2)}, u32[]{:S(2)}) collective-permute-start(bf16[2,256,1408]{2,1,0:T(8,128)(2,1)} %get-tuple-element.178), channel_id=1, source_target_pairs={{0,4},{4,0},{1,5},{5,1},{2,6},{6,2},{3,7},{7,3}} | collective-permute-start | bytes 4325384 | tf_op jit(solution)/shard_map/ppermute | solution.py:475
  572.2 97.5 %collective-permute-start.21 = (bf16[2,1408,256]{2,1,0:T(8,128)(2,1)}, bf16[2,1408,256]{2,1,0:T(8,128)(2,1)}, u32[]{:S(2)}, u32[]{:S(2)}) collective-permute-start(bf16[2,1408,256]{2,1,0:T(8,128)(2,1)} %get-tuple-element.173), channel_id=1, source_target_pairs={{0,4},{4,0},{1,5},{5,1},{2,6},{6,2},{3,7},{7,3}} | collective-permute-start | bytes 4325384 | tf_op jit(solution)/shard_map/ppermute | solution.py:475
  607.8 92.8 %collective-permute-start.16 = (bf16[2,256,1408]{2,1,0:T(8,128)(2,1)}, bf16[2,256,1408]{2,1,0:T(8,128)(2,1)}, u32[]{:S(2)}, u32[]{:S(2)}) collective-permute-start(bf16[2,256,1408]{2,1,0:T(8,128)(2,1)} %get-tuple-element.184), channel_id=1, source_target_pairs={{0,4},{4,0},{1,5},{5,1},{2,6},{6,2},{3,7},{7,3}} | collective-permute-start | bytes 4325384 | tf_op jit(solution)/shard_map/ppermute | solution.py:475
  731.4 126.0 %collective-permute-start.4 = (bf16[2048,8,128]{2,1,0:T(8,128)(2,1)}, bf16[2048,8,128]{2,1,0:T(8,128)(2,1)}, u32[]{:S(2)}, u32[]{:S(2)}) collective-permute-start(bf16[2048,8,128]{2,1,0:T(8,128)(2,1)} %bitcast.19.refs_0_), channel_id=1, source_target_pairs={{0,1},{1,0},{2,3},{3,2},{4,5},{5,4},{6,7},{7,6}} | collective-permute-start | bytes 12582920 | tf_op jit(solution)/shard_map/ppermute | solution.py:475
  762.3 97.1 %collective-permute-start.1 = (bf16[2048,8,128]{2,1,0:T(8,128)(2,1)}, bf16[2048,8,128]{2,1,0:T(8,128)(2,1)}, u32[]{:S(2)}, u32[]{:S(2)}) collective-permute-start(bf16[2048,8,128]{2,1,0:T(8,128)(2,1)} %collective-permute-done.refs_0_), channel_id=1, source_target_pairs={{0,1},{1,0},{2,3},{3,2},{4,5},{5,4},{6,7},{7,6}} | collective-permute-start | bytes 12582920 | tf_op jit(solution)/shard_map/ppermute | solution.py:475
  762.4 95.4 %collective-permute-start.6 = (bf16[2048,8,128]{2,1,0:T(8,128)(2,1)}, bf16[2048,8,128]{2,1,0:T(8,128)(2,1)}, u32[]{:S(2)}, u32[]{:S(2)}) collective-permute-start(bf16[2048,8,128]{2,1,0:T(8,128)(2,1)} %collective-permute-done.5.refs_2_), channel_id=1, source_target_pairs={{0,1},{1,0},{2,3},{3,2},{4,5},{5,4},{6,7},{7,6}} | collective-permute-start | bytes 12582920 | tf_op jit(solution)/shard_map/ppermute | solution.py:475
  762.9 96.9 %collective-permute-start.3 = (bf16[2048,8,128]{2,1,0:T(8,128)(2,1)}, bf16[2048,8,128]{2,1,0:T(8,128)(2,1)}, u32[]{:S(2)}, u32[]{:S(2)}) collective-permute-start(bf16[2048,8,128]{2,1,0:T(8,128)(2,1)} %collective-permute-done.2.refs_2_), channel_id=1, source_target_pairs={{0,1},{1,0},{2,3},{3,2},{4,5},{5,4},{6,7},{7,6}} | collective-permute-start | bytes 12582920 | tf_op jit(solution)/shard_map/ppermute | solution.py:475
  855.7 514.0 %collective-permute-start.11 = (bf16[1,256,1408]{2,1,0:T(8,128)(2,1)}, bf16[1,256,1408]{2,1,0:T(8,128)(2,1)}, u32[]{:S(2)}, u32[]{:S(2)}) collective-permute-start(bf16[1,256,1408]{2,1,0:T(8,128)(2,1)} %get-tuple-element.188), channel_id=1, source_target_pairs={{0,4},{4,0},{1,5},{5,1},{2,6},{6,2},{3,7},{7,3}} | collective-permute-start | bytes 2162696 | tf_op jit(solution)/shard_map/ppermute | solution.py:475
  857.4 512.3 %collective-permute-start.12 = (bf16[1,1408,256]{2,1,0:T(8,128)(2,1)}, bf16[1,1408,256]{2,1,0:T(8,128)(2,1)}, u32[]{:S(2)}, u32[]{:S(2)}) collective-permute-start(bf16[1,1408,256]{2,1,0:T(8,128)(2,1)} %get-tuple-element.186), channel_id=1, source_target_pairs={{0,4},{4,0},{1,5},{5,1},{2,6},{6,2},{3,7},{7,3}} | collective-permute-start | bytes 2162696 | tf_op jit(solution)/shard_map/ppermute | solution.py:475
  857.7 538.2 %collective-permute-start.7 = (bf16[1,256,1408]{2,1,0:T(8,128)(2,1)}, bf16[1,256,1408]{2,1,0:T(8,128)(2,1)}, u32[]{:S(2)}, u32[]{:S(2)}) collective-permute-start(bf16[1,256,1408]{2,1,0:T(8,128)(2,1)} %get-tuple-element.191), channel_id=1, source_target_pairs={{0,4},{4,0},{1,5},{5,1},{2,6},{6,2},{3,7},{7,3}} | collective-permute-start | bytes 2162696 | tf_op jit(solution)/shard_map/ppermute | solution.py:475
  859.5 536.4 %collective-permute-start.8 = (bf16[1,256,1408]{2,1,0:T(8,128)(2,1)}, bf16[1,256,1408]{2,1,0:T(8,128)(2,1)}, u32[]{:S(2)}, u32[]{:S(2)}) collective-permute-start(bf16[1,256,1408]{2,1,0:T(8,128)(2,1)} %get-tuple-element.189), channel_id=1, source_target_pairs={{0,4},{4,0},{1,5},{5,1},{2,6},{6,2},{3,7},{7,3}} | collective-permute-start | bytes 2162696 | tf_op jit(solution)/shard_map/ppermute | solution.py:475
  859.8 536.1 %collective-permute-start.9 = (bf16[1,1408,256]{2,1,0:T(8,128)(2,1)}, bf16[1,1408,256]{2,1,0:T(8,128)(2,1)}, u32[]{:S(2)}, u32[]{:S(2)}) collective-permute-start(bf16[1,1408,256]{2,1,0:T(8,128)(2,1)} %get-tuple-element.187), channel_id=1, source_target_pairs={{0,4},{4,0},{1,5},{5,1},{2,6},{6,2},{3,7},{7,3}} | collective-permute-start | bytes 2162696 | tf_op jit(solution)/shard_map/ppermute | solution.py:475
  1547.1 101.1 %collective-permute-start.57 = (bf16[2,4,144,512]{3,2,1,0:T(8,128)(2,1)}, bf16[2,4,144,512]{3,2,1,0:T(8,128)(2,1)}, u32[]{:S(2)}, u32[]{:S(2)}) collective-permute-start(bf16[2,4,144,512]{3,2,1,0:T(8,128)(2,1)} %get-tuple-element.135), channel_id=1, source_target_pairs={{0,3},{1,2},{2,1},{3,0},{4,7},{5,6},{6,5},{7,4}} | collective-permute-start | bytes 3538952 | tf_op jit(solution)/shard_map/ppermute | solution.py:475
  1599.2 200.4 %collective-permute-start.49 = (bf16[4,4,144,512]{3,2,1,0:T(8,128)(2,1)}, bf16[4,4,144,512]{3,2,1,0:T(8,128)(2,1)}, u32[]{:S(2)}, u32[]{:S(2)}) collective-permute-start(bf16[4,4,144,512]{3,2,1,0:T(8,128)(2,1)} %get-tuple-element.125), channel_id=1, source_target_pairs={{0,1},{1,0},{2,3},{3,2},{4,5},{5,4},{6,7},{7,6}} | collective-permute-start | bytes 7077896 | tf_op jit(solution)/shard_map/ppermute | solution.py:475
  1621.0 179.7 %collective-permute-start.50 = (bf16[4,4,144,512]{3,2,1,0:T(8,128)(2,1)}, bf16[4,4,144,512]{3,2,1,0:T(8,128)(2,1)}, u32[]{:S(2)}, u32[]{:S(2)}) collective-permute-start(bf16[4,4,144,512]{3,2,1,0:T(8,128)(2,1)} %get-tuple-element.126), channel_id=1, source_target_pairs={{0,2},{1,3},{2,0},{3,1},{4,6},{5,7},{6,4},{7,5}} | collective-permute-start | bytes 7077896 | tf_op jit(solution)/shard_map/ppermute | solution.py:475
  1648.2 153.6 %collective-permute-start.51 = (bf16[4,4,144,512]{3,2,1,0:T(8,128)(2,1)}, bf16[4,4,144,512]{3,2,1,0:T(8,128)(2,1)}, u32[]{:S(2)}, u32[]{:S(2)}) collective-permute-start(bf16[4,4,144,512]{3,2,1,0:T(8,128)(2,1)} %get-tuple-element.127), channel_id=1, source_target_pairs={{0,3},{1,2},{2,1},{3,0},{4,7},{5,6},{6,5},{7,4}} | collective-permute-start | bytes 7077896 | tf_op jit(solution)/shard_map/ppermute | solution.py:475
  1649.5 149.1 %collective-permute-start.54 = (bf16[2,4,144,512]{3,2,1,0:T(8,128)(2,1)}, bf16[2,4,144,512]{3,2,1,0:T(8,128)(2,1)}, u32[]{:S(2)}, u32[]{:S(2)}) collective-permute-start(bf16[2,4,144,512]{3,2,1,0:T(8,128)(2,1)} %get-tuple-element.131), channel_id=1, source_target_pairs={{0,3},{1,2},{2,1},{3,0},{4,7},{5,6},{6,5},{7,4}} | collective-permute-start | bytes 3538952 | tf_op jit(solution)/shard_map/ppermute | solution.py:475
  1671.5 128.1 %collective-permute-start.37 = (bf16[2,4,144,512]{3,2,1,0:T(8,128)(2,1)}, bf16[2,4,144,512]{3,2,1,0:T(8,128)(2,1)}, u32[]{:S(2)}, u32[]{:S(2)}) collective-permute-start(bf16[2,4,144,512]{3,2,1,0:T(8,128)(2,1)} %get-tuple-element.113), channel_id=1, source_target_pairs={{0,1},{1,0},{2,3},{3,2},{4,5},{5,4},{6,7},{7,6}} | collective-permute-start | bytes 3538952 | tf_op jit(solution)/shard_map/ppermute | solution.py:475
  1801.8 99.6 %collective-permute-start.36 = (bf16[2,4,144,512]{3,2,1,0:T(8,128)(2,1)}, bf16[2,4,144,512]{3,2,1,0:T(8,128)(2,1)}, u32[]{:S(2)}, u32[]{:S(2)}) collective-permute-start(bf16[2,4,144,512]{3,2,1,0:T(8,128)(2,1)} %get-tuple-element.111), channel_id=1, source_target_pairs={{0,3},{1,2},{2,1},{3,0},{4,7},{5,6},{6,5},{7,4}} | collective-permute-start | bytes 3538952 | tf_op jit(solution)/shard_map/ppermute | solution.py:475
  (73 other events, 6507.3 us)
Sparse Core Ops, SparseCore 0:
  79.3 26.2 all-gather.6
  574.8 23.4 all-gather.8
